TPU v7x, 32 devices: a whole 2x2x4 slice. The times are simulated.
32 devices in a mesh: dp: 2 (over x), tp: 4 (over z), pp: 4 (over y, core).
Axes of the slice: x: 2, y: 2, z: 4, core: 2. Of those that a mesh axis runs over, the one named last changes fastest.
Arguments:
- x_in: bfloat16 [4, 2, 1024, 512], P('dp'), parts along dimension 0
- g_out: float32 [4, 2, 1024, 512], P('dp'), parts along dimension 0
- ln1_gain: float32 [4, 512], P('pp')
- ln1_bias: float32 [4, 512], P('pp')
- w_qkv: bfloat16 [4, 512, 8, 3, 64], P('pp', None, 'tp')
- b_qkv: bfloat16 [4, 8, 3, 64], P('pp', 'tp')
- w_out: bfloat16 [4, 8, 64, 512], P('pp', 'tp')
- b_out: bfloat16 [4, 512], P('pp')
- ln2_gain: float32 [4, 512], P('pp')
- ln2_bias: float32 [4, 512], P('pp')
- w_up: bfloat16 [4, 512, 2048], P('pp', None, 'tp')
- b_up: bfloat16 [4, 2048], P('pp', 'tp')
- w_down: bfloat16 [4, 2048, 512], P('pp', 'tp')
- b_down: bfloat16 [4, 512], P('pp')
Outputs:
- output 1: bfloat16 [4, 2, 1024, 512], P('dp'), parts along dimension 0
- output 2: float32 [8, 512], P(('dp', 'pp')), parts along dimension 0
- output 3: float32 [8, 512], P(('dp', 'pp')), parts along dimension 0
- output 4: float32 [8, 512, 8, 3, 64], P(('dp', 'pp'), None, 'tp'), parts along dimension 0
- output 5: float32 [8, 8, 3, 64], P(('dp', 'pp'), 'tp'), parts along dimension 0
- output 6: float32 [8, 8, 64, 512], P(('dp', 'pp'), 'tp'), parts along dimension 0
- output 7: float32 [8, 512], P(('dp', 'pp')), parts along dimension 0
- output 8: float32 [8, 512], P(('dp', 'pp')), parts along dimension 0
- output 9: float32 [8, 512], P(('dp', 'pp')), parts along dimension 0
- output 10: float32 [8, 512, 2048], P(('dp', 'pp'), None, 'tp'), parts along dimension 0
- output 11: float32 [8, 2048], P(('dp', 'pp'), 'tp'), parts along dimension 0
- output 12: float32 [8, 2048, 512], P(('dp', 'pp'), 'tp'), parts along dimension 0
- output 13: float32 [8, 512], P(('dp', 'pp')), parts along dimension 0
There are 2 independent parts. A program takes and returns all parts, laid end to end along the dimension named above; an argument that names none is the same for every part.
All inputs are finite; a program needn't handle non-finite values.
Results may differ from a plain program's by a relative error of at most 0.0183014.
Values are sent between devices in bfloat16 or wider.
A program may use at most 1 GiB of HBM per device.

v0:
```python
import jax
import jax.numpy as jnp
from jax import lax
from jax.sharding import PartitionSpec as P

ROPE_BASE = 10000.0
LN_EPS = 1e-5
STAGE_SPECS = (P('pp', None), P('pp', None), P('pp', None, 'tp', None, None), P('pp', 'tp', None, None), P('pp', 'tp', None, None), P('pp', None), P('pp', None), P('pp', None), P('pp', None, 'tp'), P('pp', 'tp'), P('pp', 'tp', None), P('pp', None))
GRAD_SPECS = (P(('dp', 'pp'), None), P(('dp', 'pp'), None), P(('dp', 'pp'), None, 'tp', None, None), P(('dp', 'pp'), 'tp', None, None), P(('dp', 'pp'), 'tp', None, None), P(('dp', 'pp'), None), P(('dp', 'pp'), None), P(('dp', 'pp'), None), P(('dp', 'pp'), None, 'tp'), P(('dp', 'pp'), 'tp'), P(('dp', 'pp'), 'tp', None), P(('dp', 'pp'), None))


def norm_core(hidden, gain, shift):
    center = hidden - jnp.mean(hidden, axis=-1, keepdims=True)
    var_term = jnp.mean(center * center, axis=-1, keepdims=True)
    return center * lax.rsqrt(var_term + LN_EPS) * gain + shift


def rotary_tables(seq_len, head_dim):
    rot_dim = head_dim // 4
    half_rot = rot_dim // 2
    inv_freq = ROPE_BASE ** (-(jnp.arange(half_rot, dtype=jnp.float32) * 2.0) / rot_dim)
    angles = jnp.arange(seq_len, dtype=jnp.float32)[:, None] * inv_freq[None, :]
    angles = jnp.concatenate([angles, angles], axis=-1)
    return jnp.cos(angles)[None, :, None, :], jnp.sin(angles)[None, :, None, :]


def apply_rotary(values, cos_tab, sin_tab):
    rot_dim = cos_tab.shape[-1]
    half_rot = rot_dim // 2
    rot_part = values[..., :rot_dim]
    turned = jnp.concatenate([-rot_part[..., half_rot:], rot_part[..., :half_rot]], axis=-1)
    return jnp.concatenate([rot_part * cos_tab + turned * sin_tab, values[..., rot_dim:]], axis=-1)


def attention_core(qkv_proj, cos_tab, sin_tab):
    head_dim = qkv_proj.shape[-1]
    seq_len = qkv_proj.shape[1]
    query = apply_rotary(qkv_proj[:, :, :, 0].astype(jnp.float32), cos_tab, sin_tab).astype(jnp.bfloat16)
    key_rot = apply_rotary(qkv_proj[:, :, :, 1].astype(jnp.float32), cos_tab, sin_tab).astype(jnp.bfloat16)
    value_part = qkv_proj[:, :, :, 2]
    scores = jnp.einsum('bqhe,bkhe->bhqk', query, key_rot, preferred_element_type=jnp.float32) * (head_dim ** -0.5)
    positions = jnp.arange(seq_len)
    causal = positions[:, None] >= positions[None, :]
    scores = jnp.where(causal, scores, -1e30)
    probs = jax.nn.softmax(scores, axis=-1).astype(jnp.bfloat16)
    return jnp.einsum('bhqk,bkhe->bqhe', probs, value_part, preferred_element_type=jnp.float32).astype(jnp.bfloat16)


def stage_forward(hidden, layer_wts, cos_tab, sin_tab):
    ln1_gain, ln1_bias, w_qkv, b_qkv, w_out, b_out, ln2_gain, ln2_bias, w_up, b_up, w_down, b_down = layer_wts
    hidden_f = hidden.astype(jnp.float32)
    normed_a = norm_core(hidden_f, ln1_gain, ln1_bias).astype(jnp.bfloat16)
    normed_m = norm_core(hidden_f, ln2_gain, ln2_bias).astype(jnp.bfloat16)
    qkv_proj = jnp.einsum('btd,dhce->bthce', normed_a, w_qkv, preferred_element_type=jnp.float32)
    qkv_proj = (qkv_proj + b_qkv.astype(jnp.float32)).astype(jnp.bfloat16)
    context = attention_core(qkv_proj, cos_tab, sin_tab)
    attn_part = jnp.einsum('bthe,hed->btd', context, w_out, preferred_element_type=jnp.float32)
    pre_act = jnp.einsum('btd,df->btf', normed_m, w_up, preferred_element_type=jnp.float32) + b_up.astype(jnp.float32)
    hidden_mlp = jax.nn.gelu(pre_act, approximate=False).astype(jnp.bfloat16)
    mlp_part = jnp.einsum('btf,fd->btd', hidden_mlp, w_down, preferred_element_type=jnp.float32)
    attn_sum = lax.psum(attn_part.astype(jnp.bfloat16), 'tp')
    mlp_sum = lax.psum(mlp_part.astype(jnp.bfloat16), 'tp')
    total = hidden_f + attn_sum.astype(jnp.float32) + b_out.astype(jnp.float32) + mlp_sum.astype(jnp.float32) + b_down.astype(jnp.float32)
    return total.astype(jnp.bfloat16)


def stage_backward(hidden, grad_out, layer_wts, cos_tab, sin_tab):
    ln1_gain, ln1_bias, w_qkv, b_qkv, w_out, b_out, ln2_gain, ln2_bias, w_up, b_up, w_down, b_down = layer_wts
    hidden_f = hidden.astype(jnp.float32)
    normed_a32, pull_ln1 = jax.vjp(norm_core, hidden_f, ln1_gain, ln1_bias)
    normed_m32, pull_ln2 = jax.vjp(norm_core, hidden_f, ln2_gain, ln2_bias)
    normed_a = normed_a32.astype(jnp.bfloat16)
    normed_m = normed_m32.astype(jnp.bfloat16)
    qkv_proj = jnp.einsum('btd,dhce->bthce', normed_a, w_qkv, preferred_element_type=jnp.float32)
    qkv_proj = (qkv_proj + b_qkv.astype(jnp.float32)).astype(jnp.bfloat16)
    context, pull_attn = jax.vjp(lambda proj: attention_core(proj, cos_tab, sin_tab), qkv_proj)
    pre_act = jnp.einsum('btd,df->btf', normed_m, w_up, preferred_element_type=jnp.float32) + b_up.astype(jnp.float32)
    hidden_mlp, pull_gelu = jax.vjp(lambda act_in: jax.nn.gelu(act_in, approximate=False), pre_act)
    hidden_mlp_b = hidden_mlp.astype(jnp.bfloat16)
    grad_f = grad_out.astype(jnp.float32)
    grad_bias_out = jnp.sum(grad_f, axis=(0, 1))
    grad_w_out = jnp.einsum('bthe,btd->hed', context, grad_out, preferred_element_type=jnp.float32)
    grad_context = jnp.einsum('btd,hed->bthe', grad_out, w_out, preferred_element_type=jnp.float32).astype(jnp.bfloat16)
    (grad_qkv,) = pull_attn(grad_context)
    grad_b_qkv = jnp.sum(grad_qkv.astype(jnp.float32), axis=(0, 1))
    grad_w_qkv = jnp.einsum('btd,bthce->dhce', normed_a, grad_qkv, preferred_element_type=jnp.float32)
    grad_norm_a = jnp.einsum('bthce,dhce->btd', grad_qkv, w_qkv, preferred_element_type=jnp.float32)
    grad_w_down = jnp.einsum('btf,btd->fd', hidden_mlp_b, grad_out, preferred_element_type=jnp.float32)
    grad_mlp = jnp.einsum('btd,fd->btf', grad_out, w_down, preferred_element_type=jnp.float32)
    (grad_pre,) = pull_gelu(grad_mlp)
    grad_b_up = jnp.sum(grad_pre, axis=(0, 1))
    grad_pre_b = grad_pre.astype(jnp.bfloat16)
    grad_w_up = jnp.einsum('btd,btf->df', normed_m, grad_pre_b, preferred_element_type=jnp.float32)
    grad_norm_m = jnp.einsum('btf,df->btd', grad_pre_b, w_up, preferred_element_type=jnp.float32)
    grad_h1, grad_ln1_gain, grad_ln1_bias = pull_ln1(grad_norm_a)
    grad_h2, grad_ln2_gain, grad_ln2_bias = pull_ln2(grad_norm_m)
    grad_branch = lax.psum((grad_h1 + grad_h2).astype(jnp.bfloat16), 'tp')
    grad_in = (grad_f + grad_branch.astype(jnp.float32)).astype(jnp.bfloat16)
    layer_grads = (grad_ln1_gain, grad_ln1_bias, grad_w_qkv, grad_b_qkv, grad_w_out, grad_bias_out, grad_ln2_gain, grad_ln2_bias, grad_w_up, grad_b_up, grad_w_down, grad_bias_out)
    return grad_in, layer_grads


def solution(mesh):
    n_stages = mesh.shape['pp']
    tp_size = mesh.shape['tp']
    fwd_perm = [(src_stage, src_stage + 1) for src_stage in range(n_stages - 1)]
    bwd_perm = [(src_stage + 1, src_stage) for src_stage in range(n_stages - 1)]

    def device_fn(x_in, g_out, ln1_gain, ln1_bias, w_qkv, b_qkv, w_out, b_out, ln2_gain, ln2_bias, w_up, b_up, w_down, b_down):
        layer_wts = (ln1_gain[0], ln1_bias[0], w_qkv[0], b_qkv[0], w_out[0], b_out[0], ln2_gain[0], ln2_bias[0], w_up[0], b_up[0], w_down[0], b_down[0])
        stage_id = lax.axis_index('pp')
        tp_rank = lax.axis_index('tp')
        n_micro, n_rows, seq_len, width = x_in.shape
        cos_tab, sin_tab = rotary_tables(seq_len, w_qkv.shape[-1])
        piece_len = seq_len // tp_size
        n_steps = n_micro + n_stages - 1
        last_stage = n_stages - 1

        def pass_on(full, perm):
            own_rows = lax.dynamic_slice_in_dim(full, tp_rank * piece_len, piece_len, axis=1)
            arrived = lax.ppermute(own_rows, 'pp', perm)
            return lax.all_gather(arrived, 'tp', axis=1, tiled=True)

        def forward_body(step, carry):
            incoming, saved_in, y_all = carry
            micro_idx = step - stage_id
            valid = (micro_idx >= 0) & (micro_idx < n_micro)
            micro_slot = jnp.clip(micro_idx, 0, n_micro - 1)
            x_micro = lax.dynamic_index_in_dim(x_in, micro_slot, 0, keepdims=False)
            hidden = jnp.where(stage_id == 0, x_micro, incoming)
            result = stage_forward(hidden, layer_wts, cos_tab, sin_tab)
            old_in = lax.dynamic_index_in_dim(saved_in, micro_slot, 0, keepdims=False)
            saved_in = lax.dynamic_update_index_in_dim(saved_in, jnp.where(valid, hidden, old_in), micro_slot, 0)
            old_y = lax.dynamic_index_in_dim(y_all, micro_slot, 0, keepdims=False)
            keep_y = valid & (stage_id == last_stage)
            y_all = lax.dynamic_update_index_in_dim(y_all, jnp.where(keep_y, result, old_y), micro_slot, 0)
            return pass_on(result, fwd_perm), saved_in, y_all

        act_zero = jnp.zeros((n_rows, seq_len, width), jnp.bfloat16)
        fwd_state = lax.fori_loop(0, n_steps, forward_body, (act_zero, jnp.zeros_like(x_in), jnp.zeros_like(x_in)))
        saved_in = fwd_state[1]

        def backward_body(step, carry):
            incoming, grad_acc = carry
            micro_idx = step - (last_stage - stage_id)
            valid = (micro_idx >= 0) & (micro_idx < n_micro)
            micro_slot = jnp.clip(micro_idx, 0, n_micro - 1)
            hidden = lax.dynamic_index_in_dim(saved_in, micro_slot, 0, keepdims=False)
            g_micro = lax.dynamic_index_in_dim(g_out, micro_slot, 0, keepdims=False).astype(jnp.bfloat16)
            grad_out = jnp.where(stage_id == last_stage, g_micro, incoming)
            grad_in, layer_grads = stage_backward(hidden, grad_out, layer_wts, cos_tab, sin_tab)
            grad_acc = tuple(running + jnp.where(valid, update, 0.0) for running, update in zip(grad_acc, layer_grads))
            return pass_on(grad_in, bwd_perm), grad_acc

        grad_init = tuple(jnp.zeros(weight.shape, jnp.float32) for weight in layer_wts)
        bwd_state = lax.fori_loop(0, n_steps, backward_body, (act_zero, grad_init))
        grads = list(bwd_state[1])
        for norm_pos in (0, 1, 6, 7):
            grads[norm_pos] = lax.psum(grads[norm_pos], 'tp')
        y_out = lax.psum(fwd_state[2], 'pp')
        return tuple([y_out] + [grad[None] for grad in grads])

    return jax.shard_map(device_fn, mesh=mesh, in_specs=(P('dp'), P('dp')) + STAGE_SPECS, out_specs=(P('dp'),) + GRAD_SPECS, check_vma=False)
```

profile of v0, /device:TPU:0, one launch (start us, length us, event | category | flops | bytes accessed | tf_op | source)
XLA Modules:
  0.0 2646.7 jit_solution(8444947276094300644)
XLA Ops:
  26.2 1319.9 %while.59 = (s32[]{:T(128)}, bf16[2,1024,512]{2,1,0:T(8,128)(2,1)}, bf16[2,2,1024,512]{3,2,1,0:T(8,128)(2,1)}, bf16[2,2,1024,512]{3,2,1,0:T(8,128)(2,1)}, pred[]...) while((s32[]{:T(128)}, bf16[2,1024,512]{2,1,0:T(8,128)(2,1)}, ...), condition=%wide.region_7.8_spmd, body=%wide.region_0.7_spmd.sunk | while | flops 4449047552 | bytes 185734768 | solution.py:140
  39.0 11.5 fusion.335
  50.6 9.5 bitcast_convert_fusion.2
  63.1 11.2 fusion.332
  78.1 153.7 %all-reduce.21.cloned.1.call-done = (bf16[2,1024,512]{2,1,0:T(8,128)(2,1)}, bf16[2,1024,512]{2,1,0:T(8,128)(2,1)}) async-done(((bf16[2,1024,512]{2,1,0:T(8,128)(2,1)}, bf16[2,1024,512]{2,1,0:T(8,128)(2,1)}), (bf16[2,1024,512]{2,1,0:T(8,128)(2,1)}, bf16[2,1024,512]{2,1,0:T(8,128)(2,1)})) %all-reduce.21.cloned.1.call-update) | async-done | bytes 4194320 | tf_op jit(solution)/shard_map/while/body/eval_jaxpr/psum | solution.py:62
  241.1 52.1 %all-gather.3.cloned.1.call-done = bf16[2,1024,512]{2,1,0:T(8,128)(2,1)} async-done(((bf16[2,256,512]{2,1,0:T(8,128)(2,1)}), bf16[2,1024,512]{2,1,0:T(8,128)(2,1)}) %all-gather.3.cloned.1.call-update) | async-done | bytes 2097168 | tf_op jit(solution)/shard_map/while/body/eval_jaxpr/all_gather | solution.py:122
  306.0 11.5 fusion.335
  317.5 9.5 bitcast_convert_fusion.2
  330.1 11.2 fusion.332
  345.1 149.9 %all-reduce.21.cloned.1.call-done = (bf16[2,1024,512]{2,1,0:T(8,128)(2,1)}, bf16[2,1024,512]{2,1,0:T(8,128)(2,1)}) async-done(((bf16[2,1024,512]{2,1,0:T(8,128)(2,1)}, bf16[2,1024,512]{2,1,0:T(8,128)(2,1)}), (bf16[2,1024,512]{2,1,0:T(8,128)(2,1)}, bf16[2,1024,512]{2,1,0:T(8,128)(2,1)})) %all-reduce.21.cloned.1.call-update) | async-done | bytes 4194320 | tf_op jit(solution)/shard_map/while/body/eval_jaxpr/psum | solution.py:62
  504.3 52.1 %all-gather.3.cloned.1.call-done = bf16[2,1024,512]{2,1,0:T(8,128)(2,1)} async-done(((bf16[2,256,512]{2,1,0:T(8,128)(2,1)}), bf16[2,1024,512]{2,1,0:T(8,128)(2,1)}) %all-gather.3.cloned.1.call-update) | async-done | bytes 2097168 | tf_op jit(solution)/shard_map/while/body/eval_jaxpr/all_gather | solution.py:122
  569.2 11.5 fusion.335
  580.7 9.5 bitcast_convert_fusion.2
  593.3 11.2 fusion.332
  608.3 149.9 %all-reduce.21.cloned.1.call-done = (bf16[2,1024,512]{2,1,0:T(8,128)(2,1)}, bf16[2,1024,512]{2,1,0:T(8,128)(2,1)}) async-done(((bf16[2,1024,512]{2,1,0:T(8,128)(2,1)}, bf16[2,1024,512]{2,1,0:T(8,128)(2,1)}), (bf16[2,1024,512]{2,1,0:T(8,128)(2,1)}, bf16[2,1024,512]{2,1,0:T(8,128)(2,1)})) %all-reduce.21.cloned.1.call-update) | async-done | bytes 4194320 | tf_op jit(solution)/shard_map/while/body/eval_jaxpr/psum | solution.py:62
  767.6 52.0 %all-gather.3.cloned.1.call-done = bf16[2,1024,512]{2,1,0:T(8,128)(2,1)} async-done(((bf16[2,256,512]{2,1,0:T(8,128)(2,1)}), bf16[2,1024,512]{2,1,0:T(8,128)(2,1)}) %all-gather.3.cloned.1.call-update) | async-done | bytes 2097168 | tf_op jit(solution)/shard_map/while/body/eval_jaxpr/all_gather | solution.py:122
  832.4 11.5 fusion.335
  843.9 9.5 bitcast_convert_fusion.2
  856.5 11.2 fusion.332
  871.5 149.9 %all-reduce.21.cloned.1.call-done = (bf16[2,1024,512]{2,1,0:T(8,128)(2,1)}, bf16[2,1024,512]{2,1,0:T(8,128)(2,1)}) async-done(((bf16[2,1024,512]{2,1,0:T(8,128)(2,1)}, bf16[2,1024,512]{2,1,0:T(8,128)(2,1)}), (bf16[2,1024,512]{2,1,0:T(8,128)(2,1)}, bf16[2,1024,512]{2,1,0:T(8,128)(2,1)})) %all-reduce.21.cloned.1.call-update) | async-done | bytes 4194320 | tf_op jit(solution)/shard_map/while/body/eval_jaxpr/psum | solution.py:62
  1030.8 52.1 %all-gather.3.cloned.1.call-done = bf16[2,1024,512]{2,1,0:T(8,128)(2,1)} async-done(((bf16[2,256,512]{2,1,0:T(8,128)(2,1)}), bf16[2,1024,512]{2,1,0:T(8,128)(2,1)}) %all-gather.3.cloned.1.call-update) | async-done | bytes 2097168 | tf_op jit(solution)/shard_map/while/body/eval_jaxpr/all_gather | solution.py:122
  1095.7 11.5 fusion.335
  1107.2 9.5 bitcast_convert_fusion.2
  1119.8 11.2 fusion.332
  1134.8 149.9 %all-reduce.21.cloned.1.call-done = (bf16[2,1024,512]{2,1,0:T(8,128)(2,1)}, bf16[2,1024,512]{2,1,0:T(8,128)(2,1)}) async-done(((bf16[2,1024,512]{2,1,0:T(8,128)(2,1)}, bf16[2,1024,512]{2,1,0:T(8,128)(2,1)}), (bf16[2,1024,512]{2,1,0:T(8,128)(2,1)}, bf16[2,1024,512]{2,1,0:T(8,128)(2,1)})) %all-reduce.21.cloned.1.call-update) | async-done | bytes 4194320 | tf_op jit(solution)/shard_map/while/body/eval_jaxpr/psum | solution.py:62
  1294.1 52.1 %all-gather.3.cloned.1.call-done = bf16[2,1024,512]{2,1,0:T(8,128)(2,1)} async-done(((bf16[2,256,512]{2,1,0:T(8,128)(2,1)}), bf16[2,1024,512]{2,1,0:T(8,128)(2,1)}) %all-gather.3.cloned.1.call-update) | async-done | bytes 2097168 | tf_op jit(solution)/shard_map/while/body/eval_jaxpr/all_gather | solution.py:122
  1347.6 1199.6 %while.60 = (s32[]{:T(128)}, bf16[2,1024,512]{2,1,0:T(8,128)(2,1)}, f32[512]{0:T(512)}, f32[512]{0:T(512)}, f32[512,2,3,64]{0,3,2,1:T(8,128)}, /*index=5*/f32[2,...) while((s32[]{:T(128)}, bf16[2,1024,512]{2,1,0:T(8,128)(2,1)}, ...), condition=%wide.region_27.28_spmd.clone, body=%wide.region_9.27_spmd.clone.sunk | while | flops 11846850560 | bytes 509402624 | solution.py:156
  1383.8 11.5 fusion.363
  1397.8 11.4 divide_convert_fusion.12
  1409.3 10.8 fusion.366
  1420.1 10.9 fusion.365
  1438.0 9.3 fusion.359
  1467.6 82.0 %all-reduce.23.cloned.1.call-done = bf16[2,1024,512]{2,1,0:T(8,128)(2,1)} async-done(((bf16[2,1024,512]{2,1,0:T(8,128)(2,1)}), bf16[2,1024,512]{2,1,0:T(8,128)(2,1)}) %all-reduce.23.cloned.1.call-update) | async-done | bytes 2097168 | tf_op jit(solution)/shard_map/while/body/eval_jaxpr/psum | solution.py:97
  1573.3 32.6 %all-gather.5.cloned.1.call-done = bf16[2,1024,512]{2,1,0:T(8,128)(2,1)} async-done(((bf16[2,256,512]{2,1,0:T(8,128)(2,1)}), bf16[2,1024,512]{2,1,0:T(8,128)(2,1)}) %all-gather.5.cloned.1.call-update) | async-done | bytes 2097168 | tf_op jit(solution)/shard_map/while/body/eval_jaxpr/all_gather | solution.py:122
  1619.2 11.5 fusion.363
  1633.2 11.4 divide_convert_fusion.12
  1644.6 10.8 fusion.366
  1655.4 10.9 fusion.365
  1673.3 9.3 fusion.359
  1702.9 82.1 %all-reduce.23.cloned.1.call-done = bf16[2,1024,512]{2,1,0:T(8,128)(2,1)} async-done(((bf16[2,1024,512]{2,1,0:T(8,128)(2,1)}), bf16[2,1024,512]{2,1,0:T(8,128)(2,1)}) %all-reduce.23.cloned.1.call-update) | async-done | bytes 2097168 | tf_op jit(solution)/shard_map/while/body/eval_jaxpr/psum | solution.py:97
  1808.9 32.3 %all-gather.5.cloned.1.call-done = bf16[2,1024,512]{2,1,0:T(8,128)(2,1)} async-done(((bf16[2,256,512]{2,1,0:T(8,128)(2,1)}), bf16[2,1024,512]{2,1,0:T(8,128)(2,1)}) %all-gather.5.cloned.1.call-update) | async-done | bytes 2097168 | tf_op jit(solution)/shard_map/while/body/eval_jaxpr/all_gather | solution.py:122
  1854.5 11.5 fusion.363
  1868.5 11.4 divide_convert_fusion.12
  1879.9 10.8 fusion.366
  1890.7 10.9 fusion.365
  1908.7 9.3 fusion.359
  1938.2 82.1 %all-reduce.23.cloned.1.call-done = bf16[2,1024,512]{2,1,0:T(8,128)(2,1)} async-done(((bf16[2,1024,512]{2,1,0:T(8,128)(2,1)}), bf16[2,1024,512]{2,1,0:T(8,128)(2,1)}) %all-reduce.23.cloned.1.call-update) | async-done | bytes 2097168 | tf_op jit(solution)/shard_map/while/body/eval_jaxpr/psum | solution.py:97
  2044.2 32.3 %all-gather.5.cloned.1.call-done = bf16[2,1024,512]{2,1,0:T(8,128)(2,1)} async-done(((bf16[2,256,512]{2,1,0:T(8,128)(2,1)}), bf16[2,1024,512]{2,1,0:T(8,128)(2,1)}) %all-gather.5.cloned.1.call-update) | async-done | bytes 2097168 | tf_op jit(solution)/shard_map/while/body/eval_jaxpr/all_gather | solution.py:122
  2089.8 11.5 fusion.363
  2103.8 11.4 divide_convert_fusion.12
  2115.3 10.8 fusion.366
  2126.1 10.9 fusion.365
  2144.0 9.3 fusion.359
  2173.5 82.1 %all-reduce.23.cloned.1.call-done = bf16[2,1024,512]{2,1,0:T(8,128)(2,1)} async-done(((bf16[2,1024,512]{2,1,0:T(8,128)(2,1)}), bf16[2,1024,512]{2,1,0:T(8,128)(2,1)}) %all-reduce.23.cloned.1.call-update) | async-done | bytes 2097168 | tf_op jit(solution)/shard_map/while/body/eval_jaxpr/psum | solution.py:97
  2279.6 32.3 %all-gather.5.cloned.1.call-done = bf16[2,1024,512]{2,1,0:T(8,128)(2,1)} async-done(((bf16[2,256,512]{2,1,0:T(8,128)(2,1)}), bf16[2,1024,512]{2,1,0:T(8,128)(2,1)}) %all-gather.5.cloned.1.call-update) | async-done | bytes 2097168 | tf_op jit(solution)/shard_map/while/body/eval_jaxpr/all_gather | solution.py:122
  2325.1 11.5 fusion.363
  2339.1 11.4 divide_convert_fusion.12
  2350.6 10.8 fusion.366
  2361.4 10.9 fusion.365
  2379.3 9.3 fusion.359
  2408.9 82.1 %all-reduce.23.cloned.1.call-done = bf16[2,1024,512]{2,1,0:T(8,128)(2,1)} async-done(((bf16[2,1024,512]{2,1,0:T(8,128)(2,1)}), bf16[2,1024,512]{2,1,0:T(8,128)(2,1)}) %all-reduce.23.cloned.1.call-update) | async-done | bytes 2097168 | tf_op jit(solution)/shard_map/while/body/eval_jaxpr/psum | solution.py:97
  2514.9 32.3 %all-gather.5.cloned.1.call-done = bf16[2,1024,512]{2,1,0:T(8,128)(2,1)} async-done(((bf16[2,256,512]{2,1,0:T(8,128)(2,1)}), bf16[2,1024,512]{2,1,0:T(8,128)(2,1)}) %all-gather.5.cloned.1.call-update) | async-done | bytes 2097168 | tf_op jit(solution)/shard_map/while/body/eval_jaxpr/all_gather | solution.py:122
  2548.0 10.6 all-reduce.12
  2558.6 75.8 %all-reduce.19.cloned.1.call-done = bf16[2,2,1024,512]{3,2,1,0:T(8,128)(2,1)} async-done(((bf16[2,2,1024,512]{3,2,1,0:T(8,128)(2,1)}), bf16[2,2,1024,512]{3,2,1,0:T(8,128)(2,1)}) %all-reduce.19.cloned.1.call-update) | async-done | bytes 4194320 | tf_op jit(solution)/shard_map/psum | solution.py:160
  (1200 shorter events, 498.7 us)
Async XLA Ops:
  26.2 205.6 %all-reduce.21.cloned.1.call-start = ((), (), s32[]{:S(2)}) async-start(), calls=%async_computation.1 | async-start | bytes 8388608 | tf_op jit(solution)/shard_map/while/body/eval_jaxpr/psum | solution.py:62
  74.3 218.8 %all-gather.3.cloned.1.call-start = ((), (), s32[]{:S(2)}) async-start(), calls=%async_computation.2 | async-start | bytes 2621440 | tf_op jit(solution)/shard_map/while/body/eval_jaxpr/all_gather | solution.py:122
  237.3 2.9 collective-permute-start
  293.1 201.8 %all-reduce.21.cloned.1.call-start = ((), (), s32[]{:S(2)}) async-start(), calls=%async_computation.1 | async-start | bytes 8388608 | tf_op jit(solution)/shard_map/while/body/eval_jaxpr/psum | solution.py:62
  341.3 215.1 %all-gather.3.cloned.1.call-start = ((), (), s32[]{:S(2)}) async-start(), calls=%async_computation.2 | async-start | bytes 2621440 | tf_op jit(solution)/shard_map/while/body/eval_jaxpr/all_gather | solution.py:122
  500.6 2.8 collective-permute-start
  556.3 201.8 %all-reduce.21.cloned.1.call-start = ((), (), s32[]{:S(2)}) async-start(), calls=%async_computation.1 | async-start | bytes 8388608 | tf_op jit(solution)/shard_map/while/body/eval_jaxpr/psum | solution.py:62
  604.5 215.1 %all-gather.3.cloned.1.call-start = ((), (), s32[]{:S(2)}) async-start(), calls=%async_computation.2 | async-start | bytes 2621440 | tf_op jit(solution)/shard_map/while/body/eval_jaxpr/all_gather | solution.py:122
  763.8 2.9 collective-permute-start
  819.6 201.8 %all-reduce.21.cloned.1.call-start = ((), (), s32[]{:S(2)}) async-start(), calls=%async_computation.1 | async-start | bytes 8388608 | tf_op jit(solution)/shard_map/while/body/eval_jaxpr/psum | solution.py:62
  867.7 215.1 %all-gather.3.cloned.1.call-start = ((), (), s32[]{:S(2)}) async-start(), calls=%async_computation.2 | async-start | bytes 2621440 | tf_op jit(solution)/shard_map/while/body/eval_jaxpr/all_gather | solution.py:122
  1027.0 2.9 collective-permute-start
  1082.8 201.8 %all-reduce.21.cloned.1.call-start = ((), (), s32[]{:S(2)}) async-start(), calls=%async_computation.1 | async-start | bytes 8388608 | tf_op jit(solution)/shard_map/while/body/eval_jaxpr/psum | solution.py:62
  1131.0 215.1 %all-gather.3.cloned.1.call-start = ((), (), s32[]{:S(2)}) async-start(), calls=%async_computation.2 | async-start | bytes 2621440 | tf_op jit(solution)/shard_map/while/body/eval_jaxpr/all_gather | solution.py:122
  1290.3 2.9 collective-permute-start
  1370.7 179.0 %all-reduce.23.cloned.1.call-start = ((), (), s32[]{:S(2)}) async-start(), calls=%async_computation.3 | async-start | bytes 4194304 | tf_op jit(solution)/shard_map/while/body/eval_jaxpr/psum | solution.py:97
  1464.9 90.9 %copy-start.59 = (f32[512]{0:T(512)S(1)}, f32[512]{0:T(512)}, u32[]{:S(2)}) copy-start(f32[512]{0:T(512)} %get-tuple-element.2095) | copy-start | bytes 6148 | tf_op jit(solution)/shard_map/while
  1464.9 90.9 %copy-start.45 = (f32[2,3,64]{2,0,1:T(2,128)S(1)}, f32[2,3,64]{2,0,1:T(2,128)}, u32[]{:S(2)}) copy-start(f32[2,3,64]{2,0,1:T(2,128)} %get-tuple-element.2089) | copy-start | bytes 4612 | tf_op jit(solution)/shard_map/while
  1464.9 91.0 %copy-start.37 = (f32[512]{0:T(512)S(1)}, f32[512]{0:T(512)}, u32[]{:S(2)}) copy-start(f32[512]{0:T(512)} %get-tuple-element.1966) | copy-start | bytes 6148 | tf_op jit(solution)/shard_map/while
  1464.9 91.0 %copy-start.62 = (f32[512]{0:T(512)S(1)}, f32[512]{0:T(512)}, u32[]{:S(2)}) copy-start(f32[512]{0:T(512)} %get-tuple-element.2097) | copy-start | bytes 6148 | tf_op jit(solution)/shard_map/while
  1464.9 91.0 %copy-start.64 = (f32[512]{0:T(512)S(1)}, f32[512]{0:T(512)}, u32[]{:S(2)}) copy-start(f32[512]{0:T(512)} %get-tuple-element.2091) | copy-start | bytes 6148 | tf_op jit(solution)/shard_map/while
  1464.9 141.0 %all-gather.5.cloned.1.call-start = ((), (), s32[]{:S(2)}) async-start(), calls=%async_computation.4 | async-start | bytes 2621440 | tf_op jit(solution)/shard_map/while/body/eval_jaxpr/all_gather | solution.py:122
  1467.6 93.7 %copy-start.48 = (f32[512]{0:T(512)}, f32[512]{0:T(512)S(1)}, u32[]{:S(2)}) copy-start(f32[512]{0:T(512)S(1)} %select_add_fusion.15) | copy-start | bytes 6148 | tf_op jit(solution)/shard_map/while
  1551.2 3.8 collective-permute-start.1
  1606.0 179.0 %all-reduce.23.cloned.1.call-start = ((), (), s32[]{:S(2)}) async-start(), calls=%async_computation.3 | async-start | bytes 4194304 | tf_op jit(solution)/shard_map/while/body/eval_jaxpr/psum | solution.py:97
  1700.2 90.9 %copy-start.59 = (f32[512]{0:T(512)S(1)}, f32[512]{0:T(512)}, u32[]{:S(2)}) copy-start(f32[512]{0:T(512)} %get-tuple-element.2095) | copy-start | bytes 6148 | tf_op jit(solution)/shard_map/while
  1700.2 90.9 %copy-start.45 = (f32[2,3,64]{2,0,1:T(2,128)S(1)}, f32[2,3,64]{2,0,1:T(2,128)}, u32[]{:S(2)}) copy-start(f32[2,3,64]{2,0,1:T(2,128)} %get-tuple-element.2089) | copy-start | bytes 4612 | tf_op jit(solution)/shard_map/while
  1700.2 91.0 %copy-start.37 = (f32[512]{0:T(512)S(1)}, f32[512]{0:T(512)}, u32[]{:S(2)}) copy-start(f32[512]{0:T(512)} %get-tuple-element.1966) | copy-start | bytes 6148 | tf_op jit(solution)/shard_map/while
  1700.2 91.0 %copy-start.62 = (f32[512]{0:T(512)S(1)}, f32[512]{0:T(512)}, u32[]{:S(2)}) copy-start(f32[512]{0:T(512)} %get-tuple-element.2097) | copy-start | bytes 6148 | tf_op jit(solution)/shard_map/while
  1700.2 91.0 %copy-start.64 = (f32[512]{0:T(512)S(1)}, f32[512]{0:T(512)}, u32[]{:S(2)}) copy-start(f32[512]{0:T(512)} %get-tuple-element.2091) | copy-start | bytes 6148 | tf_op jit(solution)/shard_map/while
  1700.2 141.0 %all-gather.5.cloned.1.call-start = ((), (), s32[]{:S(2)}) async-start(), calls=%async_computation.4 | async-start | bytes 2621440 | tf_op jit(solution)/shard_map/while/body/eval_jaxpr/all_gather | solution.py:122
  1702.9 94.0 %copy-start.48 = (f32[512]{0:T(512)}, f32[512]{0:T(512)S(1)}, u32[]{:S(2)}) copy-start(f32[512]{0:T(512)S(1)} %select_add_fusion.15) | copy-start | bytes 6148 | tf_op jit(solution)/shard_map/while
  1786.5 3.8 collective-permute-start.1
  1841.3 179.0 %all-reduce.23.cloned.1.call-start = ((), (), s32[]{:S(2)}) async-start(), calls=%async_computation.3 | async-start | bytes 4194304 | tf_op jit(solution)/shard_map/while/body/eval_jaxpr/psum | solution.py:97
  1935.5 87.7 %copy-start.56 = (f32[512]{0:T(512)S(1)}, f32[512]{0:T(512)}, u32[]{:S(2)}) copy-start(f32[512]{0:T(512)} %get-tuple-element.2093) | copy-start | bytes 6148 | tf_op jit(solution)/shard_map/while
  1935.5 90.9 %copy-start.59 = (f32[512]{0:T(512)S(1)}, f32[512]{0:T(512)}, u32[]{:S(2)}) copy-start(f32[512]{0:T(512)} %get-tuple-element.2095) | copy-start | bytes 6148 | tf_op jit(solution)/shard_map/while
  1935.5 91.0 %copy-start.45 = (f32[2,3,64]{2,0,1:T(2,128)S(1)}, f32[2,3,64]{2,0,1:T(2,128)}, u32[]{:S(2)}) copy-start(f32[2,3,64]{2,0,1:T(2,128)} %get-tuple-element.2089) | copy-start | bytes 4612 | tf_op jit(solution)/shard_map/while
  1935.5 91.0 %copy-start.37 = (f32[512]{0:T(512)S(1)}, f32[512]{0:T(512)}, u32[]{:S(2)}) copy-start(f32[512]{0:T(512)} %get-tuple-element.1966) | copy-start | bytes 6148 | tf_op jit(solution)/shard_map/while
  1935.5 91.0 %copy-start.62 = (f32[512]{0:T(512)S(1)}, f32[512]{0:T(512)}, u32[]{:S(2)}) copy-start(f32[512]{0:T(512)} %get-tuple-element.2097) | copy-start | bytes 6148 | tf_op jit(solution)/shard_map/while
  1935.6 91.0 %copy-start.64 = (f32[512]{0:T(512)S(1)}, f32[512]{0:T(512)}, u32[]{:S(2)}) copy-start(f32[512]{0:T(512)} %get-tuple-element.2091) | copy-start | bytes 6148 | tf_op jit(solution)/shard_map/while
  1935.6 141.0 %all-gather.5.cloned.1.call-start = ((), (), s32[]{:S(2)}) async-start(), calls=%async_computation.4 | async-start | bytes 2621440 | tf_op jit(solution)/shard_map/while/body/eval_jaxpr/all_gather | solution.py:122
  1938.2 94.0 %copy-start.48 = (f32[512]{0:T(512)}, f32[512]{0:T(512)S(1)}, u32[]{:S(2)}) copy-start(f32[512]{0:T(512)S(1)} %select_add_fusion.15) | copy-start | bytes 6148 | tf_op jit(solution)/shard_map/while
  2021.8 3.8 collective-permute-start.1
  2076.6 179.0 %all-reduce.23.cloned.1.call-start = ((), (), s32[]{:S(2)}) async-start(), calls=%async_computation.3 | async-start | bytes 4194304 | tf_op jit(solution)/shard_map/while/body/eval_jaxpr/psum | solution.py:97
  2170.8 87.7 %copy-start.56 = (f32[512]{0:T(512)S(1)}, f32[512]{0:T(512)}, u32[]{:S(2)}) copy-start(f32[512]{0:T(512)} %get-tuple-element.2093) | copy-start | bytes 6148 | tf_op jit(solution)/shard_map/while
  2170.8 90.9 %copy-start.59 = (f32[512]{0:T(512)S(1)}, f32[512]{0:T(512)}, u32[]{:S(2)}) copy-start(f32[512]{0:T(512)} %get-tuple-element.2095) | copy-start | bytes 6148 | tf_op jit(solution)/shard_map/while
  2170.9 91.0 %copy-start.45 = (f32[2,3,64]{2,0,1:T(2,128)S(1)}, f32[2,3,64]{2,0,1:T(2,128)}, u32[]{:S(2)}) copy-start(f32[2,3,64]{2,0,1:T(2,128)} %get-tuple-element.2089) | copy-start | bytes 4612 | tf_op jit(solution)/shard_map/while
  2170.9 91.0 %copy-start.37 = (f32[512]{0:T(512)S(1)}, f32[512]{0:T(512)}, u32[]{:S(2)}) copy-start(f32[512]{0:T(512)} %get-tuple-element.1966) | copy-start | bytes 6148 | tf_op jit(solution)/shard_map/while
  2170.9 91.0 %copy-start.62 = (f32[512]{0:T(512)S(1)}, f32[512]{0:T(512)}, u32[]{:S(2)}) copy-start(f32[512]{0:T(512)} %get-tuple-element.2097) | copy-start | bytes 6148 | tf_op jit(solution)/shard_map/while
  2170.9 91.0 %copy-start.64 = (f32[512]{0:T(512)S(1)}, f32[512]{0:T(512)}, u32[]{:S(2)}) copy-start(f32[512]{0:T(512)} %get-tuple-element.2091) | copy-start | bytes 6148 | tf_op jit(solution)/shard_map/while
  2170.9 141.0 %all-gather.5.cloned.1.call-start = ((), (), s32[]{:S(2)}) async-start(), calls=%async_computation.4 | async-start | bytes 2621440 | tf_op jit(solution)/shard_map/while/body/eval_jaxpr/all_gather | solution.py:122
  2173.5 94.0 %copy-start.48 = (f32[512]{0:T(512)}, f32[512]{0:T(512)S(1)}, u32[]{:S(2)}) copy-start(f32[512]{0:T(512)S(1)} %select_add_fusion.15) | copy-start | bytes 6148 | tf_op jit(solution)/shard_map/while
  2257.1 3.8 collective-permute-start.1
  2312.0 179.0 %all-reduce.23.cloned.1.call-start = ((), (), s32[]{:S(2)}) async-start(), calls=%async_computation.3 | async-start | bytes 4194304 | tf_op jit(solution)/shard_map/while/body/eval_jaxpr/psum | solution.py:97
  2406.2 87.7 %copy-start.56 = (f32[512]{0:T(512)S(1)}, f32[512]{0:T(512)}, u32[]{:S(2)}) copy-start(f32[512]{0:T(512)} %get-tuple-element.2093) | copy-start | bytes 6148 | tf_op jit(solution)/shard_map/while
  2406.2 90.9 %copy-start.59 = (f32[512]{0:T(512)S(1)}, f32[512]{0:T(512)}, u32[]{:S(2)}) copy-start(f32[512]{0:T(512)} %get-tuple-element.2095) | copy-start | bytes 6148 | tf_op jit(solution)/shard_map/while
  2406.2 91.0 %copy-start.45 = (f32[2,3,64]{2,0,1:T(2,128)S(1)}, f32[2,3,64]{2,0,1:T(2,128)}, u32[]{:S(2)}) copy-start(f32[2,3,64]{2,0,1:T(2,128)} %get-tuple-element.2089) | copy-start | bytes 4612 | tf_op jit(solution)/shard_map/while
  2406.2 91.0 %copy-start.37 = (f32[512]{0:T(512)S(1)}, f32[512]{0:T(512)}, u32[]{:S(2)}) copy-start(f32[512]{0:T(512)} %get-tuple-element.1966) | copy-start | bytes 6148 | tf_op jit(solution)/shard_map/while
  2406.2 91.0 %copy-start.62 = (f32[512]{0:T(512)S(1)}, f32[512]{0:T(512)}, u32[]{:S(2)}) copy-start(f32[512]{0:T(512)} %get-tuple-element.2097) | copy-start | bytes 6148 | tf_op jit(solution)/shard_map/while
  2406.2 91.0 %copy-start.64 = (f32[512]{0:T(512)S(1)}, f32[512]{0:T(512)}, u32[]{:S(2)}) copy-start(f32[512]{0:T(512)} %get-tuple-element.2091) | copy-start | bytes 6148 | tf_op jit(solution)/shard_map/while
  2406.2 141.0 %all-gather.5.cloned.1.call-start = ((), (), s32[]{:S(2)}) async-start(), calls=%async_computation.4 | async-start | bytes 2621440 | tf_op jit(solution)/shard_map/while/body/eval_jaxpr/all_gather | solution.py:122
  2408.9 94.0 %copy-start.48 = (f32[512]{0:T(512)}, f32[512]{0:T(512)S(1)}, u32[]{:S(2)}) copy-start(f32[512]{0:T(512)S(1)} %select_add_fusion.15) | copy-start | bytes 6148 | tf_op jit(solution)/shard_map/while
  2492.5 3.8 collective-permute-start.1
  2547.3 87.1 %all-reduce.19.cloned.1.call-start = ((), (), s32[]{:S(2)}) async-start(), calls=%async_computation | async-start | bytes 8388608 | tf_op jit(solution)/shard_map/psum | solution.py:160
  (343 other events, 4213.8 us)
Sparse Core Ops, SparseCore 0:
  74.4 157.2 all-reduce.20
  241.2 51.8 all-gather.2
  341.4 153.5 all-reduce.20
  504.4 51.8 all-gather.2
  604.6 153.5 all-reduce.20
  767.7 51.8 all-gather.2
  867.8 153.5 all-reduce.20
  1030.9 51.8 all-gather.2
  1131.1 153.5 all-reduce.20
  1294.2 51.8 all-gather.2
  1465.0 84.6 all-reduce.22
  1555.9 49.9 all-gather.4
  1700.3 84.6 all-reduce.22
  1791.2 49.9 all-gather.4
  1935.6 84.6 all-reduce.22
  2026.6 49.9 all-gather.4
  2170.9 84.6 all-reduce.22
  2261.9 49.9 all-gather.4
  2406.3 84.6 all-reduce.22
  2497.2 49.9 all-gather.4
Sparse Core Ops, SparseCore 1:
  2550.1 84.2 all-reduce.18
where the time goes:
time: 2660 us; the launch traced here: 2650 us
  waiting for transfers between devices  1680 us (63%)
  matrix products  574 us (22%)
  other arithmetic  233 us (9%)
  local copies, waits for them, and re-layouts  87.7 us (3%)
  loops' own time  29.7 us (1%)
    psum x5, waiting for transfers between devices, stage_forward(): mlp_sum = lax.psum(mlp_part.astype(jnp.bfloat16), 'tp')  753 us
    all_gather x10, waiting for transfers between devices, pass_on(): return lax.all_gather(arrived, 'tp', axis=1, tiled=True)  422 us
    psum x5, waiting for transfers between devices, stage_backward(): grad_branch = lax.psum((grad_h1 + grad_h2).astype(jnp.bfloat16), 'tp')  410 us
    sub x10, matrix products, attention_core(): probs = jax.nn.softmax(scores, axis=-1).astype(jnp.bfloat16)  115 us
    dot_general x10, matrix products, attention_core(): jnp.einsum('bqhe,bkhe->bhqk', query, key_rot, preferred_element_type=jnp....  108 us
    psum x1, waiting for transfers between devices, device_fn(): y_out = lax.psum(fwd_state[2], 'pp')  75.8 us
    dot_general x10, matrix products, attention_core(): jnp.einsum('bhqk,bkhe->bqhe', probs, value_part, preferred_element_type=j...  70.2 us
    dot_general x5, matrix products, stage_forward(): jnp.einsum('btf,fd->btd', hidden_mlp, w_down, preferred_element_type=jnp....  56 us
  transfers between devices with their start and end apart: 31, of which 31 were waited for; matrix products, arithmetic and copies ran while one was open for 4% of the time, Pallas kernels for 0%

commit v1 on v0

v1 whole, which is shorter than its diff:
```python
import functools
import math

import jax
import jax.numpy as jnp
import numpy as np
from jax import lax
from jax.experimental import pallas as pl
from jax.experimental.pallas import tpu as pltpu
from jax.sharding import PartitionSpec as P

ROPE_BASE = 10000.0
LN_EPS = 1e-5
STAGE_SPECS = (P('pp', None), P('pp', None), P('pp', None, 'tp', None, None), P('pp', 'tp', None, None), P('pp', 'tp', None, None), P('pp', None), P('pp', None), P('pp', None), P('pp', None, 'tp'), P('pp', 'tp'), P('pp', 'tp', None), P('pp', None))
GRAD_SPECS = (P(('dp', 'pp'), None), P(('dp', 'pp'), None), P(('dp', 'pp'), None, 'tp', None, None), P(('dp', 'pp'), 'tp', None, None), P(('dp', 'pp'), 'tp', None, None), P(('dp', 'pp'), None), P(('dp', 'pp'), None), P(('dp', 'pp'), None), P(('dp', 'pp'), None, 'tp'), P(('dp', 'pp'), 'tp'), P(('dp', 'pp'), 'tp', None), P(('dp', 'pp'), None))

F32 = jnp.float32
BF16 = jnp.bfloat16
NL = 4
NT = 4
NC = 4
SUB = 2
LOG2E = 1.4426950408889634
RSQRT2 = 0.7071067811865476
INV_SQRT_2PI = 0.3989422804014327


def nn(a, b):
    return lax.dot_general(a, b, (((1,), (0,)), ((), ())), preferred_element_type=F32)


def nt(a, b):
    return lax.dot_general(a, b, (((1,), (1,)), ((), ())), preferred_element_type=F32)


def tn(a, b):
    return lax.dot_general(a, b, (((0,), (0,)), ((), ())), preferred_element_type=F32)


def rotary_base(chunk, n_chunks, head_dim, n_heads):
    rot_dim = head_dim // 4
    half = rot_dim // 2
    inv_freq = np.zeros((head_dim,), np.float64)
    inv_freq[:rot_dim] = np.tile(ROPE_BASE ** (-(np.arange(half) * 2.0) / rot_dim), 2)
    inv_freq = np.tile(inv_freq, n_heads)
    pos = np.concatenate([np.arange(chunk), np.arange(8) * (np.arange(8) < n_chunks) * chunk]).astype(np.float64)
    ang = pos[:, None] * inv_freq[None, :]
    return np.stack([np.cos(ang), np.sin(ang)]).astype(np.float32)


def body(dims, x, g, wqkv, wo, wup, wdn, vec, tab,
         y, oqkv, oo, oup, odn, ovec,
         WQ, WO, WU, WD, VEC, H, Q, K, V, KT, VT, CTX, P0, P1, P2, P3, HID, GP, RA, RB, PS, PF,
         GQ, GO, GU, GD, R2Q, R2O, R2U, R2D, DK, DV, TAB, COS, SIN, GV, ZR, GZ, PR,
         AS, MS, PRE, DPB, DS, ST,
         wl, ws, wr, wf, xs, gs, sab, sc, ra_s, rb_s, rc_s, ys, yr, g1s, g1r, g2s, g2r, g3s, g3r, v1s, v1r, v2s, v2r, osem):
    S, D, E, C, F = dims
    E2 = 2 * E
    SR = C // SUB
    z = lax.axis_index('tp')
    s = lax.axis_index('pp')
    ys_ = s // 2
    c = s % 2
    sib = s + 1 - 2 * c
    oy = 2 * (1 - ys_)
    is_end = z * (NT - 1 - z) == 0
    inner = z * (NT - 1 - z) > 0
    hub = 1 + z // 3
    leaf = jnp.where(z == 1, 0, 3)
    peer = 3 - z
    PX = (P0, P1, P2, P3)
    W_IN = (wqkv, wo, wup, wdn)
    W_BUF = (WQ, WO, WU, WD)
    W_HALF = (D // 2, E, D // 2, F // 2)
    G_BUF = (GQ, GO, GU, GD)
    G_OUT = (oqkv, oo, oup, odn)
    G_HALF = W_HALF
    G_COLS = (3 * E2, D, F, D)
    R1_OFF = (0, D // 2, D // 2 + E, D + E)
    R2 = (R2Q, R2O, R2U, R2D)

    def rcopy(src, dst, ss, rs, **dev):
        return pltpu.make_async_remote_copy(src_ref=src, dst_ref=dst, send_sem=ss, recv_sem=rs, device_id=dev, device_id_type=pl.DeviceIdType.MESH)

    def lcopy(src, dst, sem):
        return pltpu.make_async_copy(src, dst, sem)

    def rows(start, n):
        return pl.ds(pl.multiple_of(start, n), n)

    xcopy = lcopy(x.at[ys_, c], H.at[0], xs.at[0])
    xcopy.start()
    gcopy = lcopy(g.at[ys_, c], GP.at[NL], gs.at[0])
    gcopy.start()
    tcopy = lcopy(tab, TAB, xs.at[1])
    tcopy.start()
    for a in range(4):
        lcopy(W_IN[a], W_BUF[a].at[s], wl.at[a]).start()
    lcopy(vec, VEC.at[s], wl.at[4]).start()

    bar = pltpu.get_barrier_semaphore()
    for o in range(1, NT):
        pl.semaphore_signal(bar, inc=1, device_id={'tp': (z + o) % NT}, device_id_type=pl.DeviceIdType.MESH)
    for o in range(1, NL):
        pl.semaphore_signal(bar, inc=1, device_id={'pp': (s + o) % NL}, device_id_type=pl.DeviceIdType.MESH)
    pl.semaphore_wait(bar, NT - 1 + NL - 1)

    def w_half(a, k):
        return rows(k * W_HALF[a], W_HALF[a])

    def sib_copies():
        out = []
        for a in range(4):
            for k in range(2):
                out.append(rcopy(W_IN[a].at[w_half(a, k)], W_BUF[a].at[s, w_half(a, k)], ws.at[2 * a + k], wr.at[s, 2 * a + k], pp=sib))
        out.append(rcopy(vec, VEC.at[s], ws.at[16], wr.at[s, 8], pp=sib))
        return out

    def y_copies():
        out = [rcopy(vec, VEC.at[s], ws.at[17 + k], wr.at[s, 8], pp=oy + k) for k in range(2)]
        for a in range(4):
            for k in range(2):
                out.append(rcopy(W_IN[a].at[w_half(a, k)], W_BUF[a].at[s, w_half(a, k)], ws.at[8 + 2 * a + k], wr.at[s, 2 * a + k], pp=oy + k))
        return out

    def start_all(copies):
        for cp in copies:
            cp.start()

    @pl.when(s != 1)
    def _():
        start_all(y_copies())
    start_all(sib_copies())

    def arrived(l, a, k):
        rcopy(W_BUF[a].at[l, w_half(a, k)], W_BUF[a].at[l, w_half(a, k)], ws.at[2 * a], wr.at[l, 2 * a + k], pp=sib).wait_recv()

    def fwd_copy(l, a):
        part = W_BUF[a].at[l, w_half(a, c)]
        return rcopy(part, part, wf.at[l % 2, a], wr.at[l, 2 * a + c], pp=sib)

    def fetch(l):
        @pl.when(l == s)
        def _():
            for a in range(4):
                lcopy(W_IN[a], W_BUF[a].at[s], wl.at[a]).wait()
            lcopy(vec, VEC.at[s], wl.at[4]).wait()

        @pl.when(l != s)
        def _():
            @pl.when(l // 2 == ys_)
            def _():
                for a in range(4):
                    for k in range(2):
                        arrived(l, a, k)

            @pl.when(l // 2 != ys_)
            def _():
                for a in range(4):
                    arrived(l, a, c)
                    fwd_copy(l, a).start()
                for a in range(4):
                    arrived(l, a, 1 - c)
            rcopy(VEC.at[l], VEC.at[l], ws.at[16], wr.at[l, 8], pp=sib).wait_recv()

    tcopy.wait()
    for i in range(NC):
        cb, sb = TAB[0, 0:C, :], TAB[1, 0:C, :]
        cr, sr = TAB[0, C + i:C + i + 1, :], TAB[1, C + i:C + i + 1, :]
        COS[i * C:(i + 1) * C, :] = cb * cr - sb * sr
        SIN[i * C:(i + 1) * C, :] = sb * cr + cb * sr

    lane = lax.broadcasted_iota(jnp.int32, (C, E2), 1)
    head_lane = lane // E
    in_head = lane % E
    rot_half = E // 8
    low = in_head < rot_half
    sub_head = lax.broadcasted_iota(jnp.int32, (E2, C), 0) // E
    lower = lax.broadcasted_iota(jnp.int32, (C, C), 0) <= lax.broadcasted_iota(jnp.int32, (C, C), 1)
    c1 = E ** -0.5 * LOG2E

    def tabs(i):
        cs, sn = COS[i * C:(i + 1) * C, :], SIN[i * C:(i + 1) * C, :]
        return cs, jnp.where(low, -sn, 0.0), jnp.where(low, 0.0, sn)

    def rotate(v, t):
        cs, sa, sb = t
        return v * cs + pltpu.roll(v, E2 - rot_half, 1) * sa + pltpu.roll(v, rot_half, 1) * sb

    def unrotate(v, t):
        cs, sa, sb = t
        return v * cs + pltpu.roll(v * sa, rot_half, 1) + pltpu.roll(v * sb, E2 - rot_half, 1)

    def end_copy(p, t):
        return rcopy(PS.at[t * SR:(t + 1) * SR], RA.at[p % 2, t * SR:(t + 1) * SR], sab.at[t], ra_s.at[p % 2, t], tp=hub)

    def peer_copy(p, t):
        return rcopy(PS.at[t * SR:(t + 1) * SR], RB.at[p % 2, t * SR:(t + 1) * SR], sab.at[t], rb_s.at[p % 2, t], tp=peer)

    def back_copy(p, di, t):
        return rcopy(H.at[di, t * SR:(t + 1) * SR], H.at[di, t * SR:(t + 1) * SR], sc.at[t], rc_s.at[p % 2, t], tp=leaf)

    def pf_row(i, back):
        return (NC if back and i == NC - 1 else i) * C

    def ar_send(p, i, back=False):
        @pl.when(is_end)
        def _():
            for t in range(i * SUB, (i + 1) * SUB):
                @pl.when(p > 0)
                def _():
                    end_copy(p, t).wait_send()
                f0 = pf_row(i, back) + (t - i * SUB) * SR
                PS[t * SR:(t + 1) * SR, :] = PF[f0:f0 + SR, :].astype(BF16)
                end_copy(p, t).start()

    def ar_mid(p, i, back=False):
        @pl.when(inner)
        def _():
            for t in range(i * SUB, (i + 1) * SUB):
                end_copy(p, t).wait_recv()
                @pl.when(p > 0)
                def _():
                    peer_copy(p, t).wait_send()
                r = slice(t * SR, (t + 1) * SR)
                f0 = pf_row(i, back) + (t - i * SUB) * SR
                PS[r, :] = (PF[f0:f0 + SR, :] + RA[p % 2, r, :].astype(F32)).astype(BF16)
                peer_copy(p, t).start()

    def ar_last(p, ri, di, i):
        @pl.when(inner)
        def _():
            keep = jnp.where(p < NL, 1.0, 0.0)
            lv = jnp.minimum(p, NL - 1)
            bias = (VEC[lv, 4:5, :] + VEC[lv, 5:6, :]) * keep
            for t in range(i * SUB, (i + 1) * SUB):
                peer_copy(p, t).wait_recv()
                @pl.when(p > 0)
                def _():
                    back_copy(p, di, t).wait_send()
                r = slice(t * SR, (t + 1) * SR)
                both = PS[r, :].astype(F32) + RB[p % 2, r, :].astype(F32)
                H[di, r, :] = (H[ri, r, :].astype(F32) + both + bias).astype(BF16)
                back_copy(p, di, t).start()

    def ar_wait(p, di, i):
        @pl.when(is_end)
        def _():
            for t in range(i * SUB, (i + 1) * SUB):
                back_copy(p, di, t).wait_recv()

    def stats(hf):
        cen = hf - jnp.mean(hf, axis=-1, keepdims=True)
        rstd = lax.rsqrt(jnp.mean(cen * cen, axis=-1, keepdims=True) + LN_EPS)
        return cen * rstd, rstd

    LB = 64

    def norms(l, i):
        g1, b1, g2, b2 = (VEC[l, k:k + 1, :] for k in range(4))

        def step(b, carry):
            hf = H[l, rows(i * C + b * LB, LB), :].astype(F32)
            xhat, unused = stats(hf)
            AS[rows(b * LB, LB), :] = (xhat * g1 + b1).astype(BF16)
            MS[rows(b * LB, LB), :] = (xhat * g2 + b2).astype(BF16)
            return carry
        lax.fori_loop(0, C // LB, step, 0)

    def forward(l, i):
        r0, r1 = i * C, (i + 1) * C
        norms(l, i)
        qkv = nn(AS[...], WQ[l]) + VEC[l, 7:8, 0:3 * E2]
        qkv = qkv.astype(BF16).astype(F32)
        t = tabs(i)
        q = rotate(qkv[:, 0:E2], t).astype(BF16)
        kf = rotate(qkv[:, E2:2 * E2], t)
        vf = qkv[:, 2 * E2:3 * E2]
        Q[l, r0:r1, :] = q
        K[l, r0:r1, :] = kf.astype(BF16)
        V[l, r0:r1, :] = vf.astype(BF16)
        KT[l, :, r0:r1] = jnp.transpose(kf).astype(BF16)
        VT[:, r0:r1] = jnp.transpose(vf).astype(BF16)
        RBK = C // 2
        outs = []
        for h in range(2):
            qm = jnp.where(head_lane == h, Q[l, r0:r1, :].astype(F32), 0.0).astype(BF16)
            ST[0:r1, :] = nt(K[l, 0:r1, :], qm)
            ST[r0:r1, :] = jnp.where(lower, ST[r0:r1, :], -1e30)

            def top(b, m):
                return jnp.maximum(m, jnp.max(ST[rows(b * RBK, RBK), :].reshape(RBK // 8, 8, C), axis=0))
            m = jnp.max(lax.fori_loop(0, r1 // RBK, top, jnp.full((8, C), -3e38, F32)), axis=0, keepdims=True)
            mc = m * c1

            def expo(b, tot):
                e = jnp.exp2(ST[rows(b * RBK, RBK), :] * c1 - mc)
                ST[rows(b * RBK, RBK), :] = e
                return tot + jnp.sum(e.reshape(RBK // 8, 8, C), axis=0)
            tot = jnp.sum(lax.fori_loop(0, r1 // RBK, expo, jnp.zeros((8, C), F32)), axis=0, keepdims=True)
            inv = 1.0 / tot

            def put(b, carry):
                PX[i][l, h, rows(b * RBK, RBK), :] = (ST[rows(b * RBK, RBK), :] * inv).astype(BF16)
                return carry
            lax.fori_loop(0, r1 // RBK, put, 0)
            outs.append(nn(VT[:, 0:r1], PX[i][l, h]))
        ctx = jnp.transpose(jnp.where(sub_head == 0, outs[0], outs[1])).astype(BF16)
        CTX[l, r0:r1, :] = ctx
        PF[r0:r1, :] = nn(ctx, WO[l])
        PRE[...] = nn(MS[...], WU[l])
        bup = VEC[l, 6:7, :]
        GB = 32

        def act(b, carry):
            u = PRE[rows(b * GB, GB), :] + bup
            cdf = 0.5 * (1.0 + lax.erf(u * RSQRT2))
            pdf = jnp.exp2(u * u * (-0.5 * LOG2E)) * INV_SQRT_2PI
            HID[l, rows(r0 + b * GB, GB), :] = (u * cdf).astype(BF16)
            GP[l, rows(r0 + b * GB, GB), :] = cdf + u * pdf
            return carry
        lax.fori_loop(0, C // GB, act, 0)
        PF[r0:r1, :] += nn(HID[l, r0:r1, :], WD[l])

    def backward(l, dl, i, last):
        r0, r1 = i * C, (i + 1) * C
        par = l % 2
        first = i == NC - 1

        def acc(ref, val):
            if first:
                ref[par] = val
            else:
                ref[par] += val

        def acc_row(k, val, w=D):
            GV[l, k:k + 1, 0:w] += val

        norms(l, i)
        dy = H[dl, r0:r1, :]
        acc_row(4, jnp.sum(dy.astype(F32), axis=0, keepdims=True))
        PRE[...] = nt(dy, WD[l])
        GB = 32

        def act(b, tot):
            d = PRE[rows(b * GB, GB), :] * GP[l, rows(r0 + b * GB, GB), :]
            DPB[rows(b * GB, GB), :] = d.astype(BF16)
            return tot + jnp.sum(d.reshape(GB // 8, 8, F), axis=0)
        dbu = lax.fori_loop(0, C // GB, act, jnp.zeros((8, F), F32))
        acc_row(5, jnp.sum(dbu, axis=0, keepdims=True))
        acc(GD, tn(HID[l, r0:r1, :], dy))
        acc(GU, tn(MS[...], DPB[...]))
        f0 = pf_row(i, True)
        PF[f0:f0 + C, :] = nt(DPB[...], WU[l])
        dctx = nt(dy, WO[l]).astype(BF16)
        ctx = CTX[l, r0:r1, :]
        acc(GO, tn(ctx, dy))
        prod = dctx.astype(F32) * ctx.astype(F32)
        q = Q[l, r0:r1, :].astype(F32)
        dcf = dctx.astype(F32)
        RBK = C // 2
        dqt = []
        for h in range(2):
            sel = head_lane == h
            qm = jnp.where(sel, q, 0.0).astype(BF16)
            dcm = jnp.where(sel, dcf, 0.0).astype(BF16)
            dsum = jnp.transpose(jnp.where(sel, prod, 0.0))
            drow = jnp.sum(dsum, axis=0, keepdims=True)
            ST[0:r1, :] = nt(V[l, 0:r1, :], dcm)

            def sub(b, carry):
                pr = PX[i][l, h, rows(b * RBK, RBK), :].astype(F32)
                DS[rows(b * RBK, RBK), :] = (pr * (ST[rows(b * RBK, RBK), :] - drow)).astype(BF16)
                return carry
            lax.fori_loop(0, r1 // RBK, sub, 0)
            dk = nn(DS[0:r1, :], qm)
            dv = nn(PX[i][l, h], dcm)
            if first and h == 0:
                DK[0:r1, :] = dk
                DV[0:r1, :] = dv
            else:
                DK[0:r1, :] += dk
                DV[0:r1, :] += dv
            dqt.append(nn(KT[l, :, 0:r1], DS[0:r1, :]))
        scale = E ** -0.5
        t = tabs(i)
        dq = unrotate(jnp.transpose(jnp.where(sub_head == 0, dqt[0], dqt[1])) * scale, t)
        dk = unrotate(DK[r0:r1, :] * scale, t)
        dv = DV[r0:r1, :]
        dqkv = jnp.concatenate([dq, dk, dv], axis=1)
        acc_row(6, jnp.sum(dqkv, axis=0, keepdims=True), 3 * E2)
        dqkv = dqkv.astype(BF16)
        acc(GQ, tn(AS[...], dqkv))
        PRE[...] = nt(dqkv, WQ[l])
        g1, g2 = VEC[l, 0:1, :], VEC[l, 2:3, :]

        def lnb(b, tots):
            hf = H[l, rows(r0 + b * LB, LB), :].astype(F32)
            xhat, rstd = stats(hf)
            da = PRE[rows(b * LB, LB), :]
            dm = PF[rows(f0 + b * LB, LB), :]
            dx = da * g1 + dm * g2
            m1 = jnp.mean(dx, axis=-1, keepdims=True)
            m2 = jnp.mean(dx * xhat, axis=-1, keepdims=True)
            if not last:
                PF[rows(f0 + b * LB, LB), :] = rstd * (dx - m1 - xhat * m2)
            terms = (da * xhat, da, dm * xhat, dm)
            return tuple(a + jnp.sum(v.reshape(LB // 8, 8, D), axis=0) for a, v in zip(tots, terms))
        tots = lax.fori_loop(0, C // LB, lnb, tuple(jnp.zeros((8, D), F32) for _ in range(4)))
        for k in range(4):
            acc_row(k, jnp.sum(tots[k], axis=0, keepdims=True))

    def g_half(a, k):
        return rows(k * G_HALF[a], G_HALF[a])

    def r1_view(l, a):
        return GP.at[l + 1, R1_OFF[a]:R1_OFF[a] + G_HALF[a], 0:G_COLS[a]]

    def g1_copy(l, a):
        return rcopy(G_BUF[a].at[l % 2, g_half(a, 1 - c)], r1_view(l, a), g1s.at[a], g1r.at[l % 2, a], pp=sib)

    def g2_copy(l, a):
        return rcopy(HID.at[l, R1_OFF[a]:R1_OFF[a] + G_HALF[a], 0:G_COLS[a]], R2[a].at[l % 2], g2s.at[a], g2r.at[l % 2, a], pp=2 * (l // 2) + c)

    def g3_local(l, a):
        return lcopy(G_BUF[a].at[l % 2, g_half(a, c)], G_OUT[a].at[g_half(a, c)], g3s.at[a])

    def g3_remote(l, a):
        return rcopy(G_BUF[a].at[l % 2, g_half(a, c)], G_OUT[a].at[g_half(a, c)], g3s.at[a], g3r.at[a], pp=sib)

    def v1_copies(l):
        return [rcopy(GV.at[l], ZR.at[l, z], v1s.at[l, o - 1], v1r.at[l, z], tp=(z + o) % NT) for o in range(1, NT)]

    def grads_out(l):
        for a in range(4):
            g1_copy(l, a).start()
        for cp in v1_copies(l):
            cp.start()

    def grads_mid(l):
        for a in range(4):
            g1_copy(l, a).wait_recv()
            n = G_HALF[a]
            nb = n // 32

            def add(b, carry):
                rr = rows(c * n + b * 32, 32)
                tot = G_BUF[a][l % 2, rr, :] + GP[l + 1, rows(R1_OFF[a] + b * 32, 32), 0:G_COLS[a]]
                G_BUF[a][l % 2, rr, :] = tot
                HID[l, rows(R1_OFF[a] + b * 32, 32), 0:G_COLS[a]] = tot.astype(BF16)
                return carry
            lax.fori_loop(0, nb, add, 0)

            @pl.when(l // 2 != ys_)
            def _():
                g2_copy(l, a).start()

    def grads_last(l):
        @pl.when(l // 2 == ys_)
        def _():
            for a in range(4):
                g2_copy(l, a).wait_recv()
                n = G_HALF[a]

                def add(b, carry):
                    rr = rows(c * n + b * 32, 32)
                    G_BUF[a][l % 2, rr, :] += R2[a][l % 2, rows(b * 32, 32), :].astype(F32)
                    return carry
                lax.fori_loop(0, n // 32, add, 0)

                @pl.when(l == s)
                def _():
                    g3_local(l, a).start()

                @pl.when(l != s)
                def _():
                    g3_remote(l, a).start()

    def grads_done(l):
        for a in range(4):
            g1_copy(l, a).wait_send()

            @pl.when(l // 2 != ys_)
            def _():
                g2_copy(l, a).wait_send()

            @pl.when(l == s)
            def _():
                g3_local(l, a).wait()

            @pl.when((l // 2 == ys_) & (l != s))
            def _():
                g3_remote(l, a).wait_send()

    def v2_copy(l):
        return rcopy(GZ.at[l], PR.at[s], v2s.at[l], v2r.at[s], pp=l)

    def vec_mid(l):
        ZR[l, z] = GV[l]
        for o in range(1, NT):
            q = (z + o) % NT
            rcopy(GV.at[l], ZR.at[l, q], v1s.at[l, o - 1], v1r.at[l, q], tp=q).wait_recv()
        tot = ZR[l, 0] + ZR[l, 1] + ZR[l, 2] + ZR[l, 3]
        row = lax.broadcasted_iota(jnp.int32, (8, D), 0)
        GZ[l] = jnp.where(row < 4, tot, GV[l])

        @pl.when(l == s)
        def _():
            PR[s] = GZ[l]

        @pl.when(l != s)
        def _():
            v2_copy(l).start()

    GV[...] = jnp.zeros_like(GV)
    fetch(0)
    xcopy.wait()

    def fwd_layer(l, carry):
        for i in range(NC):
            @pl.when(l > 0)
            def _():
                ar_wait(l - 1, l, i)
            forward(l, i)
            ar_send(l, i)
            if i == 0:
                @pl.when(l > 0)
                def _():
                    ar_last(l - 1, l - 1, l, 2)
                    ar_mid(l - 1, 3)
            elif i == 1:
                @pl.when(l > 0)
                def _():
                    ar_last(l - 1, l - 1, l, 3)
                ar_mid(l, 0)

                @pl.when(l == 0)
                def _():
                    gcopy.wait()
                    H[NL + 1] = GP[NL].astype(BF16)
            else:
                ar_last(l, l, l + 1, i - 2)
                ar_mid(l, i - 1)

            if i == 2:
                @pl.when((l == 0) & (s == 1))
                def _():
                    start_all(y_copies())

        @pl.when(l < NL - 1)
        def _():
            fetch(l + 1)
        return carry
    lax.fori_loop(0, NL, fwd_layer, 0)

    def y_copies_out():
        return [rcopy(H.at[NL], y.at[ys_, c], ys.at[o], yr.at[s], pp=(s + o) % NL) for o in range(1, NL)]

    y_local = lcopy(H.at[NL], y.at[ys_, c], ys.at[0])

    def ri(l):
        return jnp.where(l == NL - 1, NL + 1, l + 1)

    def bwd_layer(lb, carry):
        l = NL - 1 - lb
        p = NL + lb
        for n in range(NC):
            i = NC - 1 - n

            @pl.when(lb > 0)
            def _():
                ar_wait(p - 1, l + 1, i)
            backward(l, ri(l), i, False)

            @pl.when(l > 0)
            def _():
                ar_send(p, i, True)
            if n == 0:
                @pl.when(lb == 0)
                def _():
                    ar_last(NL - 1, NL - 1, NL, 2)
                    ar_mid(NL - 1, 3)

                @pl.when(lb > 0)
                def _():
                    ar_last(p - 1, ri(l + 1), l + 1, 1)
                    ar_mid(p - 1, 0, True)
                    grads_mid(l + 1)
            elif n == 1:
                @pl.when(lb == 0)
                def _():
                    ar_last(NL - 1, NL - 1, NL, 3)

                @pl.when(lb > 0)
                def _():
                    ar_last(p - 1, ri(l + 1), l + 1, 0)
                    vec_mid(l + 1)

                @pl.when(l > 0)
                def _():
                    ar_mid(p, NC - 1, True)
            else:
                @pl.when(l > 0)
                def _():
                    ar_last(p, ri(l), l, NC - 1 - (n - 2))
                    ar_mid(p, NC - 1 - (n - 1), True)
                if n == 2:
                    @pl.when(lb == 0)
                    def _():
                        for j in range(NC):
                            ar_wait(NL - 1, NL, j)
                        y_local.start()
                        start_all(y_copies_out())

                    @pl.when(lb > 0)
                    def _():
                        grads_last(l + 1)

        @pl.when(lb > 0)
        def _():
            grads_done(l + 1)
        grads_out(l)
        return carry
    lax.fori_loop(0, NL, bwd_layer, 0)

    grads_mid(0)
    vec_mid(0)
    grads_last(0)
    grads_done(0)

    for o in range(1, NL):
        q = (s + o) % NL
        rcopy(GZ.at[0], PR.at[q], v2s.at[0], v2r.at[q], pp=q).wait_recv()
    PRE[0:8, 0:D] = PR[0] + PR[1] + PR[2] + PR[3]
    vout = lcopy(PRE.at[0:8, 0:D], ovec, osem.at[0])
    vout.start()
    for l in range(NL):
        for cp in v1_copies(l):
            cp.wait_send()
    for l in range(NL):
        @pl.when(l != s)
        def _():
            v2_copy(l).wait_send()
    for a in range(4):
        rcopy(G_OUT[a].at[g_half(a, 1 - c)], G_OUT[a].at[g_half(a, 1 - c)], g3s.at[a], g3r.at[a], pp=sib).wait_recv()
    y_local.wait()
    for o, cp in enumerate(y_copies_out()):
        cp.wait_send()
        q = (s + o + 1) % NL
        rcopy(H.at[NL], y.at[q // 2, q % 2], ys.at[o + 1], yr.at[q], pp=q).wait_recv()
    for cp in sib_copies():
        cp.wait_send()
    for cp in y_copies():
        cp.wait_send()
    for k in range(2):
        for a in range(4):
            fwd_copy(oy + k, a).wait_send()

    @pl.when(is_end)
    def _():
        for t in range(NC * SUB):
            end_copy(0, t).wait_send()

    @pl.when(inner)
    def _():
        for t in range(NC * SUB):
            peer_copy(0, t).wait_send()
            back_copy(0, 1, t).wait_send()
    vout.wait()


def group_step(dims, x, g, wqkv, wo, wup, wdn, vec, tab):
    S, D, E, C, F = dims
    E2 = 2 * E
    hbm = pl.BlockSpec(memory_space=pl.ANY)
    out_shape = [
        jax.ShapeDtypeStruct(x.shape, BF16),
        jax.ShapeDtypeStruct((D, 3 * E2), F32),
        jax.ShapeDtypeStruct((E2, D), F32),
        jax.ShapeDtypeStruct((D, F), F32),
        jax.ShapeDtypeStruct((F, D), F32),
        jax.ShapeDtypeStruct((8, D), F32),
    ]

    def vm(*shape, dtype=BF16):
        return pltpu.VMEM(shape, dtype)
    dma = pltpu.SemaphoreType.DMA
    scratch = [
        vm(NL, D, 3 * E2), vm(NL, E2, D), vm(NL, D, F), vm(NL, F, D), vm(NL, 8, D, dtype=F32),
        vm(NL + 2, S, D),
        vm(NL, S, E2), vm(NL, S, E2), vm(NL, S, E2), vm(NL, E2, S), vm(E2, S), vm(NL, S, E2),
        *[vm(NL, 2, (i + 1) * C, C) for i in range(NC)],
        vm(NL, S, F), vm(NL + 1, S, F, dtype=F32),
        vm(2, S, D), vm(2, S, D), vm(S, D), vm(S + C, D, dtype=F32),
        vm(2, D, 3 * E2, dtype=F32), vm(2, E2, D, dtype=F32), vm(2, D, F, dtype=F32), vm(2, F, D, dtype=F32),
        vm(2, D // 2, 3 * E2), vm(2, E, D), vm(2, D // 2, F), vm(2, F // 2, D),
        vm(S, E2, dtype=F32), vm(S, E2, dtype=F32),
        vm(2, C + 8, E2, dtype=F32), vm(S, E2, dtype=F32), vm(S, E2, dtype=F32),
        vm(NL, 8, D, dtype=F32), vm(NL, NT, 8, D, dtype=F32), vm(NL, 8, D, dtype=F32), vm(NL, 8, D, dtype=F32),
        vm(C, D), vm(C, D), vm(C, max(D, F), dtype=F32), vm(C, F), vm(S, C), vm(S, C, dtype=F32),
        dma((5,)), dma((19,)), dma((NL, 9)), dma((2, 4)), dma((2,)), dma((1,)),
        dma((NC * SUB,)), dma((NC * SUB,)), dma((2, NC * SUB)), dma((2, NC * SUB)), dma((2, NC * SUB)),
        dma((NL,)), dma((NL,)), dma((4,)), dma((2, 4)), dma((4,)), dma((2, 4)), dma((4,)), dma((4,)),
        dma((NL, NT - 1)), dma((NL, NT)), dma((NL,)), dma((NL,)), dma((1,)),
    ]
    return pl.pallas_call(
        functools.partial(body, dims),
        out_shape=out_shape,
        in_specs=[hbm] * 8,
        out_specs=[hbm] * 6,
        scratch_shapes=scratch,
        compiler_params=pltpu.CompilerParams(collective_id=0, has_side_effects=True, vmem_limit_bytes=67043328),
        name='neox_group',
    )(x, g, wqkv, wo, wup, wdn, vec, tab)


def solution(mesh):
    def device_fn(x_in, g_out, ln1_gain, ln1_bias, w_qkv, b_qkv, w_out, b_out, ln2_gain, ln2_bias, w_up, b_up, w_down, b_down):
        n_micro, n_rows, S, D = x_in.shape
        heads, E = w_qkv.shape[2], w_qkv.shape[4]
        F = w_up.shape[2]
        C = S // NC
        qcols = heads * 3 * E
        wqkv = jnp.transpose(w_qkv[0], (0, 2, 1, 3)).reshape(D, qcols)
        bqkv = jnp.transpose(b_qkv[0], (1, 0, 2)).reshape(1, qcols).astype(F32)
        bqkv = jnp.pad(bqkv, ((0, 0), (0, D - qcols)))
        vec = jnp.concatenate([ln1_gain, ln1_bias, ln2_gain, ln2_bias, b_out.astype(F32), b_down.astype(F32), b_up.astype(F32), bqkv], axis=0)
        tab = jnp.asarray(rotary_base(C, NC, E, heads))
        y, gqkv, go, gup, gdn, gvec = group_step((S, D, E, C, F), x_in, g_out, wqkv, w_out[0].reshape(heads * E, D), w_up[0], w_down[0], vec, tab)
        gq = jnp.transpose(gqkv.reshape(D, 3, heads, E), (0, 2, 1, 3))[None]
        gbq = jnp.transpose(gvec[6, :qcols].reshape(3, heads, E), (1, 0, 2))[None]
        bias_out = gvec[4:5]
        return (y, gvec[0:1], gvec[1:2], gq, gbq, go.reshape(1, heads, E, D), bias_out, gvec[2:3], gvec[3:4], gup[None], gvec[5:6], gdn[None], bias_out)

    return jax.shard_map(device_fn, mesh=mesh, in_specs=(P('dp'), P('dp')) + STAGE_SPECS, out_specs=(P('dp'),) + GRAD_SPECS, check_vma=False)
```

time: 2660 us -> 290 us (0.11)
  waiting for transfers between devices: 1680 us -> 0 us
  matrix products: 574 us -> 0 us
  Pallas kernels: 0 us -> 271 us
  other arithmetic: 233 us -> 0.01 us
  local copies, waits for them, and re-layouts: 87.7 us -> 17.2 us
  loops' own time: 29.7 us -> 0 us
    psum x11 -> x0, waiting for transfers between devices: 1240 us -> none  [the longest x5 753 us: stage_forward(): mlp_sum = lax.psum(mlp_part.astype(jnp.bfloat16), 'tp')]
    dot_general x90 -> x0, matrix products: 459 us -> none  [the longest x10 108 us: attention_core(): jnp.einsum('bqhe,bkhe->bhqk', query, key_rot, preferred_element_type=jnp....]
    all_gather x10 -> x0, waiting for transfers between devices: 422 us -> none  [pass_on(): return lax.all_gather(arrived, 'tp', axis=1, tiled=True)]
    pallas_call x0 -> x1, Pallas kernels: none -> 271 us  [group_step(): pl.pallas_call(functools.partial(body, dims), out_shape=out_shape, in_spe...]
    sub x10 -> x0, matrix products: 115 us -> none  [attention_core(): probs = jax.nn.softmax(scores, axis=-1).astype(jnp.bfloat16)]
    reduce_sum x30 -> x0, other arithmetic: 63.5 us -> none  [the longest x5 22 us: norm_core(): return center * lax.rsqrt(var_term + LN_EPS) * gain + shift]
    convert_element_type x50 -> x0, other arithmetic: 49 us -> none  [the longest x5 20.7 us: stage_backward(): grad_branch = lax.psum((grad_h1 + grad_h2).astype(jnp.bfloat16), 'tp')]
    another operation x15 -> x0, other arithmetic: 47.3 us -> none  [the longest x5 46.4 us: stage_backward(): jax.nn.gelu(act_in, approximate=False)]
  transfers between devices with their start and end apart: 31 -> 0, of which waited for: 31 -> 0; matrix products, arithmetic and copies ran while one was open for 4% -> 0% of each run, Pallas kernels for 0% -> 0%
where the time goes in v1:
time: 290 us; the launch traced here: 289 us
  Pallas kernels  271 us (93%)
  local copies, waits for them, and re-layouts  17.2 us (6%)
    pallas_call x1, Pallas kernels, group_step(): pl.pallas_call(functools.partial(body, dims), out_shape=out_shape, in_spe...  271 us
    unnamed x15, local copies, waits for them, and re-layouts  9.81 us

profile of v1, /device:TPU:0, one launch (start us, length us, event | category | flops | bytes accessed | tf_op | source)
XLA Modules:
  0.0 289.1 jit_solution(14479846612530204495)
XLA Ops:
  0.6 0.8 convert_element_type.34
  1.4 1.4 concatenate.3.vec
  2.8 1.0 copy.30
  3.9 0.9 copy.31.wqkv
  4.8 271.2 %neox_group.1 = (bf16[2,2,1024,512]{3,2,1,0:T(8,128)(2,1)}, f32[512,384]{1,0:T(8,128)}, f32[128,512]{1,0:T(8,128)}, f32[512,512]{1,0:T(8,128)}, f32[512,512]{1,0:T(8,128)}, /*index=5*/f32[8,512]{1,0:T(8,128)}) custom-call(bf16[2,2,1024,512]{3,2,1,0:T(8,128)(2,1)} %x.3, f32[2,2,1024,512]{3,2,1,0:T(8,128)} %g.1, bf16[512,384]{1,0:T(8,128)(2,1)} %copy.31.wqkv, ...), custom_call_target="tpu_custom_call" | custom-call | tf_op jit(solution)/shard_map/neox_group/pallas_call | solution.py:706
  275.9 0.7 slice_reduce_fusion
  276.7 1.5 fusion
  278.2 0.0 copy-start.3
  278.2 0.7 reshape_squeeze.7
  278.9 1.4 copy.32
  280.3 0.9 copy.33
  281.2 0.6 copy.39
  281.8 0.0 copy-start.2
  281.8 0.0 copy-start.1
  281.8 0.0 copy-start
  281.8 4.6 %copy.40 = bf16[2,2,1024,512]{3,2,1,0:T(8,128)(2,1)} copy(bf16[2,2,1024,512]{3,2,1,0:T(8,128)(2,1)} %get-tuple-element.83) | data formatting | bytes 8388608
  286.4 0.0 copy-done.3
  286.4 0.0 copy-done.2
  286.4 0.7 copy.41
  287.1 0.0 copy-done.1
  287.1 1.0 copy.42
  288.1 0.0 copy-done
  288.1 1.0 copy.43
  (1 shorter events, 0.0 us)
Async XLA Ops:
  278.2 8.2 %copy-start.3 = (f32[1,512]{1,0:T(1,128)}, f32[1,512]{1,0:T(1,128)S(1)}, u32[]{:S(2)}) copy-start(f32[1,512]{1,0:T(1,128)S(1)} %get-tuple-element.89) | copy-start | bytes 6148
  281.8 4.6 %copy-start.2 = (f32[128,512]{1,0:T(8,128)S(1)}, f32[128,512]{1,0:T(8,128)}, u32[]{:S(2)}) copy-start(f32[128,512]{1,0:T(8,128)} %get-tuple-element.22) | copy-start | bytes 786436
  281.8 5.3 %copy-start.1 = (f32[512,512]{1,0:T(8,128)S(1)}, f32[512,512]{1,0:T(8,128)}, u32[]{:S(2)}) copy-start(f32[512,512]{1,0:T(8,128)} %get-tuple-element.23) | copy-start | bytes 3145732
  281.8 6.3 %copy-start = (f32[512,512]{1,0:T(8,128)S(1)}, f32[512,512]{1,0:T(8,128)}, u32[]{:S(2)}) copy-start(f32[512,512]{1,0:T(8,128)} %get-tuple-element.24) | copy-start | bytes 3145732

commit v2 on v1

--- a/solution.py
+++ b/solution.py
@@ -11,15 +11,20 @@
 
 ROPE_BASE = 10000.0
 LN_EPS = 1e-5
-STAGE_SPECS = (P('pp', None), P('pp', None), P('pp', None, 'tp', None, None), P('pp', 'tp', None, None), P('pp', 'tp', None, None), P('pp', None), P('pp', None), P('pp', None), P('pp', None, 'tp'), P('pp', 'tp'), P('pp', 'tp', None), P('pp', None))
-GRAD_SPECS = (P(('dp', 'pp'), None), P(('dp', 'pp'), None), P(('dp', 'pp'), None, 'tp', None, None), P(('dp', 'pp'), 'tp', None, None), P(('dp', 'pp'), 'tp', None, None), P(('dp', 'pp'), None), P(('dp', 'pp'), None), P(('dp', 'pp'), None), P(('dp', 'pp'), None, 'tp'), P(('dp', 'pp'), 'tp'), P(('dp', 'pp'), 'tp', None), P(('dp', 'pp'), None))
+STAGE_SPECS = (P('pp'), P('pp'), P('pp', None, 'tp'), P('pp', 'tp'), P('pp', 'tp'), P('pp'), P('pp'), P('pp'), P('pp', None, 'tp'), P('pp', 'tp'), P('pp', 'tp'), P('pp'))
+OWN = ('dp', 'pp')
+GRAD_SPECS = (P(OWN), P(OWN), P(OWN, None, 'tp'), P(OWN, 'tp'), P(OWN, 'tp'), P(OWN), P(OWN), P(OWN), P(OWN, None, 'tp'), P(OWN, 'tp'), P(OWN, 'tp'), P(OWN))
+
 
 F32 = jnp.float32
 BF16 = jnp.bfloat16
 NL = 4
 NT = 4
 NC = 4
+NA = 4
 SUB = 2
+FWD_AT = {0: (('mid', 1, 0), ('last', 2, 0)), 2: (('mid', 1, 1), ('last', 2, 1))}
+BWD_AT = {0: (('last', 2, 0),), 1: (('mid', 1, 0),), 3: (('last', 2, 1),), 4: (('mid', 1, 1),)}
 LOG2E = 1.4426950408889634
 RSQRT2 = 0.7071067811865476
 INV_SQRT_2PI = 0.3989422804014327
@@ -94,7 +99,7 @@
     gcopy.start()
     tcopy = lcopy(tab, TAB, xs.at[1])
     tcopy.start()
-    for a in range(4):
+    for a in range(NA):
         lcopy(W_IN[a], W_BUF[a].at[s], wl.at[a]).start()
     lcopy(vec, VEC.at[s], wl.at[4]).start()
 
@@ -110,7 +115,7 @@
 
     def sib_copies():
         out = []
-        for a in range(4):
+        for a in range(NA):
             for k in range(2):
                 out.append(rcopy(W_IN[a].at[w_half(a, k)], W_BUF[a].at[s, w_half(a, k)], ws.at[2 * a + k], wr.at[s, 2 * a + k], pp=sib))
         out.append(rcopy(vec, VEC.at[s], ws.at[16], wr.at[s, 8], pp=sib))
@@ -118,7 +123,7 @@
 
     def y_copies():
         out = [rcopy(vec, VEC.at[s], ws.at[17 + k], wr.at[s, 8], pp=oy + k) for k in range(2)]
-        for a in range(4):
+        for a in range(NA):
             for k in range(2):
                 out.append(rcopy(W_IN[a].at[w_half(a, k)], W_BUF[a].at[s, w_half(a, k)], ws.at[8 + 2 * a + k], wr.at[s, 2 * a + k], pp=oy + k))
         return out
@@ -142,7 +147,7 @@
     def fetch(l):
         @pl.when(l == s)
         def _():
-            for a in range(4):
+            for a in range(NA):
                 lcopy(W_IN[a], W_BUF[a].at[s], wl.at[a]).wait()
             lcopy(vec, VEC.at[s], wl.at[4]).wait()
 
@@ -150,22 +155,22 @@
         def _():
             @pl.when(l // 2 == ys_)
             def _():
-                for a in range(4):
+                for a in range(NA):
                     for k in range(2):
                         arrived(l, a, k)
 
             @pl.when(l // 2 != ys_)
             def _():
-                for a in range(4):
+                for a in range(NA):
                     arrived(l, a, c)
                     fwd_copy(l, a).start()
-                for a in range(4):
+                for a in range(NA):
                     arrived(l, a, 1 - c)
             rcopy(VEC.at[l], VEC.at[l], ws.at[16], wr.at[l, 8], pp=sib).wait_recv()
 
     tcopy.wait()
     for i in range(NC):
-        cb, sb = TAB[0, 0:C, :], TAB[1, 0:C, :]
+        cb, sb = TAB[0, :C, :], TAB[1, :C, :]
         cr, sr = TAB[0, C + i:C + i + 1, :], TAB[1, C + i:C + i + 1, :]
         COS[i * C:(i + 1) * C, :] = cb * cr - sb * sr
         SIN[i * C:(i + 1) * C, :] = sb * cr + cb * sr
@@ -214,34 +219,35 @@
                 PS[t * SR:(t + 1) * SR, :] = PF[f0:f0 + SR, :].astype(BF16)
                 end_copy(p, t).start()
 
-    def ar_mid(p, i, back=False):
+    def ar_mid(p, i, u, back=False):
+        t = i * SUB + u
+        r = slice(t * SR, (t + 1) * SR)
+        f0 = pf_row(i, back) + u * SR
+
         @pl.when(inner)
         def _():
-            for t in range(i * SUB, (i + 1) * SUB):
-                end_copy(p, t).wait_recv()
-                @pl.when(p > 0)
-                def _():
-                    peer_copy(p, t).wait_send()
-                r = slice(t * SR, (t + 1) * SR)
-                f0 = pf_row(i, back) + (t - i * SUB) * SR
-                PS[r, :] = (PF[f0:f0 + SR, :] + RA[p % 2, r, :].astype(F32)).astype(BF16)
-                peer_copy(p, t).start()
-
-    def ar_last(p, ri, di, i):
+            end_copy(p, t).wait_recv()
+            @pl.when(p > 0)
+            def _():
+                peer_copy(p, t).wait_send()
+            PS[r, :] = (PF[f0:f0 + SR, :] + RA[p % 2, r, :].astype(F32)).astype(BF16)
+            peer_copy(p, t).start()
+
+    def ar_last(p, ri, di, i, u):
+        t = i * SUB + u
+        r = slice(t * SR, (t + 1) * SR)
+
         @pl.when(inner)
         def _():
-            keep = jnp.where(p < NL, 1.0, 0.0)
             lv = jnp.minimum(p, NL - 1)
-            bias = (VEC[lv, 4:5, :] + VEC[lv, 5:6, :]) * keep
-            for t in range(i * SUB, (i + 1) * SUB):
-                peer_copy(p, t).wait_recv()
-                @pl.when(p > 0)
-                def _():
-                    back_copy(p, di, t).wait_send()
-                r = slice(t * SR, (t + 1) * SR)
-                both = PS[r, :].astype(F32) + RB[p % 2, r, :].astype(F32)
-                H[di, r, :] = (H[ri, r, :].astype(F32) + both + bias).astype(BF16)
-                back_copy(p, di, t).start()
+            bias = (VEC[lv, 4:5, :] + VEC[lv, 5:6, :]) * jnp.where(p < NL, 1.0, 0.0)
+            peer_copy(p, t).wait_recv()
+            @pl.when(p > 0)
+            def _():
+                back_copy(p, di, t).wait_send()
+            both = PS[r, :].astype(F32) + RB[p % 2, r, :].astype(F32)
+            H[di, r, :] = (H[ri, r, :].astype(F32) + both + bias).astype(BF16)
+            back_copy(p, di, t).start()
 
     def ar_wait(p, di, i):
         @pl.when(is_end)
@@ -255,9 +261,10 @@
         return cen * rstd, rstd
 
     LB = 64
+    GR = 32
 
     def norms(l, i):
-        g1, b1, g2, b2 = (VEC[l, k:k + 1, :] for k in range(4))
+        g1, b1, g2, b2 = (VEC[l, k:k + 1, :] for k in range(NA))
 
         def step(b, carry):
             hf = H[l, rows(i * C + b * LB, LB), :].astype(F32)
@@ -270,10 +277,10 @@
     def forward(l, i):
         r0, r1 = i * C, (i + 1) * C
         norms(l, i)
-        qkv = nn(AS[...], WQ[l]) + VEC[l, 7:8, 0:3 * E2]
+        qkv = nn(AS[...], WQ[l]) + VEC[l, 7:8, :3 * E2]
         qkv = qkv.astype(BF16).astype(F32)
         t = tabs(i)
-        q = rotate(qkv[:, 0:E2], t).astype(BF16)
+        q = rotate(qkv[:, :E2], t).astype(BF16)
         kf = rotate(qkv[:, E2:2 * E2], t)
         vf = qkv[:, 2 * E2:3 * E2]
         Q[l, r0:r1, :] = q
@@ -281,11 +288,12 @@
         V[l, r0:r1, :] = vf.astype(BF16)
         KT[l, :, r0:r1] = jnp.transpose(kf).astype(BF16)
         VT[:, r0:r1] = jnp.transpose(vf).astype(BF16)
+        yield
         RBK = C // 2
         outs = []
         for h in range(2):
             qm = jnp.where(head_lane == h, Q[l, r0:r1, :].astype(F32), 0.0).astype(BF16)
-            ST[0:r1, :] = nt(K[l, 0:r1, :], qm)
+            ST[:r1, :] = nt(K[l, :r1, :], qm)
             ST[r0:r1, :] = jnp.where(lower, ST[r0:r1, :], -1e30)
 
             def top(b, m):
@@ -304,9 +312,12 @@
                 PX[i][l, h, rows(b * RBK, RBK), :] = (ST[rows(b * RBK, RBK), :] * inv).astype(BF16)
                 return carry
             lax.fori_loop(0, r1 // RBK, put, 0)
-            outs.append(nn(VT[:, 0:r1], PX[i][l, h]))
+            outs.append(nn(VT[:, :r1], PX[i][l, h]))
+            if h == 0:
+                yield
         ctx = jnp.transpose(jnp.where(sub_head == 0, outs[0], outs[1])).astype(BF16)
         CTX[l, r0:r1, :] = ctx
+        yield
         PF[r0:r1, :] = nn(ctx, WO[l])
         PRE[...] = nn(MS[...], WU[l])
         bup = VEC[l, 6:7, :]
@@ -321,6 +332,7 @@
             return carry
         lax.fori_loop(0, C // GB, act, 0)
         PF[r0:r1, :] += nn(HID[l, r0:r1, :], WD[l])
+        yield
 
     def backward(l, dl, i, last):
         r0, r1 = i * C, (i + 1) * C
@@ -334,7 +346,7 @@
                 ref[par] += val
 
         def acc_row(k, val, w=D):
-            GV[l, k:k + 1, 0:w] += val
+            GV[l, k:k + 1, :w] += val
 
         norms(l, i)
         dy = H[dl, r0:r1, :]
@@ -349,9 +361,11 @@
         dbu = lax.fori_loop(0, C // GB, act, jnp.zeros((8, F), F32))
         acc_row(5, jnp.sum(dbu, axis=0, keepdims=True))
         acc(GD, tn(HID[l, r0:r1, :], dy))
+        yield
         acc(GU, tn(MS[...], DPB[...]))
         f0 = pf_row(i, True)
         PF[f0:f0 + C, :] = nt(DPB[...], WU[l])
+        yield
         dctx = nt(dy, WO[l]).astype(BF16)
         ctx = CTX[l, r0:r1, :]
         acc(GO, tn(ctx, dy))
@@ -366,22 +380,23 @@
             dcm = jnp.where(sel, dcf, 0.0).astype(BF16)
             dsum = jnp.transpose(jnp.where(sel, prod, 0.0))
             drow = jnp.sum(dsum, axis=0, keepdims=True)
-            ST[0:r1, :] = nt(V[l, 0:r1, :], dcm)
+            ST[:r1, :] = nt(V[l, :r1, :], dcm)
 
             def sub(b, carry):
                 pr = PX[i][l, h, rows(b * RBK, RBK), :].astype(F32)
                 DS[rows(b * RBK, RBK), :] = (pr * (ST[rows(b * RBK, RBK), :] - drow)).astype(BF16)
                 return carry
             lax.fori_loop(0, r1 // RBK, sub, 0)
-            dk = nn(DS[0:r1, :], qm)
+            dk = nn(DS[:r1, :], qm)
             dv = nn(PX[i][l, h], dcm)
             if first and h == 0:
-                DK[0:r1, :] = dk
-                DV[0:r1, :] = dv
+                DK[:r1, :] = dk
+                DV[:r1, :] = dv
             else:
-                DK[0:r1, :] += dk
-                DV[0:r1, :] += dv
-            dqt.append(nn(KT[l, :, 0:r1], DS[0:r1, :]))
+                DK[:r1, :] += dk
+                DV[:r1, :] += dv
+            dqt.append(nn(KT[l, :, :r1], DS[:r1, :]))
+            yield
         scale = E ** -0.5
         t = tabs(i)
         dq = unrotate(jnp.transpose(jnp.where(sub_head == 0, dqt[0], dqt[1])) * scale, t)
@@ -392,6 +407,7 @@
         dqkv = dqkv.astype(BF16)
         acc(GQ, tn(AS[...], dqkv))
         PRE[...] = nt(dqkv, WQ[l])
+        yield
         g1, g2 = VEC[l, 0:1, :], VEC[l, 2:3, :]
 
         def lnb(b, tots):
@@ -406,50 +422,50 @@
                 PF[rows(f0 + b * LB, LB), :] = rstd * (dx - m1 - xhat * m2)
             terms = (da * xhat, da, dm * xhat, dm)
             return tuple(a + jnp.sum(v.reshape(LB // 8, 8, D), axis=0) for a, v in zip(tots, terms))
-        tots = lax.fori_loop(0, C // LB, lnb, tuple(jnp.zeros((8, D), F32) for _ in range(4)))
-        for k in range(4):
+        tots = lax.fori_loop(0, C // LB, lnb, tuple(jnp.zeros((8, D), F32) for _ in range(NA)))
+        for k in range(NA):
             acc_row(k, jnp.sum(tots[k], axis=0, keepdims=True))
+        yield
 
     def g_half(a, k):
         return rows(k * G_HALF[a], G_HALF[a])
 
     def r1_view(l, a):
-        return GP.at[l + 1, R1_OFF[a]:R1_OFF[a] + G_HALF[a], 0:G_COLS[a]]
+        return GP.at[l + 1, R1_OFF[a]:R1_OFF[a] + G_HALF[a], :G_COLS[a]]
 
     def g1_copy(l, a):
         return rcopy(G_BUF[a].at[l % 2, g_half(a, 1 - c)], r1_view(l, a), g1s.at[a], g1r.at[l % 2, a], pp=sib)
 
     def g2_copy(l, a):
-        return rcopy(HID.at[l, R1_OFF[a]:R1_OFF[a] + G_HALF[a], 0:G_COLS[a]], R2[a].at[l % 2], g2s.at[a], g2r.at[l % 2, a], pp=2 * (l // 2) + c)
+        return rcopy(HID.at[l, R1_OFF[a]:R1_OFF[a] + G_HALF[a], :G_COLS[a]], R2[a].at[l % 2], g2s.at[l % 2, a], g2r.at[l % 2, a], pp=2 * (l // 2) + c)
 
     def g3_local(l, a):
-        return lcopy(G_BUF[a].at[l % 2, g_half(a, c)], G_OUT[a].at[g_half(a, c)], g3s.at[a])
+        return lcopy(r1_view(l, a), G_OUT[a].at[g_half(a, c)], g3s.at[l % 2, a])
 
     def g3_remote(l, a):
-        return rcopy(G_BUF[a].at[l % 2, g_half(a, c)], G_OUT[a].at[g_half(a, c)], g3s.at[a], g3r.at[a], pp=sib)
+        return rcopy(r1_view(l, a), G_OUT[a].at[g_half(a, c)], g3s.at[l % 2, a], g3r.at[a], pp=sib)
 
     def v1_copies(l):
         return [rcopy(GV.at[l], ZR.at[l, z], v1s.at[l, o - 1], v1r.at[l, z], tp=(z + o) % NT) for o in range(1, NT)]
 
     def grads_out(l):
-        for a in range(4):
+        for a in range(NA):
             g1_copy(l, a).start()
         for cp in v1_copies(l):
             cp.start()
 
     def grads_mid(l):
-        for a in range(4):
+        for a in range(NA):
             g1_copy(l, a).wait_recv()
             n = G_HALF[a]
-            nb = n // 32
 
             def add(b, carry):
-                rr = rows(c * n + b * 32, 32)
-                tot = G_BUF[a][l % 2, rr, :] + GP[l + 1, rows(R1_OFF[a] + b * 32, 32), 0:G_COLS[a]]
-                G_BUF[a][l % 2, rr, :] = tot
-                HID[l, rows(R1_OFF[a] + b * 32, 32), 0:G_COLS[a]] = tot.astype(BF16)
+                rr = rows(R1_OFF[a] + b * GR, GR)
+                tot = G_BUF[a][l % 2, rows(c * n + b * GR, GR), :] + GP[l + 1, rr, :G_COLS[a]]
+                GP[l + 1, rr, :G_COLS[a]] = tot
+                HID[l, rr, :G_COLS[a]] = tot.astype(BF16)
                 return carry
-            lax.fori_loop(0, nb, add, 0)
+            lax.fori_loop(0, n // GR, add, 0)
 
             @pl.when(l // 2 != ys_)
             def _():
@@ -458,15 +474,14 @@
     def grads_last(l):
         @pl.when(l // 2 == ys_)
         def _():
-            for a in range(4):
+            for a in range(NA):
                 g2_copy(l, a).wait_recv()
-                n = G_HALF[a]
 
                 def add(b, carry):
-                    rr = rows(c * n + b * 32, 32)
-                    G_BUF[a][l % 2, rr, :] += R2[a][l % 2, rows(b * 32, 32), :].astype(F32)
+                    rr = rows(R1_OFF[a] + b * GR, GR)
+                    GP[l + 1, rr, :G_COLS[a]] += R2[a][l % 2, rows(b * GR, GR), :].astype(F32)
                     return carry
-                lax.fori_loop(0, n // 32, add, 0)
+                lax.fori_loop(0, G_HALF[a] // GR, add, 0)
 
                 @pl.when(l == s)
                 def _():
@@ -476,10 +491,8 @@
                 def _():
                     g3_remote(l, a).start()
 
-    def grads_done(l):
-        for a in range(4):
-            g1_copy(l, a).wait_send()
-
+    def grads_sent(l):
+        for a in range(NA):
             @pl.when(l // 2 != ys_)
             def _():
                 g2_copy(l, a).wait_send()
@@ -516,32 +529,38 @@
     fetch(0)
     xcopy.wait()
 
+    def run(phases, at, handle):
+        for k, unused in enumerate(phases):
+            for op, lag, u in at.get(k, ()):
+                handle(op, lag, u)
+
     def fwd_layer(l, carry):
         for i in range(NC):
             @pl.when(l > 0)
             def _():
                 ar_wait(l - 1, l, i)
-            forward(l, i)
+
+            def handle(op, lag, u):
+                m = i - lag
+
+                def go(p, j):
+                    if op == 'mid':
+                        ar_mid(p, j, u)
+                    else:
+                        ar_last(p, p, p + 1, j, u)
+                if m >= 0:
+                    go(l, m)
+                else:
+                    @pl.when(l > 0)
+                    def _():
+                        go(l - 1, m + NC)
+            run(forward(l, i), FWD_AT, handle)
             ar_send(l, i)
-            if i == 0:
-                @pl.when(l > 0)
-                def _():
-                    ar_last(l - 1, l - 1, l, 2)
-                    ar_mid(l - 1, 3)
-            elif i == 1:
-                @pl.when(l > 0)
-                def _():
-                    ar_last(l - 1, l - 1, l, 3)
-                ar_mid(l, 0)
-
+            if i == 1:
                 @pl.when(l == 0)
                 def _():
                     gcopy.wait()
                     H[NL + 1] = GP[NL].astype(BF16)
-            else:
-                ar_last(l, l, l + 1, i - 2)
-                ar_mid(l, i - 1)
-
             if i == 2:
                 @pl.when((l == 0) & (s == 1))
                 def _():
@@ -553,10 +572,13 @@
         return carry
     lax.fori_loop(0, NL, fwd_layer, 0)
 
-    def y_copies_out():
-        return [rcopy(H.at[NL], y.at[ys_, c], ys.at[o], yr.at[s], pp=(s + o) % NL) for o in range(1, NL)]
-
     y_local = lcopy(H.at[NL], y.at[ys_, c], ys.at[0])
+    y_sib = rcopy(H.at[NL], y.at[ys_, c], ys.at[1], yr.at[s], pp=sib)
+    y_far = rcopy(H.at[NL], y.at[ys_, c], ys.at[2], yr.at[s], pp=oy + c)
+    y_fwd = rcopy(y.at[1 - ys_, c], y.at[1 - ys_, c], ys.at[3], yr.at[oy + c], pp=sib)
+
+    def y_arrived(q):
+        rcopy(H.at[NL], y.at[q // 2, q % 2], ys.at[1], yr.at[q], pp=sib).wait_recv()
 
     def ri(l):
         return jnp.where(l == NL - 1, NL + 1, l + 1)
@@ -570,63 +592,71 @@
             @pl.when(lb > 0)
             def _():
                 ar_wait(p - 1, l + 1, i)
-            backward(l, ri(l), i, False)
+
+            def handle(op, lag, u):
+                m = n - lag
+
+                def go(q, lq, j):
+                    if op == 'mid':
+                        ar_mid(q, j, u, True)
+                    else:
+                        ar_last(q, ri(lq), lq, j, u)
+                if m >= 0:
+                    @pl.when(l > 0)
+                    def _():
+                        go(p, l, NC - 1 - m)
+                else:
+                    @pl.when(lb > 0)
+                    def _():
+                        go(p - 1, l + 1, -1 - m)
+
+                    @pl.when(lb == 0)
+                    def _():
+                        if op == 'mid':
+                            ar_mid(NL - 1, m + NC, u)
+                        else:
+                            ar_last(NL - 1, NL - 1, NL, m + NC, u)
+            run(backward(l, ri(l), i, False), BWD_AT, handle)
 
             @pl.when(l > 0)
             def _():
                 ar_send(p, i, True)
             if n == 0:
+                @pl.when(lb > 0)
+                def _():
+                    grads_mid(l + 1)
+
+                @pl.when(lb == 2)
+                def _():
+                    y_arrived(oy + c)
+                    y_fwd.start()
+            if n == 1:
+                @pl.when(lb > 0)
+                def _():
+                    vec_mid(l + 1)
+            if n == 2:
                 @pl.when(lb == 0)
                 def _():
-                    ar_last(NL - 1, NL - 1, NL, 2)
-                    ar_mid(NL - 1, 3)
-
-                @pl.when(lb > 0)
-                def _():
-                    ar_last(p - 1, ri(l + 1), l + 1, 1)
-                    ar_mid(p - 1, 0, True)
-                    grads_mid(l + 1)
-            elif n == 1:
-                @pl.when(lb == 0)
-                def _():
-                    ar_last(NL - 1, NL - 1, NL, 3)
-
-                @pl.when(lb > 0)
-                def _():
-                    ar_last(p - 1, ri(l + 1), l + 1, 0)
-                    vec_mid(l + 1)
-
-                @pl.when(l > 0)
-                def _():
-                    ar_mid(p, NC - 1, True)
-            else:
-                @pl.when(l > 0)
-                def _():
-                    ar_last(p, ri(l), l, NC - 1 - (n - 2))
-                    ar_mid(p, NC - 1 - (n - 1), True)
-                if n == 2:
-                    @pl.when(lb == 0)
-                    def _():
-                        for j in range(NC):
-                            ar_wait(NL - 1, NL, j)
-                        y_local.start()
-                        start_all(y_copies_out())
-
-                    @pl.when(lb > 0)
-                    def _():
-                        grads_last(l + 1)
+                    for j in range(NC):
+                        ar_wait(NL - 1, NL, j)
+                    start_all((y_local, y_sib, y_far))
+
+                @pl.when(lb > 1)
+                def _():
+                    grads_last(l + 2)
 
         @pl.when(lb > 0)
         def _():
-            grads_done(l + 1)
+            for a in range(NA):
+                g1_copy(l + 1, a).wait_send()
         grads_out(l)
         return carry
     lax.fori_loop(0, NL, bwd_layer, 0)
 
     grads_mid(0)
+    grads_last(1)
     vec_mid(0)
     grads_last(0)
-    grads_done(0)
 
     for o in range(1, NL):
         q = (s + o) % NL
@@ -641,19 +671,23 @@
         @pl.when(l != s)
         def _():
             v2_copy(l).wait_send()
-    for a in range(4):
+    for a in range(NA):
         rcopy(G_OUT[a].at[g_half(a, 1 - c)], G_OUT[a].at[g_half(a, 1 - c)], g3s.at[a], g3r.at[a], pp=sib).wait_recv()
     y_local.wait()
-    for o, cp in enumerate(y_copies_out()):
+    for cp in (y_sib, y_far, y_fwd):
         cp.wait_send()
-        q = (s + o + 1) % NL
-        rcopy(H.at[NL], y.at[q // 2, q % 2], ys.at[o + 1], yr.at[q], pp=q).wait_recv()
+    y_arrived(sib)
+    y_arrived(oy + 1 - c)
+    for a in range(NA):
+        g1_copy(0, a).wait_send()
+    for l in range(NL):
+        grads_sent(l)
     for cp in sib_copies():
         cp.wait_send()
     for cp in y_copies():
         cp.wait_send()
     for k in range(2):
-        for a in range(4):
+        for a in range(NA):
             fwd_copy(oy + k, a).wait_send()
 
     @pl.when(is_end)
@@ -700,7 +734,7 @@
         vm(C, D), vm(C, D), vm(C, max(D, F), dtype=F32), vm(C, F), vm(S, C), vm(S, C, dtype=F32),
         dma((5,)), dma((19,)), dma((NL, 9)), dma((2, 4)), dma((2,)), dma((1,)),
         dma((NC * SUB,)), dma((NC * SUB,)), dma((2, NC * SUB)), dma((2, NC * SUB)), dma((2, NC * SUB)),
-        dma((NL,)), dma((NL,)), dma((4,)), dma((2, 4)), dma((4,)), dma((2, 4)), dma((4,)), dma((4,)),
+        dma((NL,)), dma((NL,)), dma((4,)), dma((2, 4)), dma((2, 4)), dma((2, 4)), dma((2, 4)), dma((4,)),
         dma((NL, NT - 1)), dma((NL, NT)), dma((NL,)), dma((NL,)), dma((1,)),
     ]
     return pl.pallas_call(

time: 290 us -> 261 us (0.900)
  Pallas kernels: 271 us -> 241 us
    pallas_call x1, Pallas kernels: 271 us -> 241 us  [group_step(): pl.pallas_call(functools.partial(body, dims), out_shape=out_shape, in_spe...]
where the time goes in v2:
time: 261 us; the launch traced here: 259 us
  Pallas kernels  241 us (92%)
  local copies, waits for them, and re-layouts  17.2 us (7%)
    pallas_call x1, Pallas kernels, group_step(): pl.pallas_call(functools.partial(body, dims), out_shape=out_shape, in_spe...  241 us
    unnamed x15, local copies, waits for them, and re-layouts  9.81 us

profile of v2, /device:TPU:0, one launch (start us, length us, event | category | flops | bytes accessed | tf_op | source)
XLA Modules:
  0.0 258.8 jit_solution(15963977902846004960)
XLA Ops:
  0.6 0.8 convert_element_type.34
  1.4 1.4 concatenate.3.vec
  2.8 1.0 copy.30
  3.9 0.9 copy.31.wqkv
  4.8 240.9 %neox_group.1 = (bf16[2,2,1024,512]{3,2,1,0:T(8,128)(2,1)}, f32[512,384]{1,0:T(8,128)}, f32[128,512]{1,0:T(8,128)}, f32[512,512]{1,0:T(8,128)}, f32[512,512]{1,0:T(8,128)}, /*index=5*/f32[8,512]{1,0:T(8,128)}) custom-call(bf16[2,2,1024,512]{3,2,1,0:T(8,128)(2,1)} %x.3, f32[2,2,1024,512]{3,2,1,0:T(8,128)} %g.1, bf16[512,384]{1,0:T(8,128)(2,1)} %copy.31.wqkv, ...), custom_call_target="tpu_custom_call" | custom-call | tf_op jit(solution)/shard_map/neox_group/pallas_call | solution.py:740
  245.7 0.7 slice_reduce_fusion
  246.4 1.5 fusion
  248.0 0.0 copy-start.3
  248.0 0.7 reshape_squeeze.7
  248.6 1.4 copy.32
  250.0 0.9 copy.33
  251.0 0.6 copy.39
  251.5 0.0 copy-start.2
  251.5 0.0 copy-start.1
  251.5 0.0 copy-start
  251.5 4.6 %copy.40 = bf16[2,2,1024,512]{3,2,1,0:T(8,128)(2,1)} copy(bf16[2,2,1024,512]{3,2,1,0:T(8,128)(2,1)} %get-tuple-element.83) | data formatting | bytes 8388608
  256.2 0.0 copy-done.3
  256.2 0.0 copy-done.2
  256.2 0.7 copy.41
  256.9 0.0 copy-done.1
  256.9 1.0 copy.42
  257.8 0.0 copy-done
  257.8 1.0 copy.43
  (1 shorter events, 0.0 us)
Async XLA Ops:
  248.0 8.2 %copy-start.3 = (f32[1,512]{1,0:T(1,128)}, f32[1,512]{1,0:T(1,128)S(1)}, u32[]{:S(2)}) copy-start(f32[1,512]{1,0:T(1,128)S(1)} %get-tuple-element.89) | copy-start | bytes 6148
  251.5 4.6 %copy-start.2 = (f32[128,512]{1,0:T(8,128)S(1)}, f32[128,512]{1,0:T(8,128)}, u32[]{:S(2)}) copy-start(f32[128,512]{1,0:T(8,128)} %get-tuple-element.22) | copy-start | bytes 786436
  251.5 5.3 %copy-start.1 = (f32[512,512]{1,0:T(8,128)S(1)}, f32[512,512]{1,0:T(8,128)}, u32[]{:S(2)}) copy-start(f32[512,512]{1,0:T(8,128)} %get-tuple-element.23) | copy-start | bytes 3145732
  251.5 6.3 %copy-start = (f32[512,512]{1,0:T(8,128)S(1)}, f32[512,512]{1,0:T(8,128)}, u32[]{:S(2)}) copy-start(f32[512,512]{1,0:T(8,128)} %get-tuple-element.24) | copy-start | bytes 3145732

commit v3 on v2

--- a/solution.py
+++ b/solution.py
@@ -42,6 +42,18 @@
     return lax.dot_general(a, b, (((0,), (0,)), ((), ())), preferred_element_type=F32)
 
 
+def col_sum(v):
+    return jnp.sum(v, axis=0, keepdims=True)
+
+
+def row_mean(v):
+    return jnp.mean(v, axis=-1, keepdims=True)
+
+
+def fold(v):
+    return jnp.sum(v.reshape(v.shape[0] // 8, 8, v.shape[1]), axis=0)
+
+
 def rotary_base(chunk, n_chunks, head_dim, n_heads):
     rot_dim = head_dim // 4
     half = rot_dim // 2
@@ -53,12 +65,12 @@
     return np.stack([np.cos(ang), np.sin(ang)]).astype(np.float32)
 
 
-def body(dims, x, g, wqkv, wo, wup, wdn, vec, tab,
+def body(dims, x, g, wqkv, wo, wup, wdn, n0, n1, n2, n3, n4, n5, n6, bq, tab,
          y, oqkv, oo, oup, odn, ovec,
          WQ, WO, WU, WD, VEC, H, Q, K, V, KT, VT, CTX, P0, P1, P2, P3, HID, GP, RA, RB, PS, PF,
          GQ, GO, GU, GD, R2Q, R2O, R2U, R2D, DK, DV, TAB, COS, SIN, GV, ZR, GZ, PR,
-         AS, MS, PRE, DPB, DS, ST,
-         wl, ws, wr, wf, xs, gs, sab, sc, ra_s, rb_s, rc_s, ys, yr, g1s, g1r, g2s, g2r, g3s, g3r, v1s, v1r, v2s, v2r, osem):
+         AS, MS, PRE, DPB, DS, ST, N0, N1, N2, N3, N4, N5, N6, BQ,
+         wl, ws, wr, wf, xs, gs, sab, sc, ra_s, rb_s, rc_s, ys, yr, g1s, g1r, g2s, g2r, g3s, g3r, v1s, v1r, v2s, v2r, osem, ns):
     S, D, E, C, F = dims
     E2 = 2 * E
     SR = C // SUB
@@ -76,12 +88,12 @@
     PX = (P0, P1, P2, P3)
     W_IN = (wqkv, wo, wup, wdn)
     W_BUF = (WQ, WO, WU, WD)
-    W_HALF = (D // 2, E, D // 2, F // 2)
+    W_HALF = (3 * E, E, D // 2, F // 2)
     G_BUF = (GQ, GO, GU, GD)
     G_OUT = (oqkv, oo, oup, odn)
     G_HALF = W_HALF
-    G_COLS = (3 * E2, D, F, D)
-    R1_OFF = (0, D // 2, D // 2 + E, D + E)
+    G_COLS = (D, D, F, D)
+    R1_OFF = (0, 3 * E, 4 * E, 4 * E + D // 2)
     R2 = (R2Q, R2O, R2U, R2D)
 
     def rcopy(src, dst, ss, rs, **dev):
@@ -101,7 +113,9 @@
     tcopy.start()
     for a in range(NA):
         lcopy(W_IN[a], W_BUF[a].at[s], wl.at[a]).start()
-    lcopy(vec, VEC.at[s], wl.at[4]).start()
+    small = [lcopy(a, b, ns.at[k]) for k, (a, b) in enumerate(((n0, N0), (n1, N1), (n2, N2), (n3, N3), (n4, N4), (n5, N5), (n6, N6), (bq, BQ)))]
+    for cp in small:
+        cp.start()
 
     bar = pltpu.get_barrier_semaphore()
     for o in range(1, NT):
@@ -118,19 +132,26 @@
         for a in range(NA):
             for k in range(2):
                 out.append(rcopy(W_IN[a].at[w_half(a, k)], W_BUF[a].at[s, w_half(a, k)], ws.at[2 * a + k], wr.at[s, 2 * a + k], pp=sib))
-        out.append(rcopy(vec, VEC.at[s], ws.at[16], wr.at[s, 8], pp=sib))
+        out.append(rcopy(VEC.at[s], VEC.at[s], ws.at[16], wr.at[s, 8], pp=sib))
         return out
 
     def y_copies():
-        out = [rcopy(vec, VEC.at[s], ws.at[17 + k], wr.at[s, 8], pp=oy + k) for k in range(2)]
+        out = []
         for a in range(NA):
             for k in range(2):
                 out.append(rcopy(W_IN[a].at[w_half(a, k)], W_BUF[a].at[s, w_half(a, k)], ws.at[8 + 2 * a + k], wr.at[s, 2 * a + k], pp=oy + k))
+        out += [rcopy(VEC.at[s], VEC.at[s], ws.at[17 + k], wr.at[s, 8], pp=oy + k) for k in range(2)]
         return out
 
     def start_all(copies):
         for cp in copies:
             cp.start()
+
+    for cp in small:
+        cp.wait()
+    for k, ref in enumerate((N0, N1, N2, N3, N4, N5, N6)):
+        VEC[s, k:k + 1, :] = ref[...].astype(F32)
+    VEC[s, 7:8, :3 * E2] = jnp.concatenate([BQ[k, h:h + 1, :].astype(F32) for k in range(3) for h in range(2)], axis=1)
 
     @pl.when(s != 1)
     def _():
@@ -149,7 +170,6 @@
         def _():
             for a in range(NA):
                 lcopy(W_IN[a], W_BUF[a].at[s], wl.at[a]).wait()
-            lcopy(vec, VEC.at[s], wl.at[4]).wait()
 
         @pl.when(l != s)
         def _():
@@ -256,8 +276,8 @@
                 back_copy(p, di, t).wait_recv()
 
     def stats(hf):
-        cen = hf - jnp.mean(hf, axis=-1, keepdims=True)
-        rstd = lax.rsqrt(jnp.mean(cen * cen, axis=-1, keepdims=True) + LN_EPS)
+        cen = hf - row_mean(hf)
+        rstd = lax.rsqrt(row_mean(cen * cen) + LN_EPS)
         return cen * rstd, rstd
 
     LB = 64
@@ -274,10 +294,16 @@
             return carry
         lax.fori_loop(0, C // LB, step, 0)
 
+    def by_kind():
+        return [(h * 3 + k) * E for k in range(3) for h in range(2)]
+
+    def wq(l):
+        return jnp.concatenate([WQ[l, r:r + E, :] for r in by_kind()], axis=0)
+
     def forward(l, i):
         r0, r1 = i * C, (i + 1) * C
         norms(l, i)
-        qkv = nn(AS[...], WQ[l]) + VEC[l, 7:8, :3 * E2]
+        qkv = nt(AS[...], wq(l)) + VEC[l, 7:8, :3 * E2]
         qkv = qkv.astype(BF16).astype(F32)
         t = tabs(i)
         q = rotate(qkv[:, :E2], t).astype(BF16)
@@ -304,8 +330,8 @@
             def expo(b, tot):
                 e = jnp.exp2(ST[rows(b * RBK, RBK), :] * c1 - mc)
                 ST[rows(b * RBK, RBK), :] = e
-                return tot + jnp.sum(e.reshape(RBK // 8, 8, C), axis=0)
-            tot = jnp.sum(lax.fori_loop(0, r1 // RBK, expo, jnp.zeros((8, C), F32)), axis=0, keepdims=True)
+                return tot + fold(e)
+            tot = col_sum(lax.fori_loop(0, r1 // RBK, expo, jnp.zeros((8, C), F32)))
             inv = 1.0 / tot
 
             def put(b, carry):
@@ -350,16 +376,16 @@
 
         norms(l, i)
         dy = H[dl, r0:r1, :]
-        acc_row(4, jnp.sum(dy.astype(F32), axis=0, keepdims=True))
+        acc_row(4, col_sum(dy.astype(F32)))
         PRE[...] = nt(dy, WD[l])
         GB = 32
 
         def act(b, tot):
             d = PRE[rows(b * GB, GB), :] * GP[l, rows(r0 + b * GB, GB), :]
             DPB[rows(b * GB, GB), :] = d.astype(BF16)
-            return tot + jnp.sum(d.reshape(GB // 8, 8, F), axis=0)
+            return tot + fold(d)
         dbu = lax.fori_loop(0, C // GB, act, jnp.zeros((8, F), F32))
-        acc_row(5, jnp.sum(dbu, axis=0, keepdims=True))
+        acc_row(5, col_sum(dbu))
         acc(GD, tn(HID[l, r0:r1, :], dy))
         yield
         acc(GU, tn(MS[...], DPB[...]))
@@ -379,7 +405,7 @@
             qm = jnp.where(sel, q, 0.0).astype(BF16)
             dcm = jnp.where(sel, dcf, 0.0).astype(BF16)
             dsum = jnp.transpose(jnp.where(sel, prod, 0.0))
-            drow = jnp.sum(dsum, axis=0, keepdims=True)
+            drow = col_sum(dsum)
             ST[:r1, :] = nt(V[l, :r1, :], dcm)
 
             def sub(b, carry):
@@ -403,10 +429,15 @@
         dk = unrotate(DK[r0:r1, :] * scale, t)
         dv = DV[r0:r1, :]
         dqkv = jnp.concatenate([dq, dk, dv], axis=1)
-        acc_row(6, jnp.sum(dqkv, axis=0, keepdims=True), 3 * E2)
+        acc_row(6, col_sum(dqkv), 3 * E2)
         dqkv = dqkv.astype(BF16)
-        acc(GQ, tn(AS[...], dqkv))
-        PRE[...] = nt(dqkv, WQ[l])
+        dwq = tn(dqkv, AS[...])
+        for k, r in enumerate(by_kind()):
+            if first:
+                GQ[par, r:r + E, :] = dwq[k * E:(k + 1) * E]
+            else:
+                GQ[par, r:r + E, :] += dwq[k * E:(k + 1) * E]
+        PRE[...] = nn(dqkv, wq(l))
         yield
         g1, g2 = VEC[l, 0:1, :], VEC[l, 2:3, :]
 
@@ -416,15 +447,15 @@
             da = PRE[rows(b * LB, LB), :]
             dm = PF[rows(f0 + b * LB, LB), :]
             dx = da * g1 + dm * g2
-            m1 = jnp.mean(dx, axis=-1, keepdims=True)
-            m2 = jnp.mean(dx * xhat, axis=-1, keepdims=True)
+            m1 = row_mean(dx)
+            m2 = row_mean(dx * xhat)
             if not last:
                 PF[rows(f0 + b * LB, LB), :] = rstd * (dx - m1 - xhat * m2)
             terms = (da * xhat, da, dm * xhat, dm)
-            return tuple(a + jnp.sum(v.reshape(LB // 8, 8, D), axis=0) for a, v in zip(tots, terms))
+            return tuple(a + fold(v) for a, v in zip(tots, terms))
         tots = lax.fori_loop(0, C // LB, lnb, tuple(jnp.zeros((8, D), F32) for _ in range(NA)))
         for k in range(NA):
-            acc_row(k, jnp.sum(tots[k], axis=0, keepdims=True))
+            acc_row(k, col_sum(tots[k]))
         yield
 
     def g_half(a, k):
@@ -703,13 +734,49 @@
     vout.wait()
 
 
-def group_step(dims, x, g, wqkv, wo, wup, wdn, vec, tab):
+def finish(y, gq, go, gu, gd, gv, *rest):
+    outs, small, bufs, got, put = rest[:5], rest[5:13], rest[13:18], rest[18], rest[19]
+    loads = [pltpu.make_async_copy(a, b, got.at[k]) for k, (a, b) in enumerate(zip((y, gq, go, gu, gd), bufs))]
+    stores = [pltpu.make_async_copy(b, a, put.at[k]) for k, (a, b) in enumerate(zip(outs, bufs))]
+    order = loads[1:] + loads[:1]
+    for cp in order:
+        cp.start()
+    for k, ref in enumerate(small[:7]):
+        row = k if k < 5 else k - 1
+        ref[...] = gv[row:row + 1, :]
+    e = small[7].shape[2]
+    for k in range(3):
+        for h in range(2):
+            small[7][k, h:h + 1, :] = gv[6:7, (2 * k + h) * e:(2 * k + h + 1) * e]
+    for cp, out in zip(order, stores[1:] + stores[:1]):
+        cp.wait()
+        out.start()
+    for cp in stores:
+        cp.wait()
+
+
+def finish_step(y, gq, go, gu, gd, gv, e):
+    hbm, vmem = pl.BlockSpec(memory_space=pl.ANY), pl.BlockSpec(memory_space=pltpu.VMEM)
+    big = [jax.ShapeDtypeStruct(a.shape, a.dtype) for a in (y, gq, go, gu, gd)]
+    row = jax.ShapeDtypeStruct((1, gv.shape[1]), F32)
+    return pl.pallas_call(
+        finish,
+        out_shape=big + [row] * 7 + [jax.ShapeDtypeStruct((3, 2, e), F32)],
+        in_specs=[hbm] * 5 + [vmem],
+        out_specs=[hbm] * 5 + [vmem] * 8,
+        scratch_shapes=[pltpu.VMEM(a.shape, a.dtype) for a in big] + [pltpu.SemaphoreType.DMA((5,))] * 2,
+        name='neox_out',
+    )(y, gq, go, gu, gd, gv)
+
+
+def group_step(dims, *args):
+    x = args[0]
     S, D, E, C, F = dims
     E2 = 2 * E
     hbm = pl.BlockSpec(memory_space=pl.ANY)
     out_shape = [
         jax.ShapeDtypeStruct(x.shape, BF16),
-        jax.ShapeDtypeStruct((D, 3 * E2), F32),
+        jax.ShapeDtypeStruct((3 * E2, D), F32),
         jax.ShapeDtypeStruct((E2, D), F32),
         jax.ShapeDtypeStruct((D, F), F32),
         jax.ShapeDtypeStruct((F, D), F32),
@@ -720,32 +787,33 @@
         return pltpu.VMEM(shape, dtype)
     dma = pltpu.SemaphoreType.DMA
     scratch = [
-        vm(NL, D, 3 * E2), vm(NL, E2, D), vm(NL, D, F), vm(NL, F, D), vm(NL, 8, D, dtype=F32),
+        vm(NL, 3 * E2, D), vm(NL, E2, D), vm(NL, D, F), vm(NL, F, D), vm(NL, 8, D, dtype=F32),
         vm(NL + 2, S, D),
         vm(NL, S, E2), vm(NL, S, E2), vm(NL, S, E2), vm(NL, E2, S), vm(E2, S), vm(NL, S, E2),
         *[vm(NL, 2, (i + 1) * C, C) for i in range(NC)],
         vm(NL, S, F), vm(NL + 1, S, F, dtype=F32),
         vm(2, S, D), vm(2, S, D), vm(S, D), vm(S + C, D, dtype=F32),
-        vm(2, D, 3 * E2, dtype=F32), vm(2, E2, D, dtype=F32), vm(2, D, F, dtype=F32), vm(2, F, D, dtype=F32),
-        vm(2, D // 2, 3 * E2), vm(2, E, D), vm(2, D // 2, F), vm(2, F // 2, D),
+        vm(2, 3 * E2, D, dtype=F32), vm(2, E2, D, dtype=F32), vm(2, D, F, dtype=F32), vm(2, F, D, dtype=F32),
+        vm(2, 3 * E, D), vm(2, E, D), vm(2, D // 2, F), vm(2, F // 2, D),
         vm(S, E2, dtype=F32), vm(S, E2, dtype=F32),
         vm(2, C + 8, E2, dtype=F32), vm(S, E2, dtype=F32), vm(S, E2, dtype=F32),
         vm(NL, 8, D, dtype=F32), vm(NL, NT, 8, D, dtype=F32), vm(NL, 8, D, dtype=F32), vm(NL, 8, D, dtype=F32),
         vm(C, D), vm(C, D), vm(C, max(D, F), dtype=F32), vm(C, F), vm(S, C), vm(S, C, dtype=F32),
-        dma((5,)), dma((19,)), dma((NL, 9)), dma((2, 4)), dma((2,)), dma((1,)),
+        *[vm(1, D, dtype=F32)] * 4, vm(1, D), vm(1, D), vm(1, F), vm(3, 2, E),
+        dma((5,)), dma((19,)), dma((NL, 9)), dma((2, NA)), dma((2,)), dma((1,)),
         dma((NC * SUB,)), dma((NC * SUB,)), dma((2, NC * SUB)), dma((2, NC * SUB)), dma((2, NC * SUB)),
-        dma((NL,)), dma((NL,)), dma((4,)), dma((2, 4)), dma((2, 4)), dma((2, 4)), dma((2, 4)), dma((4,)),
-        dma((NL, NT - 1)), dma((NL, NT)), dma((NL,)), dma((NL,)), dma((1,)),
+        dma((NL,)), dma((NL,)), dma((NA,)), dma((2, NA)), dma((2, NA)), dma((2, NA)), dma((2, NA)), dma((NA,)),
+        dma((NL, NT - 1)), dma((NL, NT)), dma((NL,)), dma((NL,)), dma((1,)), dma((8,)),
     ]
     return pl.pallas_call(
         functools.partial(body, dims),
         out_shape=out_shape,
-        in_specs=[hbm] * 8,
+        in_specs=[hbm] * len(args),
         out_specs=[hbm] * 6,
         scratch_shapes=scratch,
         compiler_params=pltpu.CompilerParams(collective_id=0, has_side_effects=True, vmem_limit_bytes=67043328),
         name='neox_group',
-    )(x, g, wqkv, wo, wup, wdn, vec, tab)
+    )(*args)
 
 
 def solution(mesh):
@@ -754,16 +822,13 @@
         heads, E = w_qkv.shape[2], w_qkv.shape[4]
         F = w_up.shape[2]
         C = S // NC
-        qcols = heads * 3 * E
-        wqkv = jnp.transpose(w_qkv[0], (0, 2, 1, 3)).reshape(D, qcols)
-        bqkv = jnp.transpose(b_qkv[0], (1, 0, 2)).reshape(1, qcols).astype(F32)
-        bqkv = jnp.pad(bqkv, ((0, 0), (0, D - qcols)))
-        vec = jnp.concatenate([ln1_gain, ln1_bias, ln2_gain, ln2_bias, b_out.astype(F32), b_down.astype(F32), b_up.astype(F32), bqkv], axis=0)
+        wqkv = jnp.transpose(w_qkv[0], (1, 2, 3, 0)).reshape(heads * 3 * E, D)
+        bqkv = jnp.transpose(b_qkv[0], (1, 0, 2))
         tab = jnp.asarray(rotary_base(C, NC, E, heads))
-        y, gqkv, go, gup, gdn, gvec = group_step((S, D, E, C, F), x_in, g_out, wqkv, w_out[0].reshape(heads * E, D), w_up[0], w_down[0], vec, tab)
-        gq = jnp.transpose(gqkv.reshape(D, 3, heads, E), (0, 2, 1, 3))[None]
-        gbq = jnp.transpose(gvec[6, :qcols].reshape(3, heads, E), (1, 0, 2))[None]
-        bias_out = gvec[4:5]
-        return (y, gvec[0:1], gvec[1:2], gq, gbq, go.reshape(1, heads, E, D), bias_out, gvec[2:3], gvec[3:4], gup[None], gvec[5:6], gdn[None], bias_out)
+        part = group_step((S, D, E, C, F), x_in, g_out, wqkv, w_out[0].reshape(heads * E, D), w_up[0], w_down[0], ln1_gain, ln1_bias, ln2_gain, ln2_bias, b_out, b_down, b_up, bqkv, tab)
+        y, gq, go, gup, gdn, n1g, n1b, n2g, n2b, gbo, gbd, gbu, gbq = finish_step(*part, E)
+        gq = jnp.transpose(gq.reshape(heads, 3, E, D), (3, 0, 1, 2))[None]
+        gbq = jnp.transpose(gbq, (1, 0, 2))[None]
+        return (y, n1g, n1b, gq, gbq, go.reshape(1, heads, E, D), gbo, n2g, n2b, gup[None], gbu, gdn[None], gbd)
 
     return jax.shard_map(device_fn, mesh=mesh, in_specs=(P('dp'), P('dp')) + STAGE_SPECS, out_specs=(P('dp'),) + GRAD_SPECS, check_vma=False)

time: 261 us -> 251 us (0.962)
  local copies, waits for them, and re-layouts: 17.2 us -> 0 us
  Pallas kernels: 241 us -> 248 us
    unnamed x15 -> x0, local copies, waits for them, and re-layouts: 9.81 us -> none
    pallas_call x0 -> x1, Pallas kernels: none -> 7.74 us  [finish_step(): pl.pallas_call(finish, out_shape=big + [row] * 7 + [jax.ShapeDtypeStruct(...]
where the time goes in v3:
time: 251 us; the launch traced here: 249 us
  Pallas kernels  248 us (99%)
    pallas_call x1, Pallas kernels, group_step(): pl.pallas_call(functools.partial(body, dims), out_shape=out_shape, in_spe...  241 us
    pallas_call x1, Pallas kernels, finish_step(): pl.pallas_call(finish, out_shape=big + [row] * 7 + [jax.ShapeDtypeStruct(...  7.74 us

profile of v3, /device:TPU:0, one launch (start us, length us, event | category | flops | bytes accessed | tf_op | source)
XLA Modules:
  0.0 249.3 jit_solution(3057030009527301521)
XLA Ops:
  0.7 240.7 %neox_group.1 = (bf16[2,2,1024,512]{3,2,1,0:T(8,128)(2,1)}, f32[384,512]{1,0:T(8,128)}, f32[128,512]{1,0:T(8,128)}, f32[512,512]{1,0:T(8,128)}, f32[512,512]{1,0:T(8,128)}, /*index=5*/f32[8,512]{1,0:T(8,128)}) custom-call(bf16[2,2,1024,512]{3,2,1,0:T(8,128)(2,1)} %x.1, f32[2,2,1024,512]{3,2,1,0:T(8,128)} %g.1, bf16[384,512]{1,0:T(8,128)(2,1)} %bitcast.24, ...), custom_call_target="tpu_custom_call" | custom-call | tf_op jit(solution)/shard_map/neox_group/pallas_call | solution.py:808
  241.4 7.7 %neox_out.1 = (bf16[2,2,1024,512]{3,2,1,0:T(8,128)(2,1)}, f32[384,512]{1,0:T(8,128)}, f32[128,512]{1,0:T(8,128)}, f32[512,512]{1,0:T(8,128)}, f32[512,512]{1,0:T...) custom-call(bf16[2,2,1024,512]{3,2,1,0:T(8,128)(2,1)} %get-tuple-ele, ...), custom_call_target="tpu_custom_call" | custom-call | tf_op jit(solution)/shard_map/neox_out/pallas_call | solution.py:762

commit v4 on v3

--- a/solution.py
+++ b/solution.py
@@ -70,11 +70,12 @@
          WQ, WO, WU, WD, VEC, H, Q, K, V, KT, VT, CTX, P0, P1, P2, P3, HID, GP, RA, RB, PS, PF,
          GQ, GO, GU, GD, R2Q, R2O, R2U, R2D, DK, DV, TAB, COS, SIN, GV, ZR, GZ, PR,
          AS, MS, PRE, DPB, DS, ST, N0, N1, N2, N3, N4, N5, N6, BQ,
-         wl, ws, wr, wf, xs, gs, sab, sc, ra_s, rb_s, rc_s, ys, yr, g1s, g1r, g2s, g2r, g3s, g3r, v1s, v1r, v2s, v2r, osem, ns):
+         wl, ws, wy, wr, wf, xs, gs, sab, sc, ra_s, rb_s, rc_s, ys, yr, g1s, g1r, g2s, g2r, g3s, g3r, v1s, v1r, v2s, v2r, osem, ns):
     S, D, E, C, F = dims
     E2 = 2 * E
     SR = C // SUB
     z = lax.axis_index('tp')
+    xg = lax.axis_index('dp')
     s = lax.axis_index('pp')
     ys_ = s // 2
     c = s % 2
@@ -88,10 +89,12 @@
     PX = (P0, P1, P2, P3)
     W_IN = (wqkv, wo, wup, wdn)
     W_BUF = (WQ, WO, WU, WD)
-    W_HALF = (3 * E, E, D // 2, F // 2)
+    G_HALF = (3 * E, E, D // 2, F // 2)
+    W_PART = tuple(n // 2 for n in G_HALF)
+    ALL, FIRST, REST = tuple(range(NA)), (0,), (1, 2, 3)
+    ATT, MLP = ALL[:2], ALL[2:]
     G_BUF = (GQ, GO, GU, GD)
     G_OUT = (oqkv, oo, oup, odn)
-    G_HALF = W_HALF
     G_COLS = (D, D, F, D)
     R1_OFF = (0, 3 * E, 4 * E, 4 * E + D // 2)
     R2 = (R2Q, R2O, R2U, R2D)
@@ -122,26 +125,23 @@
         pl.semaphore_signal(bar, inc=1, device_id={'tp': (z + o) % NT}, device_id_type=pl.DeviceIdType.MESH)
     for o in range(1, NL):
         pl.semaphore_signal(bar, inc=1, device_id={'pp': (s + o) % NL}, device_id_type=pl.DeviceIdType.MESH)
-    pl.semaphore_wait(bar, NT - 1 + NL - 1)
-
-    def w_half(a, k):
-        return rows(k * W_HALF[a], W_HALF[a])
+    pl.semaphore_signal(bar, inc=1, device_id={'dp': 1 - xg}, device_id_type=pl.DeviceIdType.MESH)
+    pl.semaphore_wait(bar, NT + NL - 1)
+
+    def w_part(l, a, q):
+        return W_BUF[a].at[l, rows(q * W_PART[a], W_PART[a])]
 
     def sib_copies():
-        out = []
-        for a in range(NA):
-            for k in range(2):
-                out.append(rcopy(W_IN[a].at[w_half(a, k)], W_BUF[a].at[s, w_half(a, k)], ws.at[2 * a + k], wr.at[s, 2 * a + k], pp=sib))
-        out.append(rcopy(VEC.at[s], VEC.at[s], ws.at[16], wr.at[s, 8], pp=sib))
-        return out
+        out = [rcopy(W_IN[a], W_BUF[a].at[s], ws.at[a], wr.at[s, NA * a], pp=sib) for a in ALL]
+        return out + [rcopy(VEC.at[s], VEC.at[s], ws.at[NA], wr.at[s, NA * NA], pp=sib)]
 
     def y_copies():
         out = []
-        for a in range(NA):
+        for a in ALL:
             for k in range(2):
-                out.append(rcopy(W_IN[a].at[w_half(a, k)], W_BUF[a].at[s, w_half(a, k)], ws.at[8 + 2 * a + k], wr.at[s, 2 * a + k], pp=oy + k))
-        out += [rcopy(VEC.at[s], VEC.at[s], ws.at[17 + k], wr.at[s, 8], pp=oy + k) for k in range(2)]
-        return out
+                q = 2 * xg + k
+                out.append(rcopy(W_IN[a].at[rows(q * W_PART[a], W_PART[a])], w_part(s, a, q), wy.at[k, a], wr.at[s, NA * a + q], pp=oy + k))
+        return out + [rcopy(VEC.at[s], VEC.at[s], wy.at[k, NA], wr.at[s, NA * NA], pp=oy + k) for k in range(2)]
 
     def start_all(copies):
         for cp in copies:
@@ -158,35 +158,44 @@
         start_all(y_copies())
     start_all(sib_copies())
 
-    def arrived(l, a, k):
-        rcopy(W_BUF[a].at[l, w_half(a, k)], W_BUF[a].at[l, w_half(a, k)], ws.at[2 * a], wr.at[l, 2 * a + k], pp=sib).wait_recv()
-
-    def fwd_copy(l, a):
-        part = W_BUF[a].at[l, w_half(a, c)]
-        return rcopy(part, part, wf.at[l % 2, a], wr.at[l, 2 * a + c], pp=sib)
-
-    def fetch(l):
+    def arrived(l, a, q):
+        rcopy(w_part(l, a, q), w_part(l, a, q), ws.at[a], wr.at[l, NA * a + q], pp=sib).wait_recv()
+
+    def mine(hop):
+        return 2 * (xg if hop == 0 else 1 - xg) + c
+
+    def pass_copies(l, a, hop):
+        part, sem = w_part(l, a, mine(hop)), wr.at[l, NA * a + mine(hop)]
+        out = [rcopy(part, part, wf.at[l % 2, hop, a], sem, pp=sib)]
+        return out if hop else out + [rcopy(part, part, wf.at[l % 2, 2, a], sem, dp=1 - xg)]
+
+    def relay(l, arrays, hop):
+        @pl.when(l // 2 != ys_)
+        def _():
+            for a in arrays:
+                arrived(l, a, mine(hop))
+                start_all(pass_copies(l, a, hop))
+
+    def settle(l, arrays, small):
         @pl.when(l == s)
         def _():
-            for a in range(NA):
+            for a in arrays:
                 lcopy(W_IN[a], W_BUF[a].at[s], wl.at[a]).wait()
 
-        @pl.when(l != s)
-        def _():
-            @pl.when(l // 2 == ys_)
-            def _():
-                for a in range(NA):
-                    for k in range(2):
-                        arrived(l, a, k)
-
-            @pl.when(l // 2 != ys_)
-            def _():
-                for a in range(NA):
-                    arrived(l, a, c)
-                    fwd_copy(l, a).start()
-                for a in range(NA):
-                    arrived(l, a, 1 - c)
-            rcopy(VEC.at[l], VEC.at[l], ws.at[16], wr.at[l, 8], pp=sib).wait_recv()
+        @pl.when(l == sib)
+        def _():
+            for a in arrays:
+                rcopy(W_IN[a], W_BUF[a].at[l], ws.at[a], wr.at[l, NA * a], pp=sib).wait_recv()
+
+        @pl.when(l // 2 != ys_)
+        def _():
+            for a in arrays:
+                for k in range(2):
+                    arrived(l, a, 2 * k + 1 - c)
+        if small:
+            @pl.when(l != s)
+            def _():
+                rcopy(VEC.at[l], VEC.at[l], ws.at[NA], wr.at[l, NA * NA], pp=sib).wait_recv()
 
     tcopy.wait()
     for i in range(NC):
@@ -344,6 +353,12 @@
         ctx = jnp.transpose(jnp.where(sub_head == 0, outs[0], outs[1])).astype(BF16)
         CTX[l, r0:r1, :] = ctx
         yield
+        if i == 0:
+            @pl.when(l == 0)
+            def _():
+                for hop in range(2):
+                    relay(l, REST, hop)
+            settle(l, REST, False)
         PF[r0:r1, :] = nn(ctx, WO[l])
         PRE[...] = nn(MS[...], WU[l])
         bup = VEC[l, 6:7, :]
@@ -479,14 +494,8 @@
     def v1_copies(l):
         return [rcopy(GV.at[l], ZR.at[l, z], v1s.at[l, o - 1], v1r.at[l, z], tp=(z + o) % NT) for o in range(1, NT)]
 
-    def grads_out(l):
-        for a in range(NA):
-            g1_copy(l, a).start()
-        for cp in v1_copies(l):
-            cp.start()
-
-    def grads_mid(l):
-        for a in range(NA):
+    def grads_mid(l, arrays):
+        for a in arrays:
             g1_copy(l, a).wait_recv()
             n = G_HALF[a]
 
@@ -505,7 +514,7 @@
     def grads_last(l):
         @pl.when(l // 2 == ys_)
         def _():
-            for a in range(NA):
+            for a in MLP + ATT:
                 g2_copy(l, a).wait_recv()
 
                 def add(b, carry):
@@ -557,11 +566,14 @@
             v2_copy(l).start()
 
     GV[...] = jnp.zeros_like(GV)
-    fetch(0)
+    for hop in range(2):
+        relay(0, FIRST, hop)
+    settle(0, FIRST, True)
     xcopy.wait()
 
-    def run(phases, at, handle):
+    def run(phases, at, handle, after=lambda k: None):
         for k, unused in enumerate(phases):
+            after(k)
             for op, lag, u in at.get(k, ()):
                 handle(op, lag, u)
 
@@ -592,14 +604,17 @@
                 def _():
                     gcopy.wait()
                     H[NL + 1] = GP[NL].astype(BF16)
-            if i == 2:
-                @pl.when((l == 0) & (s == 1))
+
+                    @pl.when(s == 1)
+                    def _():
+                        start_all(y_copies())
+            if i > 0:
+                @pl.when(l < NL - 1)
                 def _():
-                    start_all(y_copies())
-
-        @pl.when(l < NL - 1)
-        def _():
-            fetch(l + 1)
+                    if i < NC - 1:
+                        relay(l + 1, ALL, i - 1)
+                    else:
+                        settle(l + 1, FIRST, True)
         return carry
     lax.fori_loop(0, NL, fwd_layer, 0)
 
@@ -647,16 +662,23 @@
                             ar_mid(NL - 1, m + NC, u)
                         else:
                             ar_last(NL - 1, NL - 1, NL, m + NC, u)
-            run(backward(l, ri(l), i, False), BWD_AT, handle)
+
+            def after(k):
+                if k == 0 and n == 0:
+                    @pl.when(lb > 0)
+                    def _():
+                        grads_mid(l + 1, ATT)
+                        for a in ALL:
+                            g1_copy(l + 1, a).wait_send()
+                if k == 1 and n == NC - 1:
+                    for a in MLP:
+                        g1_copy(l, a).start()
+            run(backward(l, ri(l), i, False), BWD_AT, handle, after)
 
             @pl.when(l > 0)
             def _():
                 ar_send(p, i, True)
             if n == 0:
-                @pl.when(lb > 0)
-                def _():
-                    grads_mid(l + 1)
-
                 @pl.when(lb == 2)
                 def _():
                     y_arrived(oy + c)
@@ -676,15 +698,14 @@
                 def _():
                     grads_last(l + 2)
 
-        @pl.when(lb > 0)
-        def _():
-            for a in range(NA):
-                g1_copy(l + 1, a).wait_send()
-        grads_out(l)
+        for a in ATT:
+            g1_copy(l, a).start()
+        start_all(v1_copies(l))
+        grads_mid(l, MLP)
         return carry
     lax.fori_loop(0, NL, bwd_layer, 0)
 
-    grads_mid(0)
+    grads_mid(0, ATT)
     grads_last(1)
     vec_mid(0)
     grads_last(0)
@@ -718,8 +739,10 @@
     for cp in y_copies():
         cp.wait_send()
     for k in range(2):
-        for a in range(NA):
-            fwd_copy(oy + k, a).wait_send()
+        for a in ALL:
+            for hop in range(2):
+                for cp in pass_copies(oy + k, a, hop):
+                    cp.wait_send()
 
     @pl.when(is_end)
     def _():
@@ -734,21 +757,21 @@
     vout.wait()
 
 
-def finish(y, gq, go, gu, gd, gv, *rest):
-    outs, small, bufs, got, put = rest[:5], rest[5:13], rest[13:18], rest[18], rest[19]
-    loads = [pltpu.make_async_copy(a, b, got.at[k]) for k, (a, b) in enumerate(zip((y, gq, go, gu, gd), bufs))]
-    stores = [pltpu.make_async_copy(b, a, put.at[k]) for k, (a, b) in enumerate(zip(outs, bufs))]
-    order = loads[1:] + loads[:1]
-    for cp in order:
+def finish(y, gq, go, gu, gd, gv, yo, qo, oo, uo, do, n0, n1, n2, n3, n4, n5, n6, bq, yb, qb, ob, ub, db, got, put):
+    trips = [(gd, db, do), (gu, ub, uo), (go, ob, oo), (gq, qb, qo)]
+    trips += [tuple(ref.at[m, r] for ref in (y, yb, yo)) for m in range(y.shape[0]) for r in range(y.shape[1])]
+    loads = [pltpu.make_async_copy(a, b, got.at[k]) for k, (a, b, o) in enumerate(trips)]
+    stores = [pltpu.make_async_copy(b, o, put.at[k]) for k, (a, b, o) in enumerate(trips)]
+    for cp in loads:
         cp.start()
-    for k, ref in enumerate(small[:7]):
-        row = k if k < 5 else k - 1
-        ref[...] = gv[row:row + 1, :]
-    e = small[7].shape[2]
+    for row, refs in enumerate(((n0,), (n1,), (n2,), (n3,), (n4, n5), (n6,))):
+        for ref in refs:
+            ref[...] = gv[row:row + 1, :]
+    e = bq.shape[2]
     for k in range(3):
         for h in range(2):
-            small[7][k, h:h + 1, :] = gv[6:7, (2 * k + h) * e:(2 * k + h + 1) * e]
-    for cp, out in zip(order, stores[1:] + stores[:1]):
+            bq[k, h:h + 1, :] = gv[6:7, (2 * k + h) * e:(2 * k + h + 1) * e]
+    for cp, out in zip(loads, stores):
         cp.wait()
         out.start()
     for cp in stores:
@@ -764,7 +787,7 @@
         out_shape=big + [row] * 7 + [jax.ShapeDtypeStruct((3, 2, e), F32)],
         in_specs=[hbm] * 5 + [vmem],
         out_specs=[hbm] * 5 + [vmem] * 8,
-        scratch_shapes=[pltpu.VMEM(a.shape, a.dtype) for a in big] + [pltpu.SemaphoreType.DMA((5,))] * 2,
+        scratch_shapes=[pltpu.VMEM(a.shape, a.dtype) for a in big] + [pltpu.SemaphoreType.DMA((8,))] * 2,
         name='neox_out',
     )(y, gq, go, gu, gd, gv)
 
@@ -800,7 +823,7 @@
         vm(NL, 8, D, dtype=F32), vm(NL, NT, 8, D, dtype=F32), vm(NL, 8, D, dtype=F32), vm(NL, 8, D, dtype=F32),
         vm(C, D), vm(C, D), vm(C, max(D, F), dtype=F32), vm(C, F), vm(S, C), vm(S, C, dtype=F32),
         *[vm(1, D, dtype=F32)] * 4, vm(1, D), vm(1, D), vm(1, F), vm(3, 2, E),
-        dma((5,)), dma((19,)), dma((NL, 9)), dma((2, NA)), dma((2,)), dma((1,)),
+        dma((NA,)), dma((NA + 1,)), dma((2, NA + 1)), dma((NL, NA * NA + 1)), dma((2, 3, NA)), dma((2,)), dma((1,)),
         dma((NC * SUB,)), dma((NC * SUB,)), dma((2, NC * SUB)), dma((2, NC * SUB)), dma((2, NC * SUB)),
         dma((NL,)), dma((NL,)), dma((NA,)), dma((2, NA)), dma((2, NA)), dma((2, NA)), dma((2, NA)), dma((NA,)),
         dma((NL, NT - 1)), dma((NL, NT)), dma((NL,)), dma((NL,)), dma((1,)), dma((8,)),

time: 251 us -> 250 us (level)
  no operation moved by 1% of the time
where the time goes in v4:
time: 250 us; the launch traced here: 248 us
  Pallas kernels  248 us (99%)
    pallas_call x1, Pallas kernels, group_step(): pl.pallas_call(functools.partial(body, dims), out_shape=out_shape, in_spe...  240 us
    pallas_call x1, Pallas kernels, finish_step(): pl.pallas_call(finish, out_shape=big + [row] * 7 + [jax.ShapeDtypeStruct(...  7.41 us

profile of v4, /device:TPU:0, one launch (start us, length us, event | category | flops | bytes accessed | tf_op | source)
XLA Modules:
  0.0 248.3 jit_solution(2129299190361863620)
XLA Ops:
  0.7 240.1 %neox_group.1 = (bf16[2,2,1024,512]{3,2,1,0:T(8,128)(2,1)}, f32[384,512]{1,0:T(8,128)}, f32[128,512]{1,0:T(8,128)}, f32[512,512]{1,0:T(8,128)}, f32[512,512]{1,0:T(8,128)}, /*index=5*/f32[8,512]{1,0:T(8,128)}) custom-call(bf16[2,2,1024,512]{3,2,1,0:T(8,128)(2,1)} %x.1, f32[2,2,1024,512]{3,2,1,0:T(8,128)} %g.1, bf16[384,512]{1,0:T(8,128)(2,1)} %bitcast.24, ...), custom_call_target="tpu_custom_call" | custom-call | tf_op jit(solution)/shard_map/neox_group/pallas_call | solution.py:831
  240.8 7.4 %neox_out.1 = (bf16[2,2,1024,512]{3,2,1,0:T(8,128)(2,1)}, f32[384,512]{1,0:T(8,128)}, f32[128,512]{1,0:T(8,128)}, f32[512,512]{1,0:T(8,128)}, f32[512,512]{1,0:T...) custom-call(bf16[2,2,1024,512]{3,2,1,0:T(8,128)(2,1)} %get-tuple-ele, ...), custom_call_target="tpu_custom_call" | custom-call | tf_op jit(solution)/shard_map/neox_out/pallas_call | solution.py:785

commit v5 on v4

--- a/solution.py
+++ b/solution.py
@@ -75,7 +75,6 @@
     E2 = 2 * E
     SR = C // SUB
     z = lax.axis_index('tp')
-    xg = lax.axis_index('dp')
     s = lax.axis_index('pp')
     ys_ = s // 2
     c = s % 2
@@ -90,7 +89,6 @@
     W_IN = (wqkv, wo, wup, wdn)
     W_BUF = (WQ, WO, WU, WD)
     G_HALF = (3 * E, E, D // 2, F // 2)
-    W_PART = tuple(n // 2 for n in G_HALF)
     ALL, FIRST, REST = tuple(range(NA)), (0,), (1, 2, 3)
     ATT, MLP = ALL[:2], ALL[2:]
     G_BUF = (GQ, GO, GU, GD)
@@ -125,23 +123,18 @@
         pl.semaphore_signal(bar, inc=1, device_id={'tp': (z + o) % NT}, device_id_type=pl.DeviceIdType.MESH)
     for o in range(1, NL):
         pl.semaphore_signal(bar, inc=1, device_id={'pp': (s + o) % NL}, device_id_type=pl.DeviceIdType.MESH)
-    pl.semaphore_signal(bar, inc=1, device_id={'dp': 1 - xg}, device_id_type=pl.DeviceIdType.MESH)
-    pl.semaphore_wait(bar, NT + NL - 1)
-
-    def w_part(l, a, q):
-        return W_BUF[a].at[l, rows(q * W_PART[a], W_PART[a])]
+    pl.semaphore_wait(bar, NT + NL - 2)
+
+    def half(ref, a, k):
+        return ref.at[rows(k * G_HALF[a], G_HALF[a])]
 
     def sib_copies():
-        out = [rcopy(W_IN[a], W_BUF[a].at[s], ws.at[a], wr.at[s, NA * a], pp=sib) for a in ALL]
-        return out + [rcopy(VEC.at[s], VEC.at[s], ws.at[NA], wr.at[s, NA * NA], pp=sib)]
+        out = [rcopy(W_IN[a], W_BUF[a].at[s], ws.at[a], wr.at[s, 2 * a], pp=sib) for a in ALL]
+        return out + [rcopy(VEC.at[s], VEC.at[s], ws.at[NA], wr.at[s, 2 * NA], pp=sib)]
 
     def y_copies():
-        out = []
-        for a in ALL:
-            for k in range(2):
-                q = 2 * xg + k
-                out.append(rcopy(W_IN[a].at[rows(q * W_PART[a], W_PART[a])], w_part(s, a, q), wy.at[k, a], wr.at[s, NA * a + q], pp=oy + k))
-        return out + [rcopy(VEC.at[s], VEC.at[s], wy.at[k, NA], wr.at[s, NA * NA], pp=oy + k) for k in range(2)]
+        out = [rcopy(half(W_IN[a], a, k), half(W_BUF[a].at[s], a, k), wy.at[k, a], wr.at[s, 2 * a + k], pp=oy + k) for a in ALL for k in range(2)]
+        return out[:2] + [rcopy(VEC.at[s], VEC.at[s], wy.at[k, NA], wr.at[s, 2 * NA], pp=oy + k) for k in range(2)] + out[2:]
 
     def start_all(copies):
         for cp in copies:
@@ -158,23 +151,16 @@
         start_all(y_copies())
     start_all(sib_copies())
 
-    def arrived(l, a, q):
-        rcopy(w_part(l, a, q), w_part(l, a, q), ws.at[a], wr.at[l, NA * a + q], pp=sib).wait_recv()
-
-    def mine(hop):
-        return 2 * (xg if hop == 0 else 1 - xg) + c
-
-    def pass_copies(l, a, hop):
-        part, sem = w_part(l, a, mine(hop)), wr.at[l, NA * a + mine(hop)]
-        out = [rcopy(part, part, wf.at[l % 2, hop, a], sem, pp=sib)]
-        return out if hop else out + [rcopy(part, part, wf.at[l % 2, 2, a], sem, dp=1 - xg)]
-
-    def relay(l, arrays, hop):
+    def pass_copy(l, a, k):
+        part = half(W_BUF[a].at[l], a, k)
+        return rcopy(part, part, wf.at[l % 2, a], wr.at[l, 2 * a + k], pp=sib)
+
+    def relay(l, arrays):
         @pl.when(l // 2 != ys_)
         def _():
             for a in arrays:
-                arrived(l, a, mine(hop))
-                start_all(pass_copies(l, a, hop))
+                pass_copy(l, a, c).wait_recv()
+                pass_copy(l, a, c).start()
 
     def settle(l, arrays, small):
         @pl.when(l == s)
@@ -185,17 +171,16 @@
         @pl.when(l == sib)
         def _():
             for a in arrays:
-                rcopy(W_IN[a], W_BUF[a].at[l], ws.at[a], wr.at[l, NA * a], pp=sib).wait_recv()
+                rcopy(W_IN[a], W_BUF[a].at[l], ws.at[a], wr.at[l, 2 * a], pp=sib).wait_recv()
 
         @pl.when(l // 2 != ys_)
         def _():
             for a in arrays:
-                for k in range(2):
-                    arrived(l, a, 2 * k + 1 - c)
+                pass_copy(l, a, 1 - c).wait_recv()
         if small:
             @pl.when(l != s)
             def _():
-                rcopy(VEC.at[l], VEC.at[l], ws.at[NA], wr.at[l, NA * NA], pp=sib).wait_recv()
+                rcopy(VEC.at[l], VEC.at[l], ws.at[NA], wr.at[l, 2 * NA], pp=sib).wait_recv()
 
     tcopy.wait()
     for i in range(NC):
@@ -289,7 +274,7 @@
         rstd = lax.rsqrt(row_mean(cen * cen) + LN_EPS)
         return cen * rstd, rstd
 
-    LB = 64
+    LB = 32
     GR = 32
 
     def norms(l, i):
@@ -301,7 +286,7 @@
             AS[rows(b * LB, LB), :] = (xhat * g1 + b1).astype(BF16)
             MS[rows(b * LB, LB), :] = (xhat * g2 + b2).astype(BF16)
             return carry
-        lax.fori_loop(0, C // LB, step, 0)
+        lax.fori_loop(0, C // LB, step, 0, unroll=True)
 
     def by_kind():
         return [(h * 3 + k) * E for k in range(3) for h in range(2)]
@@ -333,20 +318,20 @@
 
             def top(b, m):
                 return jnp.maximum(m, jnp.max(ST[rows(b * RBK, RBK), :].reshape(RBK // 8, 8, C), axis=0))
-            m = jnp.max(lax.fori_loop(0, r1 // RBK, top, jnp.full((8, C), -3e38, F32)), axis=0, keepdims=True)
+            m = jnp.max(lax.fori_loop(0, r1 // RBK, top, jnp.full((8, C), -3e38, F32), unroll=True), axis=0, keepdims=True)
             mc = m * c1
 
             def expo(b, tot):
                 e = jnp.exp2(ST[rows(b * RBK, RBK), :] * c1 - mc)
                 ST[rows(b * RBK, RBK), :] = e
                 return tot + fold(e)
-            tot = col_sum(lax.fori_loop(0, r1 // RBK, expo, jnp.zeros((8, C), F32)))
+            tot = col_sum(lax.fori_loop(0, r1 // RBK, expo, jnp.zeros((8, C), F32), unroll=True))
             inv = 1.0 / tot
 
             def put(b, carry):
                 PX[i][l, h, rows(b * RBK, RBK), :] = (ST[rows(b * RBK, RBK), :] * inv).astype(BF16)
                 return carry
-            lax.fori_loop(0, r1 // RBK, put, 0)
+            lax.fori_loop(0, r1 // RBK, put, 0, unroll=True)
             outs.append(nn(VT[:, :r1], PX[i][l, h]))
             if h == 0:
                 yield
@@ -356,8 +341,7 @@
         if i == 0:
             @pl.when(l == 0)
             def _():
-                for hop in range(2):
-                    relay(l, REST, hop)
+                relay(l, REST)
             settle(l, REST, False)
         PF[r0:r1, :] = nn(ctx, WO[l])
         PRE[...] = nn(MS[...], WU[l])
@@ -371,7 +355,7 @@
             HID[l, rows(r0 + b * GB, GB), :] = (u * cdf).astype(BF16)
             GP[l, rows(r0 + b * GB, GB), :] = cdf + u * pdf
             return carry
-        lax.fori_loop(0, C // GB, act, 0)
+        lax.fori_loop(0, C // GB, act, 0, unroll=True)
         PF[r0:r1, :] += nn(HID[l, r0:r1, :], WD[l])
         yield
 
@@ -399,7 +383,7 @@
             d = PRE[rows(b * GB, GB), :] * GP[l, rows(r0 + b * GB, GB), :]
             DPB[rows(b * GB, GB), :] = d.astype(BF16)
             return tot + fold(d)
-        dbu = lax.fori_loop(0, C // GB, act, jnp.zeros((8, F), F32))
+        dbu = lax.fori_loop(0, C // GB, act, jnp.zeros((8, F), F32), unroll=True)
         acc_row(5, col_sum(dbu))
         acc(GD, tn(HID[l, r0:r1, :], dy))
         yield
@@ -427,7 +411,7 @@
                 pr = PX[i][l, h, rows(b * RBK, RBK), :].astype(F32)
                 DS[rows(b * RBK, RBK), :] = (pr * (ST[rows(b * RBK, RBK), :] - drow)).astype(BF16)
                 return carry
-            lax.fori_loop(0, r1 // RBK, sub, 0)
+            lax.fori_loop(0, r1 // RBK, sub, 0, unroll=True)
             dk = nn(DS[:r1, :], qm)
             dv = nn(PX[i][l, h], dcm)
             if first and h == 0:
@@ -468,7 +452,7 @@
                 PF[rows(f0 + b * LB, LB), :] = rstd * (dx - m1 - xhat * m2)
             terms = (da * xhat, da, dm * xhat, dm)
             return tuple(a + fold(v) for a, v in zip(tots, terms))
-        tots = lax.fori_loop(0, C // LB, lnb, tuple(jnp.zeros((8, D), F32) for _ in range(NA)))
+        tots = lax.fori_loop(0, C // LB, lnb, tuple(jnp.zeros((8, D), F32) for _ in range(NA)), unroll=True)
         for k in range(NA):
             acc_row(k, col_sum(tots[k]))
         yield
@@ -566,8 +550,7 @@
             v2_copy(l).start()
 
     GV[...] = jnp.zeros_like(GV)
-    for hop in range(2):
-        relay(0, FIRST, hop)
+    relay(0, FIRST)
     settle(0, FIRST, True)
     xcopy.wait()
 
@@ -608,11 +591,11 @@
                     @pl.when(s == 1)
                     def _():
                         start_all(y_copies())
-            if i > 0:
+            if i > 1:
                 @pl.when(l < NL - 1)
                 def _():
                     if i < NC - 1:
-                        relay(l + 1, ALL, i - 1)
+                        relay(l + 1, ALL)
                     else:
                         settle(l + 1, FIRST, True)
         return carry
@@ -740,9 +723,7 @@
         cp.wait_send()
     for k in range(2):
         for a in ALL:
-            for hop in range(2):
-                for cp in pass_copies(oy + k, a, hop):
-                    cp.wait_send()
+            pass_copy(oy + k, a, c).wait_send()
 
     @pl.when(is_end)
     def _():
@@ -823,7 +804,7 @@
         vm(NL, 8, D, dtype=F32), vm(NL, NT, 8, D, dtype=F32), vm(NL, 8, D, dtype=F32), vm(NL, 8, D, dtype=F32),
         vm(C, D), vm(C, D), vm(C, max(D, F), dtype=F32), vm(C, F), vm(S, C), vm(S, C, dtype=F32),
         *[vm(1, D, dtype=F32)] * 4, vm(1, D), vm(1, D), vm(1, F), vm(3, 2, E),
-        dma((NA,)), dma((NA + 1,)), dma((2, NA + 1)), dma((NL, NA * NA + 1)), dma((2, 3, NA)), dma((2,)), dma((1,)),
+        dma((NA,)), dma((NA + 1,)), dma((2, NA + 1)), dma((NL, 2 * NA + 1)), dma((2, NA)), dma((2,)), dma((1,)),
         dma((NC * SUB,)), dma((NC * SUB,)), dma((2, NC * SUB)), dma((2, NC * SUB)), dma((2, NC * SUB)),
         dma((NL,)), dma((NL,)), dma((NA,)), dma((2, NA)), dma((2, NA)), dma((2, NA)), dma((2, NA)), dma((NA,)),
         dma((NL, NT - 1)), dma((NL, NT)), dma((NL,)), dma((NL,)), dma((1,)), dma((8,)),

time: 250 us -> 242 us (0.968)
  Pallas kernels: 248 us -> 241 us
    pallas_call x1, Pallas kernels: 240 us -> 234 us  [group_step(): pl.pallas_call(functools.partial(body, dims), out_shape=out_shape, in_spe...]
where the time goes in v5:
time: 242 us
  Pallas kernels  241 us (100%)
    pallas_call x1, Pallas kernels, group_step(): pl.pallas_call(functools.partial(body, dims), out_shape=out_shape, in_spe...  234 us
    pallas_call x1, Pallas kernels, finish_step(): pl.pallas_call(finish, out_shape=big + [row] * 7 + [jax.ShapeDtypeStruct(...  7.41 us

profile of v5, /device:TPU:0, one launch (start us, length us, event | category | flops | bytes accessed | tf_op | source)
XLA Modules:
  0.0 242.1 jit_solution(3350342718250035903)
XLA Ops:
  0.7 233.9 %neox_group.1 = (bf16[2,2,1024,512]{3,2,1,0:T(8,128)(2,1)}, f32[384,512]{1,0:T(8,128)}, f32[128,512]{1,0:T(8,128)}, f32[512,512]{1,0:T(8,128)}, f32[512,512]{1,0:T(8,128)}, /*index=5*/f32[8,512]{1,0:T(8,128)}) custom-call(bf16[2,2,1024,512]{3,2,1,0:T(8,128)(2,1)} %x.1, f32[2,2,1024,512]{3,2,1,0:T(8,128)} %g.1, bf16[384,512]{1,0:T(8,128)(2,1)} %bitcast.24, ...), custom_call_target="tpu_custom_call" | custom-call | tf_op jit(solution)/shard_map/neox_group/pallas_call | solution.py:812
  234.6 7.4 %neox_out.1 = (bf16[2,2,1024,512]{3,2,1,0:T(8,128)(2,1)}, f32[384,512]{1,0:T(8,128)}, f32[128,512]{1,0:T(8,128)}, f32[512,512]{1,0:T(8,128)}, f32[512,512]{1,0:T...) custom-call(bf16[2,2,1024,512]{3,2,1,0:T(8,128)(2,1)} %get-tuple-ele, ...), custom_call_target="tpu_custom_call" | custom-call | tf_op jit(solution)/shard_map/neox_out/pallas_call | solution.py:766

commit v6 on v5

--- a/solution.py
+++ b/solution.py
@@ -22,6 +22,7 @@
 NT = 4
 NC = 4
 NA = 4
+CORES = 2
 SUB = 2
 FWD_AT = {0: (('mid', 1, 0), ('last', 2, 0)), 2: (('mid', 1, 1), ('last', 2, 1))}
 BWD_AT = {0: (('last', 2, 0),), 1: (('mid', 1, 0),), 3: (('last', 2, 1),), 4: (('mid', 1, 1),)}
@@ -56,7 +57,7 @@
 
 def rotary_base(chunk, n_chunks, head_dim, n_heads):
     rot_dim = head_dim // 4
-    half = rot_dim // 2
+    half = rot_dim // CORES
     inv_freq = np.zeros((head_dim,), np.float64)
     inv_freq[:rot_dim] = np.tile(ROPE_BASE ** (-(np.arange(half) * 2.0) / rot_dim), 2)
     inv_freq = np.tile(inv_freq, n_heads)
@@ -70,14 +71,15 @@
          WQ, WO, WU, WD, VEC, H, Q, K, V, KT, VT, CTX, P0, P1, P2, P3, HID, GP, RA, RB, PS, PF,
          GQ, GO, GU, GD, R2Q, R2O, R2U, R2D, DK, DV, TAB, COS, SIN, GV, ZR, GZ, PR,
          AS, MS, PRE, DPB, DS, ST, N0, N1, N2, N3, N4, N5, N6, BQ,
-         wl, ws, wy, wr, wf, xs, gs, sab, sc, ra_s, rb_s, rc_s, ys, yr, g1s, g1r, g2s, g2r, g3s, g3r, v1s, v1r, v2s, v2r, osem, ns):
+         wl, ws, wy, wr, wf, w0s, w0r, xs, gs, sab, sc, ra_s, rb_s, rc_s, ys, yr, g1s, g1r, g2s, g2r, g3s, g3r, v1s, v1r, v2s, v2r, osem, ns):
     S, D, E, C, F = dims
     E2 = 2 * E
     SR = C // SUB
     z = lax.axis_index('tp')
+    xg = lax.axis_index('dp')
     s = lax.axis_index('pp')
-    ys_ = s // 2
-    c = s % 2
+    ys_ = s // CORES
+    c = s % CORES
     sib = s + 1 - 2 * c
     oy = 2 * (1 - ys_)
     is_end = z * (NT - 1 - z) == 0
@@ -88,13 +90,13 @@
     PX = (P0, P1, P2, P3)
     W_IN = (wqkv, wo, wup, wdn)
     W_BUF = (WQ, WO, WU, WD)
-    G_HALF = (3 * E, E, D // 2, F // 2)
+    G_HALF = (3 * E, E, D // CORES, F // CORES)
     ALL, FIRST, REST = tuple(range(NA)), (0,), (1, 2, 3)
     ATT, MLP = ALL[:2], ALL[2:]
     G_BUF = (GQ, GO, GU, GD)
     G_OUT = (oqkv, oo, oup, odn)
     G_COLS = (D, D, F, D)
-    R1_OFF = (0, 3 * E, 4 * E, 4 * E + D // 2)
+    R1_OFF = (0, 3 * E, 4 * E, 4 * E + D // CORES)
     R2 = (R2Q, R2O, R2U, R2D)
 
     def rcopy(src, dst, ss, rs, **dev):
@@ -123,7 +125,8 @@
         pl.semaphore_signal(bar, inc=1, device_id={'tp': (z + o) % NT}, device_id_type=pl.DeviceIdType.MESH)
     for o in range(1, NL):
         pl.semaphore_signal(bar, inc=1, device_id={'pp': (s + o) % NL}, device_id_type=pl.DeviceIdType.MESH)
-    pl.semaphore_wait(bar, NT + NL - 2)
+    pl.semaphore_signal(bar, inc=1, device_id={'dp': 1 - xg}, device_id_type=pl.DeviceIdType.MESH)
+    pl.semaphore_wait(bar, NT + NL - 1)
 
     def half(ref, a, k):
         return ref.at[rows(k * G_HALF[a], G_HALF[a])]
@@ -133,8 +136,37 @@
         return out + [rcopy(VEC.at[s], VEC.at[s], ws.at[NA], wr.at[s, 2 * NA], pp=sib)]
 
     def y_copies():
-        out = [rcopy(half(W_IN[a], a, k), half(W_BUF[a].at[s], a, k), wy.at[k, a], wr.at[s, 2 * a + k], pp=oy + k) for a in ALL for k in range(2)]
-        return out[:2] + [rcopy(VEC.at[s], VEC.at[s], wy.at[k, NA], wr.at[s, 2 * NA], pp=oy + k) for k in range(2)] + out[2:]
+        out = [rcopy(half(W_IN[a], a, k), half(W_BUF[a].at[s], a, k), wy.at[k, a], wr.at[s, 2 * a + k], pp=oy + k) for a in ALL for k in range(CORES)]
+        return out[:2] + [rcopy(VEC.at[s], VEC.at[s], wy.at[k, NA], wr.at[s, 2 * NA], pp=oy + k) for k in range(CORES)] + out[2:]
+
+    def quarter(ref, a, q):
+        return ref.at[rows(q * (G_HALF[a] // CORES), G_HALF[a] // CORES)]
+
+    def first_copies():
+        out = []
+        for a in ALL:
+            for k in range(CORES):
+                q = 2 * xg + k
+                out.append(rcopy(quarter(W_IN[a], a, q), quarter(W_BUF[a].at[0], a, q), wy.at[k, a], w0r.at[a, q], pp=oy + k))
+        return out + [rcopy(VEC.at[s], VEC.at[s], wy.at[k, NA], wr.at[s, 2 * NA], pp=oy + k) for k in range(CORES)]
+
+    def mine(hop):
+        return 2 * (xg if hop == 0 else 1 - xg) + c
+
+    def hop_copies(a, hop):
+        part, sem = quarter(W_BUF[a].at[0], a, mine(hop)), w0r.at[a, mine(hop)]
+        out = [rcopy(part, part, w0s.at[hop, a], sem, pp=sib)]
+        return out if hop else out + [rcopy(part, part, w0s.at[2, a], sem, dp=1 - xg)]
+
+    def hop_on(a, hop):
+        copies = hop_copies(a, hop)
+        copies[0].wait_recv()
+        start_all(copies)
+
+    def hop_end(a):
+        for k in range(CORES):
+            part = quarter(W_BUF[a].at[0], a, 2 * k + 1 - c)
+            rcopy(part, part, w0s.at[0, a], w0r.at[a, 2 * k + 1 - c], pp=sib).wait_recv()
 
     def start_all(copies):
         for cp in copies:
@@ -144,19 +176,23 @@
         cp.wait()
     for k, ref in enumerate((N0, N1, N2, N3, N4, N5, N6)):
         VEC[s, k:k + 1, :] = ref[...].astype(F32)
-    VEC[s, 7:8, :3 * E2] = jnp.concatenate([BQ[k, h:h + 1, :].astype(F32) for k in range(3) for h in range(2)], axis=1)
-
-    @pl.when(s != 1)
+    VEC[s, 7:8, :3 * E2] = jnp.concatenate([BQ[k, h:h + 1, :].astype(F32) for k in range(3) for h in range(CORES)], axis=1)
+
+    @pl.when(s == 0)
+    def _():
+        start_all(first_copies())
+
+    @pl.when(s > 1)
     def _():
         start_all(y_copies())
     start_all(sib_copies())
 
     def pass_copy(l, a, k):
         part = half(W_BUF[a].at[l], a, k)
-        return rcopy(part, part, wf.at[l % 2, a], wr.at[l, 2 * a + k], pp=sib)
+        return rcopy(part, part, wf.at[l % CORES, a], wr.at[l, 2 * a + k], pp=sib)
 
     def relay(l, arrays):
-        @pl.when(l // 2 != ys_)
+        @pl.when(l // CORES != ys_)
         def _():
             for a in arrays:
                 pass_copy(l, a, c).wait_recv()
@@ -173,7 +209,7 @@
             for a in arrays:
                 rcopy(W_IN[a], W_BUF[a].at[l], ws.at[a], wr.at[l, 2 * a], pp=sib).wait_recv()
 
-        @pl.when(l // 2 != ys_)
+        @pl.when((l // CORES != ys_) & (l > 0))
         def _():
             for a in arrays:
                 pass_copy(l, a, 1 - c).wait_recv()
@@ -211,13 +247,13 @@
         return v * cs + pltpu.roll(v * sa, rot_half, 1) + pltpu.roll(v * sb, E2 - rot_half, 1)
 
     def end_copy(p, t):
-        return rcopy(PS.at[t * SR:(t + 1) * SR], RA.at[p % 2, t * SR:(t + 1) * SR], sab.at[t], ra_s.at[p % 2, t], tp=hub)
+        return rcopy(PS.at[t * SR:(t + 1) * SR], RA.at[p % CORES, t * SR:(t + 1) * SR], sab.at[t], ra_s.at[p % CORES, t], tp=hub)
 
     def peer_copy(p, t):
-        return rcopy(PS.at[t * SR:(t + 1) * SR], RB.at[p % 2, t * SR:(t + 1) * SR], sab.at[t], rb_s.at[p % 2, t], tp=peer)
+        return rcopy(PS.at[t * SR:(t + 1) * SR], RB.at[p % CORES, t * SR:(t + 1) * SR], sab.at[t], rb_s.at[p % CORES, t], tp=peer)
 
     def back_copy(p, di, t):
-        return rcopy(H.at[di, t * SR:(t + 1) * SR], H.at[di, t * SR:(t + 1) * SR], sc.at[t], rc_s.at[p % 2, t], tp=leaf)
+        return rcopy(H.at[di, t * SR:(t + 1) * SR], H.at[di, t * SR:(t + 1) * SR], sc.at[t], rc_s.at[p % CORES, t], tp=leaf)
 
     def pf_row(i, back):
         return (NC if back and i == NC - 1 else i) * C
@@ -244,7 +280,7 @@
             @pl.when(p > 0)
             def _():
                 peer_copy(p, t).wait_send()
-            PS[r, :] = (PF[f0:f0 + SR, :] + RA[p % 2, r, :].astype(F32)).astype(BF16)
+            PS[r, :] = (PF[f0:f0 + SR, :] + RA[p % CORES, r, :].astype(F32)).astype(BF16)
             peer_copy(p, t).start()
 
     def ar_last(p, ri, di, i, u):
@@ -259,7 +295,7 @@
             @pl.when(p > 0)
             def _():
                 back_copy(p, di, t).wait_send()
-            both = PS[r, :].astype(F32) + RB[p % 2, r, :].astype(F32)
+            both = PS[r, :].astype(F32) + RB[p % CORES, r, :].astype(F32)
             H[di, r, :] = (H[ri, r, :].astype(F32) + both + bias).astype(BF16)
             back_copy(p, di, t).start()
 
@@ -289,7 +325,7 @@
         lax.fori_loop(0, C // LB, step, 0, unroll=True)
 
     def by_kind():
-        return [(h * 3 + k) * E for k in range(3) for h in range(2)]
+        return [(h * 3 + k) * E for k in range(3) for h in range(CORES)]
 
     def wq(l):
         return jnp.concatenate([WQ[l, r:r + E, :] for r in by_kind()], axis=0)
@@ -309,9 +345,9 @@
         KT[l, :, r0:r1] = jnp.transpose(kf).astype(BF16)
         VT[:, r0:r1] = jnp.transpose(vf).astype(BF16)
         yield
-        RBK = C // 2
+        RBK = C // CORES
         outs = []
-        for h in range(2):
+        for h in range(CORES):
             qm = jnp.where(head_lane == h, Q[l, r0:r1, :].astype(F32), 0.0).astype(BF16)
             ST[:r1, :] = nt(K[l, :r1, :], qm)
             ST[r0:r1, :] = jnp.where(lower, ST[r0:r1, :], -1e30)
@@ -339,9 +375,13 @@
         CTX[l, r0:r1, :] = ctx
         yield
         if i == 0:
-            @pl.when(l == 0)
-            def _():
-                relay(l, REST)
+            @pl.when((l == 0) & (ys_ == 1))
+            def _():
+                hop_on(3, 0)
+                hop_on(2, 1)
+                hop_on(3, 1)
+                for a in REST:
+                    hop_end(a)
             settle(l, REST, False)
         PF[r0:r1, :] = nn(ctx, WO[l])
         PRE[...] = nn(MS[...], WU[l])
@@ -361,7 +401,7 @@
 
     def backward(l, dl, i, last):
         r0, r1 = i * C, (i + 1) * C
-        par = l % 2
+        par = l % CORES
         first = i == NC - 1
 
         def acc(ref, val):
@@ -397,9 +437,9 @@
         prod = dctx.astype(F32) * ctx.astype(F32)
         q = Q[l, r0:r1, :].astype(F32)
         dcf = dctx.astype(F32)
-        RBK = C // 2
+        RBK = C // CORES
         dqt = []
-        for h in range(2):
+        for h in range(CORES):
             sel = head_lane == h
             qm = jnp.where(sel, q, 0.0).astype(BF16)
             dcm = jnp.where(sel, dcf, 0.0).astype(BF16)
@@ -464,16 +504,16 @@
         return GP.at[l + 1, R1_OFF[a]:R1_OFF[a] + G_HALF[a], :G_COLS[a]]
 
     def g1_copy(l, a):
-        return rcopy(G_BUF[a].at[l % 2, g_half(a, 1 - c)], r1_view(l, a), g1s.at[a], g1r.at[l % 2, a], pp=sib)
+        return rcopy(G_BUF[a].at[l % CORES, g_half(a, 1 - c)], r1_view(l, a), g1s.at[a], g1r.at[l % CORES, a], pp=sib)
 
     def g2_copy(l, a):
-        return rcopy(HID.at[l, R1_OFF[a]:R1_OFF[a] + G_HALF[a], :G_COLS[a]], R2[a].at[l % 2], g2s.at[l % 2, a], g2r.at[l % 2, a], pp=2 * (l // 2) + c)
+        return rcopy(HID.at[l, R1_OFF[a]:R1_OFF[a] + G_HALF[a], :G_COLS[a]], R2[a].at[l % CORES], g2s.at[l % CORES, a], g2r.at[l % CORES, a], pp=2 * (l // CORES) + c)
 
     def g3_local(l, a):
-        return lcopy(r1_view(l, a), G_OUT[a].at[g_half(a, c)], g3s.at[l % 2, a])
+        return lcopy(r1_view(l, a), G_OUT[a].at[g_half(a, c)], g3s.at[l % CORES, a])
 
     def g3_remote(l, a):
-        return rcopy(r1_view(l, a), G_OUT[a].at[g_half(a, c)], g3s.at[l % 2, a], g3r.at[a], pp=sib)
+        return rcopy(r1_view(l, a), G_OUT[a].at[g_half(a, c)], g3s.at[l % CORES, a], g3r.at[a], pp=sib)
 
     def v1_copies(l):
         return [rcopy(GV.at[l], ZR.at[l, z], v1s.at[l, o - 1], v1r.at[l, z], tp=(z + o) % NT) for o in range(1, NT)]
@@ -485,25 +525,25 @@
 
             def add(b, carry):
                 rr = rows(R1_OFF[a] + b * GR, GR)
-                tot = G_BUF[a][l % 2, rows(c * n + b * GR, GR), :] + GP[l + 1, rr, :G_COLS[a]]
+                tot = G_BUF[a][l % CORES, rows(c * n + b * GR, GR), :] + GP[l + 1, rr, :G_COLS[a]]
                 GP[l + 1, rr, :G_COLS[a]] = tot
                 HID[l, rr, :G_COLS[a]] = tot.astype(BF16)
                 return carry
             lax.fori_loop(0, n // GR, add, 0)
 
-            @pl.when(l // 2 != ys_)
+            @pl.when(l // CORES != ys_)
             def _():
                 g2_copy(l, a).start()
 
     def grads_last(l):
-        @pl.when(l // 2 == ys_)
+        @pl.when(l // CORES == ys_)
         def _():
             for a in MLP + ATT:
                 g2_copy(l, a).wait_recv()
 
                 def add(b, carry):
                     rr = rows(R1_OFF[a] + b * GR, GR)
-                    GP[l + 1, rr, :G_COLS[a]] += R2[a][l % 2, rows(b * GR, GR), :].astype(F32)
+                    GP[l + 1, rr, :G_COLS[a]] += R2[a][l % CORES, rows(b * GR, GR), :].astype(F32)
                     return carry
                 lax.fori_loop(0, G_HALF[a] // GR, add, 0)
 
@@ -517,7 +557,7 @@
 
     def grads_sent(l):
         for a in range(NA):
-            @pl.when(l // 2 != ys_)
+            @pl.when(l // CORES != ys_)
             def _():
                 g2_copy(l, a).wait_send()
 
@@ -525,7 +565,7 @@
             def _():
                 g3_local(l, a).wait()
 
-            @pl.when((l // 2 == ys_) & (l != s))
+            @pl.when((l // CORES == ys_) & (l != s))
             def _():
                 g3_remote(l, a).wait_send()
 
@@ -550,7 +590,11 @@
             v2_copy(l).start()
 
     GV[...] = jnp.zeros_like(GV)
-    relay(0, FIRST)
+    @pl.when(ys_ == 1)
+    def _():
+        for a, hop in ((0, 0), (1, 0), (0, 1), (2, 0), (1, 1)):
+            hop_on(a, hop)
+        hop_end(0)
     settle(0, FIRST, True)
     xcopy.wait()
 
@@ -591,13 +635,18 @@
                     @pl.when(s == 1)
                     def _():
                         start_all(y_copies())
-            if i > 1:
+            if i == 2:
+                @pl.when((l > 0) & (l < NL - 1))
+                def _():
+                    relay(l + 1, ALL)
+            if i == NC - 1:
+                @pl.when(l == 0)
+                def _():
+                    relay(l + 1, ALL)
+
                 @pl.when(l < NL - 1)
                 def _():
-                    if i < NC - 1:
-                        relay(l + 1, ALL)
-                    else:
-                        settle(l + 1, FIRST, True)
+                    settle(l + 1, FIRST, True)
         return carry
     lax.fori_loop(0, NL, fwd_layer, 0)
 
@@ -607,7 +656,7 @@
     y_fwd = rcopy(y.at[1 - ys_, c], y.at[1 - ys_, c], ys.at[3], yr.at[oy + c], pp=sib)
 
     def y_arrived(q):
-        rcopy(H.at[NL], y.at[q // 2, q % 2], ys.at[1], yr.at[q], pp=sib).wait_recv()
+        rcopy(H.at[NL], y.at[q // CORES, q % CORES], ys.at[1], yr.at[q], pp=sib).wait_recv()
 
     def ri(l):
         return jnp.where(l == NL - 1, NL + 1, l + 1)
@@ -661,11 +710,6 @@
             @pl.when(l > 0)
             def _():
                 ar_send(p, i, True)
-            if n == 0:
-                @pl.when(lb == 2)
-                def _():
-                    y_arrived(oy + c)
-                    y_fwd.start()
             if n == 1:
                 @pl.when(lb > 0)
                 def _():
@@ -689,6 +733,8 @@
     lax.fori_loop(0, NL, bwd_layer, 0)
 
     grads_mid(0, ATT)
+    y_arrived(oy + c)
+    y_fwd.start()
     grads_last(1)
     vec_mid(0)
     grads_last(0)
@@ -719,11 +765,27 @@
         grads_sent(l)
     for cp in sib_copies():
         cp.wait_send()
-    for cp in y_copies():
-        cp.wait_send()
-    for k in range(2):
-        for a in ALL:
-            pass_copy(oy + k, a, c).wait_send()
+    @pl.when(s == 0)
+    def _():
+        for cp in first_copies():
+            cp.wait_send()
+
+    @pl.when(s > 0)
+    def _():
+        for cp in y_copies():
+            cp.wait_send()
+    for a in ALL:
+        pass_copy(oy + 1, a, c).wait_send()
+
+        @pl.when(ys_ == 0)
+        def _():
+            pass_copy(oy, a, c).wait_send()
+
+        @pl.when(ys_ == 1)
+        def _():
+            for hop in range(CORES):
+                for cp in hop_copies(a, hop):
+                    cp.wait_send()
 
     @pl.when(is_end)
     def _():
@@ -750,7 +812,7 @@
             ref[...] = gv[row:row + 1, :]
     e = bq.shape[2]
     for k in range(3):
-        for h in range(2):
+        for h in range(CORES):
             bq[k, h:h + 1, :] = gv[6:7, (2 * k + h) * e:(2 * k + h + 1) * e]
     for cp, out in zip(loads, stores):
         cp.wait()
@@ -796,17 +858,17 @@
         vm(NL, S, E2), vm(NL, S, E2), vm(NL, S, E2), vm(NL, E2, S), vm(E2, S), vm(NL, S, E2),
         *[vm(NL, 2, (i + 1) * C, C) for i in range(NC)],
         vm(NL, S, F), vm(NL + 1, S, F, dtype=F32),
-        vm(2, S, D), vm(2, S, D), vm(S, D), vm(S + C, D, dtype=F32),
-        vm(2, 3 * E2, D, dtype=F32), vm(2, E2, D, dtype=F32), vm(2, D, F, dtype=F32), vm(2, F, D, dtype=F32),
-        vm(2, 3 * E, D), vm(2, E, D), vm(2, D // 2, F), vm(2, F // 2, D),
+        vm(CORES, S, D), vm(CORES, S, D), vm(S, D), vm(S + C, D, dtype=F32),
+        vm(CORES, 3 * E2, D, dtype=F32), vm(CORES, E2, D, dtype=F32), vm(CORES, D, F, dtype=F32), vm(CORES, F, D, dtype=F32),
+        vm(CORES, 3 * E, D), vm(CORES, E, D), vm(CORES, D // CORES, F), vm(CORES, F // CORES, D),
         vm(S, E2, dtype=F32), vm(S, E2, dtype=F32),
-        vm(2, C + 8, E2, dtype=F32), vm(S, E2, dtype=F32), vm(S, E2, dtype=F32),
+        vm(CORES, C + 8, E2, dtype=F32), vm(S, E2, dtype=F32), vm(S, E2, dtype=F32),
         vm(NL, 8, D, dtype=F32), vm(NL, NT, 8, D, dtype=F32), vm(NL, 8, D, dtype=F32), vm(NL, 8, D, dtype=F32),
         vm(C, D), vm(C, D), vm(C, max(D, F), dtype=F32), vm(C, F), vm(S, C), vm(S, C, dtype=F32),
         *[vm(1, D, dtype=F32)] * 4, vm(1, D), vm(1, D), vm(1, F), vm(3, 2, E),
-        dma((NA,)), dma((NA + 1,)), dma((2, NA + 1)), dma((NL, 2 * NA + 1)), dma((2, NA)), dma((2,)), dma((1,)),
-        dma((NC * SUB,)), dma((NC * SUB,)), dma((2, NC * SUB)), dma((2, NC * SUB)), dma((2, NC * SUB)),
-        dma((NL,)), dma((NL,)), dma((NA,)), dma((2, NA)), dma((2, NA)), dma((2, NA)), dma((2, NA)), dma((NA,)),
+        dma((NA,)), dma((NA + 1,)), dma((CORES, NA + 1)), dma((NL, 2 * NA + 1)), dma((CORES, NA)), dma((3, NA)), dma((NA, 4)), dma((CORES,)), dma((1,)),
+        dma((NC * SUB,)), dma((NC * SUB,)), dma((CORES, NC * SUB)), dma((CORES, NC * SUB)), dma((CORES, NC * SUB)),
+        dma((NL,)), dma((NL,)), dma((NA,)), dma((CORES, NA)), dma((CORES, NA)), dma((CORES, NA)), dma((CORES, NA)), dma((NA,)),
         dma((NL, NT - 1)), dma((NL, NT)), dma((NL,)), dma((NL,)), dma((1,)), dma((8,)),
     ]
     return pl.pallas_call(

time: 242 us -> 234 us (0.967)
  Pallas kernels: 241 us -> 233 us
    pallas_call x1, Pallas kernels: 234 us -> 225 us  [group_step(): pl.pallas_call(functools.partial(body, dims), out_shape=out_shape, in_spe...]
where the time goes in v6:
time: 234 us; the launch traced here: 233 us
  Pallas kernels  233 us (100%)
    pallas_call x1, Pallas kernels, group_step(): pl.pallas_call(functools.partial(body, dims), out_shape=out_shape, in_spe...  225 us
    pallas_call x1, Pallas kernels, finish_step(): pl.pallas_call(finish, out_shape=big + [row] * 7 + [jax.ShapeDtypeStruct(...  7.41 us

profile of v6, /device:TPU:0, one launch (start us, length us, event | category | flops | bytes accessed | tf_op | source)
XLA Modules:
  0.0 233.4 jit_solution(14050753201140288970)
XLA Ops:
  0.7 225.2 %neox_group.1 = (bf16[2,2,1024,512]{3,2,1,0:T(8,128)(2,1)}, f32[384,512]{1,0:T(8,128)}, f32[128,512]{1,0:T(8,128)}, f32[512,512]{1,0:T(8,128)}, f32[512,512]{1,0:T(8,128)}, /*index=5*/f32[8,512]{1,0:T(8,128)}) custom-call(bf16[2,2,1024,512]{3,2,1,0:T(8,128)(2,1)} %x.1, f32[2,2,1024,512]{3,2,1,0:T(8,128)} %g.1, bf16[384,512]{1,0:T(8,128)(2,1)} %bitcast.24, ...), custom_call_target="tpu_custom_call" | custom-call | tf_op jit(solution)/shard_map/neox_group/pallas_call | solution.py:874
  225.8 7.4 %neox_out.1 = (bf16[2,2,1024,512]{3,2,1,0:T(8,128)(2,1)}, f32[384,512]{1,0:T(8,128)}, f32[128,512]{1,0:T(8,128)}, f32[512,512]{1,0:T(8,128)}, f32[512,512]{1,0:T...) custom-call(bf16[2,2,1024,512]{3,2,1,0:T(8,128)(2,1)} %get-tuple-ele, ...), custom_call_target="tpu_custom_call" | custom-call | tf_op jit(solution)/shard_map/neox_out/pallas_call | solution.py:828

commit v7 on v6

--- a/solution.py
+++ b/solution.py
@@ -23,9 +23,9 @@
 NC = 4
 NA = 4
 CORES = 2
-SUB = 2
-FWD_AT = {0: (('mid', 1, 0), ('last', 2, 0)), 2: (('mid', 1, 1), ('last', 2, 1))}
-BWD_AT = {0: (('last', 2, 0),), 1: (('mid', 1, 0),), 3: (('last', 2, 1),), 4: (('mid', 1, 1),)}
+SUB = 4
+FWD_AT = {k: (('mid', 1, k), ('last', 2, k)) for k in range(SUB)}
+BWD_AT = {k: (('last', 2, k),) * (k < SUB) + (('mid', 1, k - 1),) * (k > 0) for k in range(SUB + 1)}
 LOG2E = 1.4426950408889634
 RSQRT2 = 0.7071067811865476
 INV_SQRT_2PI = 0.3989422804014327
@@ -345,6 +345,14 @@
         KT[l, :, r0:r1] = jnp.transpose(kf).astype(BF16)
         VT[:, r0:r1] = jnp.transpose(vf).astype(BF16)
         yield
+
+        def far(*hops):
+            if i == 0:
+                @pl.when((l == 0) & (ys_ == 1))
+                def _():
+                    for a, hop in hops:
+                        hop_on(a, hop)
+        far((2, 0), (1, 1))
         RBK = C // CORES
         outs = []
         for h in range(CORES):
@@ -371,15 +379,15 @@
             outs.append(nn(VT[:, :r1], PX[i][l, h]))
             if h == 0:
                 yield
+                far((3, 0))
         ctx = jnp.transpose(jnp.where(sub_head == 0, outs[0], outs[1])).astype(BF16)
         CTX[l, r0:r1, :] = ctx
         yield
         if i == 0:
+            far((2, 1), (3, 1))
+
             @pl.when((l == 0) & (ys_ == 1))
             def _():
-                hop_on(3, 0)
-                hop_on(2, 1)
-                hop_on(3, 1)
                 for a in REST:
                     hop_end(a)
             settle(l, REST, False)
@@ -592,7 +600,7 @@
     GV[...] = jnp.zeros_like(GV)
     @pl.when(ys_ == 1)
     def _():
-        for a, hop in ((0, 0), (1, 0), (0, 1), (2, 0), (1, 1)):
+        for a, hop in ((0, 0), (1, 0), (0, 1)):
             hop_on(a, hop)
         hop_end(0)
     settle(0, FIRST, True)
@@ -702,9 +710,11 @@
                         grads_mid(l + 1, ATT)
                         for a in ALL:
                             g1_copy(l + 1, a).wait_send()
-                if k == 1 and n == NC - 1:
+                if n == NC - 1 and k == 1:
                     for a in MLP:
                         g1_copy(l, a).start()
+                if n == NC - 1 and k == 3:
+                    grads_mid(l, MLP)
             run(backward(l, ri(l), i, False), BWD_AT, handle, after)
 
             @pl.when(l > 0)
@@ -728,7 +738,6 @@
         for a in ATT:
             g1_copy(l, a).start()
         start_all(v1_copies(l))
-        grads_mid(l, MLP)
         return carry
     lax.fori_loop(0, NL, bwd_layer, 0)
 
@@ -800,37 +809,45 @@
     vout.wait()
 
 
-def finish(y, gq, go, gu, gd, gv, yo, qo, oo, uo, do, n0, n1, n2, n3, n4, n5, n6, bq, yb, qb, ob, ub, db, got, put):
+def finish(y, gq, go, gu, gd, gv, yo, qo, oo, uo, do, n0, n1, n2, n3, n4, n5, n6, bq,
+           yb, qb, ob, ub, db, vb, r0, r1, r2, r3, r4, r5, r6, rq, got, put, small):
     trips = [(gd, db, do), (gu, ub, uo), (go, ob, oo), (gq, qb, qo)]
     trips += [tuple(ref.at[m, r] for ref in (y, yb, yo)) for m in range(y.shape[0]) for r in range(y.shape[1])]
     loads = [pltpu.make_async_copy(a, b, got.at[k]) for k, (a, b, o) in enumerate(trips)]
     stores = [pltpu.make_async_copy(b, o, put.at[k]) for k, (a, b, o) in enumerate(trips)]
+    vecs = pltpu.make_async_copy(gv, vb, small.at[len(trips)])
+    vecs.start()
     for cp in loads:
         cp.start()
-    for row, refs in enumerate(((n0,), (n1,), (n2,), (n3,), (n4, n5), (n6,))):
+    vecs.wait()
+    for row, refs in enumerate(((r0,), (r1,), (r2,), (r3,), (r4, r5), (r6,))):
         for ref in refs:
-            ref[...] = gv[row:row + 1, :]
-    e = bq.shape[2]
+            ref[...] = vb[row:row + 1, :]
+    e = rq.shape[2]
     for k in range(3):
         for h in range(CORES):
-            bq[k, h:h + 1, :] = gv[6:7, (2 * k + h) * e:(2 * k + h + 1) * e]
+            rq[k, h:h + 1, :] = vb[6:7, (CORES * k + h) * e:(CORES * k + h + 1) * e]
+    tiny = [pltpu.make_async_copy(a, b, small.at[k]) for k, (a, b) in enumerate(((r0, n0), (r1, n1), (r2, n2), (r3, n3), (r4, n4), (r5, n5), (r6, n6), (rq, bq)))]
+    for cp in tiny:
+        cp.start()
     for cp, out in zip(loads, stores):
         cp.wait()
         out.start()
-    for cp in stores:
+    for cp in tiny + stores:
         cp.wait()
 
 
 def finish_step(y, gq, go, gu, gd, gv, e):
-    hbm, vmem = pl.BlockSpec(memory_space=pl.ANY), pl.BlockSpec(memory_space=pltpu.VMEM)
-    big = [jax.ShapeDtypeStruct(a.shape, a.dtype) for a in (y, gq, go, gu, gd)]
+    hbm = pl.BlockSpec(memory_space=pl.ANY)
     row = jax.ShapeDtypeStruct((1, gv.shape[1]), F32)
+    outs = [jax.ShapeDtypeStruct(a.shape, a.dtype) for a in (y, gq, go, gu, gd)] + [row] * 7 + [jax.ShapeDtypeStruct((3, CORES, e), F32)]
+    bufs = outs[:5] + [gv] + outs[5:]
     return pl.pallas_call(
         finish,
-        out_shape=big + [row] * 7 + [jax.ShapeDtypeStruct((3, 2, e), F32)],
-        in_specs=[hbm] * 5 + [vmem],
-        out_specs=[hbm] * 5 + [vmem] * 8,
-        scratch_shapes=[pltpu.VMEM(a.shape, a.dtype) for a in big] + [pltpu.SemaphoreType.DMA((8,))] * 2,
+        out_shape=outs,
+        in_specs=[hbm] * 6,
+        out_specs=[hbm] * len(outs),
+        scratch_shapes=[pltpu.VMEM(a.shape, a.dtype) for a in bufs] + [pltpu.SemaphoreType.DMA((9,))] * 3,
         name='neox_out',
     )(y, gq, go, gu, gd, gv)
 

time: 234 us -> 234 us (level)
  no operation moved by 1% of the time
where the time goes in v7:
time: 234 us; the launch traced here: 233 us
  Pallas kernels  233 us (100%)
    pallas_call x1, Pallas kernels, group_step(): pl.pallas_call(functools.partial(body, dims), out_shape=out_shape, in_spe...  227 us
    pallas_call x1, Pallas kernels, finish_step(): pl.pallas_call(finish, out_shape=outs, in_specs=[hbm] * 6, out_specs=[hbm...  5.89 us

profile of v7, /device:TPU:0, one launch (start us, length us, event | category | flops | bytes accessed | tf_op | source)
XLA Modules:
  0.0 233.3 jit_solution(7151921011811147991)
XLA Ops:
  0.7 226.6 %neox_group.1 = (bf16[2,2,1024,512]{3,2,1,0:T(8,128)(2,1)}, f32[384,512]{1,0:T(8,128)}, f32[128,512]{1,0:T(8,128)}, f32[512,512]{1,0:T(8,128)}, f32[512,512]{1,0:T(8,128)}, /*index=5*/f32[8,512]{1,0:T(8,128)}) custom-call(bf16[2,2,1024,512]{3,2,1,0:T(8,128)(2,1)} %x.1, f32[2,2,1024,512]{3,2,1,0:T(8,128)} %g.1, bf16[384,512]{1,0:T(8,128)(2,1)} %bitcast.24, ...), custom_call_target="tpu_custom_call" | custom-call | tf_op jit(solution)/shard_map/neox_group/pallas_call | solution.py:891
  227.3 5.9 %neox_out.1 = (bf16[2,2,1024,512]{3,2,1,0:T(8,128)(2,1)}, f32[384,512]{1,0:T(8,128)}, f32[128,512]{1,0:T(8,128)}, f32[512,512]{1,0:T(8,128)}, f32[512,512]{1,0:T...) custom-call(bf16[2,2,1024,512]{3,2,1,0:T(8,128)(2,1)} %get-tuple-ele, ...), custom_call_target="tpu_custom_call" | custom-call | tf_op jit(solution)/shard_map/neox_out/pallas_call | solution.py:845

commit v8 on v7

--- a/solution.py
+++ b/solution.py
@@ -23,9 +23,9 @@
 NC = 4
 NA = 4
 CORES = 2
-SUB = 4
-FWD_AT = {k: (('mid', 1, k), ('last', 2, k)) for k in range(SUB)}
-BWD_AT = {k: (('last', 2, k),) * (k < SUB) + (('mid', 1, k - 1),) * (k > 0) for k in range(SUB + 1)}
+SUB = 2
+FWD_AT = {0: (('mid', 1, 0), ('last', 2, 0)), 2: (('mid', 1, 1), ('last', 2, 1))}
+BWD_AT = {0: (('last', 2, 0),), 1: (('mid', 1, 0),), 3: (('last', 2, 1),), 4: (('mid', 1, 1),)}
 LOG2E = 1.4426950408889634
 RSQRT2 = 0.7071067811865476
 INV_SQRT_2PI = 0.3989422804014327

time: 234 us -> 235 us (level)
  no operation moved by 1% of the time
where the time goes in v8:
time: 235 us
  Pallas kernels  235 us (100%)
    pallas_call x1, Pallas kernels, group_step(): pl.pallas_call(functools.partial(body, dims), out_shape=out_shape, in_spe...  229 us
    pallas_call x1, Pallas kernels, finish_step(): pl.pallas_call(finish, out_shape=outs, in_specs=[hbm] * 6, out_specs=[hbm...  5.89 us

profile of v8, /device:TPU:0, one launch (start us, length us, event | category | flops | bytes accessed | tf_op | source)
XLA Modules:
  0.0 235.3 jit_solution(3825744950975419357)
XLA Ops:
  0.7 228.6 %neox_group.1 = (bf16[2,2,1024,512]{3,2,1,0:T(8,128)(2,1)}, f32[384,512]{1,0:T(8,128)}, f32[128,512]{1,0:T(8,128)}, f32[512,512]{1,0:T(8,128)}, f32[512,512]{1,0:T(8,128)}, /*index=5*/f32[8,512]{1,0:T(8,128)}) custom-call(bf16[2,2,1024,512]{3,2,1,0:T(8,128)(2,1)} %x.1, f32[2,2,1024,512]{3,2,1,0:T(8,128)} %g.1, bf16[384,512]{1,0:T(8,128)(2,1)} %bitcast.24, ...), custom_call_target="tpu_custom_call" | custom-call | tf_op jit(solution)/shard_map/neox_group/pallas_call | solution.py:891
  229.3 5.9 %neox_out.1 = (bf16[2,2,1024,512]{3,2,1,0:T(8,128)(2,1)}, f32[384,512]{1,0:T(8,128)}, f32[128,512]{1,0:T(8,128)}, f32[512,512]{1,0:T(8,128)}, f32[512,512]{1,0:T...) custom-call(bf16[2,2,1024,512]{3,2,1,0:T(8,128)(2,1)} %get-tuple-ele, ...), custom_call_target="tpu_custom_call" | custom-call | tf_op jit(solution)/shard_map/neox_out/pallas_call | solution.py:845

commit v9 on v7

--- a/solution.py
+++ b/solution.py
@@ -714,7 +714,9 @@
                     for a in MLP:
                         g1_copy(l, a).start()
                 if n == NC - 1 and k == 3:
-                    grads_mid(l, MLP)
+                    @pl.when(l == 0)
+                    def _():
+                        grads_mid(l, MLP)
             run(backward(l, ri(l), i, False), BWD_AT, handle, after)
 
             @pl.when(l > 0)
@@ -738,6 +740,10 @@
         for a in ATT:
             g1_copy(l, a).start()
         start_all(v1_copies(l))
+
+        @pl.when(l > 0)
+        def _():
+            grads_mid(l, MLP)
         return carry
     lax.fori_loop(0, NL, bwd_layer, 0)
 

time: 234 us -> 233 us (level)
  no operation moved by 1% of the time
where the time goes in v9:
time: 233 us
  Pallas kernels  232 us (100%)
    pallas_call x1, Pallas kernels, group_step(): pl.pallas_call(functools.partial(body, dims), out_shape=out_shape, in_spe...  226 us
    pallas_call x1, Pallas kernels, finish_step(): pl.pallas_call(finish, out_shape=outs, in_specs=[hbm] * 6, out_specs=[hbm...  5.89 us

profile of v9, /device:TPU:0, one launch (start us, length us, event | category | flops | bytes accessed | tf_op | source)
XLA Modules:
  0.0 233.1 jit_solution(13967656070032663136)
XLA Ops:
  0.7 226.4 %neox_group.1 = (bf16[2,2,1024,512]{3,2,1,0:T(8,128)(2,1)}, f32[384,512]{1,0:T(8,128)}, f32[128,512]{1,0:T(8,128)}, f32[512,512]{1,0:T(8,128)}, f32[512,512]{1,0:T(8,128)}, /*index=5*/f32[8,512]{1,0:T(8,128)}) custom-call(bf16[2,2,1024,512]{3,2,1,0:T(8,128)(2,1)} %x.1, f32[2,2,1024,512]{3,2,1,0:T(8,128)} %g.1, bf16[384,512]{1,0:T(8,128)(2,1)} %bitcast.24, ...), custom_call_target="tpu_custom_call" | custom-call | tf_op jit(solution)/shard_map/neox_group/pallas_call | solution.py:897
  227.0 5.9 %neox_out.1 = (bf16[2,2,1024,512]{3,2,1,0:T(8,128)(2,1)}, f32[384,512]{1,0:T(8,128)}, f32[128,512]{1,0:T(8,128)}, f32[512,512]{1,0:T(8,128)}, f32[512,512]{1,0:T...) custom-call(bf16[2,2,1024,512]{3,2,1,0:T(8,128)(2,1)} %get-tuple-ele, ...), custom_call_target="tpu_custom_call" | custom-call | tf_op jit(solution)/shard_map/neox_out/pallas_call | solution.py:851

commit v10 on v8

--- a/solution.py
+++ b/solution.py
@@ -352,7 +352,7 @@
                 def _():
                     for a, hop in hops:
                         hop_on(a, hop)
-        far((2, 0), (1, 1))
+        far((3, 0))
         RBK = C // CORES
         outs = []
         for h in range(CORES):
@@ -379,7 +379,6 @@
             outs.append(nn(VT[:, :r1], PX[i][l, h]))
             if h == 0:
                 yield
-                far((3, 0))
         ctx = jnp.transpose(jnp.where(sub_head == 0, outs[0], outs[1])).astype(BF16)
         CTX[l, r0:r1, :] = ctx
         yield
@@ -600,7 +599,7 @@
     GV[...] = jnp.zeros_like(GV)
     @pl.when(ys_ == 1)
     def _():
-        for a, hop in ((0, 0), (1, 0), (0, 1)):
+        for a, hop in ((0, 0), (1, 0), (0, 1), (2, 0), (1, 1)):
             hop_on(a, hop)
         hop_end(0)
     settle(0, FIRST, True)
@@ -713,8 +712,6 @@
                 if n == NC - 1 and k == 1:
                     for a in MLP:
                         g1_copy(l, a).start()
-                if n == NC - 1 and k == 3:
-                    grads_mid(l, MLP)
             run(backward(l, ri(l), i, False), BWD_AT, handle, after)
 
             @pl.when(l > 0)
@@ -738,6 +735,7 @@
         for a in ATT:
             g1_copy(l, a).start()
         start_all(v1_copies(l))
+        grads_mid(l, MLP)
         return carry
     lax.fori_loop(0, NL, bwd_layer, 0)
 

time: 235 us -> 231 us (0.983)
  Pallas kernels: 235 us -> 230 us
    pallas_call x1, Pallas kernels: 229 us -> 224 us  [group_step(): pl.pallas_call(functools.partial(body, dims), out_shape=out_shape, in_spe...]
where the time goes in v10:
time: 231 us
  Pallas kernels  230 us (100%)
    pallas_call x1, Pallas kernels, group_step(): pl.pallas_call(functools.partial(body, dims), out_shape=out_shape, in_spe...  224 us
    pallas_call x1, Pallas kernels, finish_step(): pl.pallas_call(finish, out_shape=outs, in_specs=[hbm] * 6, out_specs=[hbm...  5.89 us

profile of v10, /device:TPU:0, one launch (start us, length us, event | category | flops | bytes accessed | tf_op | source)
XLA Modules:
  0.0 231.0 jit_solution(6712385028652167927)
XLA Ops:
  0.7 224.3 %neox_group.1 = (bf16[2,2,1024,512]{3,2,1,0:T(8,128)(2,1)}, f32[384,512]{1,0:T(8,128)}, f32[128,512]{1,0:T(8,128)}, f32[512,512]{1,0:T(8,128)}, f32[512,512]{1,0:T(8,128)}, /*index=5*/f32[8,512]{1,0:T(8,128)}) custom-call(bf16[2,2,1024,512]{3,2,1,0:T(8,128)(2,1)} %x.1, f32[2,2,1024,512]{3,2,1,0:T(8,128)} %g.1, bf16[384,512]{1,0:T(8,128)(2,1)} %bitcast.24, ...), custom_call_target="tpu_custom_call" | custom-call | tf_op jit(solution)/shard_map/neox_group/pallas_call | solution.py:889
  225.0 5.9 %neox_out.1 = (bf16[2,2,1024,512]{3,2,1,0:T(8,128)(2,1)}, f32[384,512]{1,0:T(8,128)}, f32[128,512]{1,0:T(8,128)}, f32[512,512]{1,0:T(8,128)}, f32[512,512]{1,0:T...) custom-call(bf16[2,2,1024,512]{3,2,1,0:T(8,128)(2,1)} %get-tuple-ele, ...), custom_call_target="tpu_custom_call" | custom-call | tf_op jit(solution)/shard_map/neox_out/pallas_call | solution.py:843

commit v11 on v10

--- a/solution.py
+++ b/solution.py
@@ -69,9 +69,9 @@
 def body(dims, x, g, wqkv, wo, wup, wdn, n0, n1, n2, n3, n4, n5, n6, bq, tab,
          y, oqkv, oo, oup, odn, ovec,
          WQ, WO, WU, WD, VEC, H, Q, K, V, KT, VT, CTX, P0, P1, P2, P3, HID, GP, RA, RB, PS, PF,
-         GQ, GO, GU, GD, R2Q, R2O, R2U, R2D, DK, DV, TAB, COS, SIN, GV, ZR, GZ, PR,
-         AS, MS, PRE, DPB, DS, ST, N0, N1, N2, N3, N4, N5, N6, BQ,
-         wl, ws, wy, wr, wf, w0s, w0r, xs, gs, sab, sc, ra_s, rb_s, rc_s, ys, yr, g1s, g1r, g2s, g2r, g3s, g3r, v1s, v1r, v2s, v2r, osem, ns):
+         GQ, GO, GU, GD, R2Q, R2O, R2U, R2D, DK, DV, TAB, GV, ZR, GZ, PR,
+         AS, MS, PRE, DPB, DS, ST, N0, N1, N2, N3, N4, N5, N6, BQ, GX,
+         wl, ws, wy, wr, wf, w0s, w0r, xs, gs, sab, sc, ra_s, rb_s, rc_s, ys, yr, g1s, g1r, g2s, g2r, g3s, g3r, v1s, v1r, v2s, v2r, osem, ns, gxs, gxr, gs2, gs3, ygs):
     S, D, E, C, F = dims
     E2 = 2 * E
     SR = C // SUB
@@ -84,6 +84,7 @@
     oy = 2 * (1 - ys_)
     is_end = z * (NT - 1 - z) == 0
     inner = z * (NT - 1 - z) > 0
+    edge = 1 - jnp.minimum(z * (NT - 1 - z), 1)
     hub = 1 + z // 3
     leaf = jnp.where(z == 1, 0, 3)
     peer = 3 - z
@@ -91,12 +92,13 @@
     W_IN = (wqkv, wo, wup, wdn)
     W_BUF = (WQ, WO, WU, WD)
     G_HALF = (3 * E, E, D // CORES, F // CORES)
-    ALL, FIRST, REST = tuple(range(NA)), (0,), (1, 2, 3)
+    ALL = tuple(range(NA))
+    FIRST, REST = ALL[:1], ALL[1:]
     ATT, MLP = ALL[:2], ALL[2:]
     G_BUF = (GQ, GO, GU, GD)
     G_OUT = (oqkv, oo, oup, odn)
     G_COLS = (D, D, F, D)
-    R1_OFF = (0, 3 * E, 4 * E, 4 * E + D // CORES)
+    R1_OFF = tuple(sum(G_HALF[:k]) for k in range(NA))
     R2 = (R2Q, R2O, R2U, R2D)
 
     def rcopy(src, dst, ss, rs, **dev):
@@ -219,11 +221,6 @@
                 rcopy(VEC.at[l], VEC.at[l], ws.at[NA], wr.at[l, 2 * NA], pp=sib).wait_recv()
 
     tcopy.wait()
-    for i in range(NC):
-        cb, sb = TAB[0, :C, :], TAB[1, :C, :]
-        cr, sr = TAB[0, C + i:C + i + 1, :], TAB[1, C + i:C + i + 1, :]
-        COS[i * C:(i + 1) * C, :] = cb * cr - sb * sr
-        SIN[i * C:(i + 1) * C, :] = sb * cr + cb * sr
 
     lane = lax.broadcasted_iota(jnp.int32, (C, E2), 1)
     head_lane = lane // E
@@ -235,7 +232,8 @@
     c1 = E ** -0.5 * LOG2E
 
     def tabs(i):
-        cs, sn = COS[i * C:(i + 1) * C, :], SIN[i * C:(i + 1) * C, :]
+        (cb, sb), (cr, sr) = ([TAB[k, r, :] for k in range(CORES)] for r in (slice(C), slice(C + i, C + i + 1)))
+        cs, sn = cb * cr - sb * sr, sb * cr + cb * sr
         return cs, jnp.where(low, -sn, 0.0), jnp.where(low, 0.0, sn)
 
     def rotate(v, t):
@@ -269,6 +267,9 @@
                 PS[t * SR:(t + 1) * SR, :] = PF[f0:f0 + SR, :].astype(BF16)
                 end_copy(p, t).start()
 
+    def out_bias(l):
+        return VEC[l, 4:5, :] + VEC[l, 5:6, :]
+
     def ar_mid(p, i, u, back=False):
         t = i * SUB + u
         r = slice(t * SR, (t + 1) * SR)
@@ -283,27 +284,91 @@
             PS[r, :] = (PF[f0:f0 + SR, :] + RA[p % CORES, r, :].astype(F32)).astype(BF16)
             peer_copy(p, t).start()
 
-    def ar_last(p, ri, di, i, u):
+    def ar_last(p, ri, di, i, u, back=False):
         t = i * SUB + u
         r = slice(t * SR, (t + 1) * SR)
 
         @pl.when(inner)
         def _():
-            lv = jnp.minimum(p, NL - 1)
-            bias = (VEC[lv, 4:5, :] + VEC[lv, 5:6, :]) * jnp.where(p < NL, 1.0, 0.0)
             peer_copy(p, t).wait_recv()
             @pl.when(p > 0)
             def _():
                 back_copy(p, di, t).wait_send()
             both = PS[r, :].astype(F32) + RB[p % CORES, r, :].astype(F32)
-            H[di, r, :] = (H[ri, r, :].astype(F32) + both + bias).astype(BF16)
+            own = H[ri, r, :].astype(F32)
+            H[di, r, :] = (own + both if back else own + both + out_bias(p)).astype(BF16)
             back_copy(p, di, t).start()
 
-    def ar_wait(p, di, i):
-        @pl.when(is_end)
+    def ar_wait(p, di, i, on=1):
+        @pl.when(on * edge > 0)
         def _():
             for t in range(i * SUB, (i + 1) * SUB):
                 back_copy(p, di, t).wait_recv()
+
+    GP1 = NL % 3
+
+    def guest_copy(i):
+        part = GX.at[i * C:(i + 1) * C]
+        return rcopy(part, part, gxs.at[i], gxr.at[i], pp=c)
+
+    def guest_send(i):
+        r = slice(i * C, (i + 1) * C)
+        once = jnp.where(z == 1, 1.0, 0.0)
+        GX[r, :] = (PF[r, :] + once * (H[NL - 1, r, :].astype(F32) + out_bias(NL - 1))).astype(BF16)
+        guest_copy(i).start()
+
+    def guest_hop(t, dst, sem, arrive, to):
+        return rcopy(GX.at[t * SR:(t + 1) * SR], dst.at[GP1, t * SR:(t + 1) * SR], sem.at[t], arrive.at[GP1, t], tp=to)
+
+    def guest_to_hub(t):
+        return guest_hop(t, RA, gs2, ra_s, hub)
+
+    def guest_to_peer(t):
+        return guest_hop(t, RB, gs2, rb_s, peer)
+
+    def guest_to_leaf(t):
+        return guest_hop(t, RB, gs3, rc_s, leaf)
+
+    def parts(i):
+        return [(t, slice(t * SR, (t + 1) * SR)) for t in range(i * SUB, (i + 1) * SUB)]
+
+    def guest_in(i):
+        guest_copy(i).wait_recv()
+
+        @pl.when(is_end)
+        def _():
+            for t, r in parts(i):
+                guest_to_hub(t).start()
+
+    def guest_mid(i):
+        @pl.when(inner)
+        def _():
+            for t, r in parts(i):
+                guest_to_hub(t).wait_recv()
+                GX[r, :] = (GX[r, :].astype(F32) + RA[GP1, r, :].astype(F32)).astype(BF16)
+                guest_to_peer(t).start()
+
+    def guest_last(i):
+        @pl.when(inner)
+        def _():
+            for t, r in parts(i):
+                guest_to_peer(t).wait_recv()
+                guest_to_peer(t).wait_send()
+                GX[r, :] = (GX[r, :].astype(F32) + RB[GP1, r, :].astype(F32)).astype(BF16)
+                guest_to_leaf(t).start()
+
+    def guest_back(i):
+        @pl.when(is_end)
+        def _():
+            for t, r in parts(i):
+                guest_to_leaf(t).wait_recv()
+
+    def guest_out(act):
+        for role, src in ((is_end, RB.at[GP1]), (inner, GX)):
+            @pl.when(role)
+            def _():
+                dst = y.at[1, c]
+                act(lcopy(src, dst, ygs.at[0]), rcopy(src, dst, ygs.at[1], yr.at[s + CORES], pp=sib), rcopy(src, dst, ygs.at[2], yr.at[s + CORES], pp=s + CORES))
 
     def stats(hf):
         cen = hf - row_mean(hf)
@@ -584,7 +649,7 @@
         for o in range(1, NT):
             q = (z + o) % NT
             rcopy(GV.at[l], ZR.at[l, q], v1s.at[l, o - 1], v1r.at[l, q], tp=q).wait_recv()
-        tot = ZR[l, 0] + ZR[l, 1] + ZR[l, 2] + ZR[l, 3]
+        tot = sum(ZR[l, k] for k in range(NT))
         row = lax.broadcasted_iota(jnp.int32, (8, D), 0)
         GZ[l] = jnp.where(row < 4, tot, GV[l])
 
@@ -613,9 +678,7 @@
 
     def fwd_layer(l, carry):
         for i in range(NC):
-            @pl.when(l > 0)
-            def _():
-                ar_wait(l - 1, l, i)
+            ar_wait(l - 1, l, i, l)
 
             def handle(op, lag, u):
                 m = i - lag
@@ -626,13 +689,22 @@
                     else:
                         ar_last(p, p, p + 1, j, u)
                 if m >= 0:
-                    go(l, m)
+                    @pl.when(l * ys_ < NL - 1)
+                    def _():
+                        go(l, m)
                 else:
                     @pl.when(l > 0)
                     def _():
                         go(l - 1, m + NC)
             run(forward(l, i), FWD_AT, handle)
-            ar_send(l, i)
+
+            @pl.when(l * ys_ < NL - 1)
+            def _():
+                ar_send(l, i)
+
+            @pl.when(l * ys_ == NL - 1)
+            def _():
+                guest_send(i)
             if i == 1:
                 @pl.when(l == 0)
                 def _():
@@ -661,6 +733,7 @@
     y_sib = rcopy(H.at[NL], y.at[ys_, c], ys.at[1], yr.at[s], pp=sib)
     y_far = rcopy(H.at[NL], y.at[ys_, c], ys.at[2], yr.at[s], pp=oy + c)
     y_fwd = rcopy(y.at[1 - ys_, c], y.at[1 - ys_, c], ys.at[3], yr.at[oy + c], pp=sib)
+    y_own = rcopy(y.at[ys_, c], y.at[ys_, c], ys.at[2], yr.at[s], pp=sib)
 
     def y_arrived(q):
         rcopy(H.at[NL], y.at[q // CORES, q % CORES], ys.at[1], yr.at[q], pp=sib).wait_recv()
@@ -668,15 +741,17 @@
     def ri(l):
         return jnp.where(l == NL - 1, NL + 1, l + 1)
 
+    def pass_of(lb):
+        return NL - 1 + lb + (1 - ys_) * (1 + jnp.minimum(lb, 1))
+
     def bwd_layer(lb, carry):
         l = NL - 1 - lb
-        p = NL + lb
+        p = pass_of(lb)
+        before = pass_of(lb - 1)
         for n in range(NC):
             i = NC - 1 - n
 
-            @pl.when(lb > 0)
-            def _():
-                ar_wait(p - 1, l + 1, i)
+            ar_wait(before, l + 1, i, lb)
 
             def handle(op, lag, u):
                 m = n - lag
@@ -685,7 +760,7 @@
                     if op == 'mid':
                         ar_mid(q, j, u, True)
                     else:
-                        ar_last(q, ri(lq), lq, j, u)
+                        ar_last(q, ri(lq), lq, j, u, True)
                 if m >= 0:
                     @pl.when(l > 0)
                     def _():
@@ -693,16 +768,27 @@
                 else:
                     @pl.when(lb > 0)
                     def _():
-                        go(p - 1, l + 1, -1 - m)
-
-                    @pl.when(lb == 0)
+                        go(before, l + 1, -1 - m)
+
+                    @pl.when(lb == NL * ys_)
                     def _():
                         if op == 'mid':
                             ar_mid(NL - 1, m + NC, u)
                         else:
                             ar_last(NL - 1, NL - 1, NL, m + NC, u)
 
+            def guests(layer, what, j):
+                @pl.when(lb == layer + NL * ys_)
+                def _():
+                    what(j)
+
             def after(k):
+                if k == 0:
+                    guests(1, guest_in, i)
+                if k == 1:
+                    guests(1 if n else 2, guest_last, i + 1 if n else 0)
+                if k == NC:
+                    guests(1, guest_mid, i)
                 if k == 0 and n == 0:
                     @pl.when(lb > 0)
                     def _():
@@ -714,15 +800,23 @@
                         g1_copy(l, a).start()
             run(backward(l, ri(l), i, False), BWD_AT, handle, after)
 
+            @pl.when(lb == 2 + NL * ys_)
+            def _():
+                guest_back(i)
+
             @pl.when(l > 0)
             def _():
                 ar_send(p, i, True)
+            if n == NC - 1:
+                @pl.when(lb == 2 + NL * ys_)
+                def _():
+                    guest_out(lambda *copies: start_all(copies))
             if n == 1:
                 @pl.when(lb > 0)
                 def _():
                     vec_mid(l + 1)
             if n == 2:
-                @pl.when(lb == 0)
+                @pl.when(lb == NL * ys_)
                 def _():
                     for j in range(NC):
                         ar_wait(NL - 1, NL, j)
@@ -740,8 +834,13 @@
     lax.fori_loop(0, NL, bwd_layer, 0)
 
     grads_mid(0, ATT)
-    y_arrived(oy + c)
-    y_fwd.start()
+
+    @pl.when(ys_ == 1)
+    def _():
+        y_arrived(oy + c)
+        y_fwd.start()
+        y_arrived(s)
+        y_own.start()
     grads_last(1)
     vec_mid(0)
     grads_last(0)
@@ -749,8 +848,8 @@
     for o in range(1, NL):
         q = (s + o) % NL
         rcopy(GZ.at[0], PR.at[q], v2s.at[0], v2r.at[q], pp=q).wait_recv()
-    PRE[0:8, 0:D] = PR[0] + PR[1] + PR[2] + PR[3]
-    vout = lcopy(PRE.at[0:8, 0:D], ovec, osem.at[0])
+    PRE[:8, :D] = sum(PR[k] for k in range(NL))
+    vout = lcopy(PRE.at[:8, :D], ovec, osem.at[0])
     vout.start()
     for l in range(NL):
         for cp in v1_copies(l):
@@ -761,9 +860,33 @@
             v2_copy(l).wait_send()
     for a in range(NA):
         rcopy(G_OUT[a].at[g_half(a, 1 - c)], G_OUT[a].at[g_half(a, 1 - c)], g3s.at[a], g3r.at[a], pp=sib).wait_recv()
-    y_local.wait()
-    for cp in (y_sib, y_far, y_fwd):
-        cp.wait_send()
+
+    def out_done(local, *sent):
+        local.wait()
+        for cp in sent:
+            cp.wait_send()
+
+    @pl.when(ys_ == 0)
+    def _():
+        out_done(y_local, y_sib, y_far)
+        guest_out(out_done)
+
+        @pl.when(is_end)
+        def _():
+            for t in range(NC * SUB):
+                guest_to_hub(t).wait_send()
+
+        @pl.when(inner)
+        def _():
+            for t in range(NC * SUB):
+                guest_to_leaf(t).wait_send()
+
+    @pl.when(ys_ == 1)
+    def _():
+        y_fwd.wait_send()
+        y_own.wait_send()
+        for i in range(NC):
+            guest_copy(i).wait_send()
     y_arrived(sib)
     y_arrived(oy + 1 - c)
     for a in range(NA):
@@ -874,17 +997,18 @@
         *[vm(NL, 2, (i + 1) * C, C) for i in range(NC)],
         vm(NL, S, F), vm(NL + 1, S, F, dtype=F32),
         vm(CORES, S, D), vm(CORES, S, D), vm(S, D), vm(S + C, D, dtype=F32),
-        vm(CORES, 3 * E2, D, dtype=F32), vm(CORES, E2, D, dtype=F32), vm(CORES, D, F, dtype=F32), vm(CORES, F, D, dtype=F32),
-        vm(CORES, 3 * E, D), vm(CORES, E, D), vm(CORES, D // CORES, F), vm(CORES, F // CORES, D),
+        *[vm(CORES, *k, dtype=F32) for k in ((3 * E2, D), (E2, D), (D, F), (F, D))],
+        *[vm(CORES, *k) for k in ((3 * E, D), (E, D), (D // CORES, F), (F // CORES, D))],
         vm(S, E2, dtype=F32), vm(S, E2, dtype=F32),
-        vm(CORES, C + 8, E2, dtype=F32), vm(S, E2, dtype=F32), vm(S, E2, dtype=F32),
-        vm(NL, 8, D, dtype=F32), vm(NL, NT, 8, D, dtype=F32), vm(NL, 8, D, dtype=F32), vm(NL, 8, D, dtype=F32),
+        vm(CORES, C + 8, E2, dtype=F32),
+        *[vm(*k, 8, D, dtype=F32) for k in ((NL,), (NL, NT), (NL,), (NL,))],
         vm(C, D), vm(C, D), vm(C, max(D, F), dtype=F32), vm(C, F), vm(S, C), vm(S, C, dtype=F32),
-        *[vm(1, D, dtype=F32)] * 4, vm(1, D), vm(1, D), vm(1, F), vm(3, 2, E),
+        *[vm(1, D, dtype=F32)] * 4, vm(1, D), vm(1, D), vm(1, F), vm(3, CORES, E), vm(S, D),
         dma((NA,)), dma((NA + 1,)), dma((CORES, NA + 1)), dma((NL, 2 * NA + 1)), dma((CORES, NA)), dma((3, NA)), dma((NA, 4)), dma((CORES,)), dma((1,)),
         dma((NC * SUB,)), dma((NC * SUB,)), dma((CORES, NC * SUB)), dma((CORES, NC * SUB)), dma((CORES, NC * SUB)),
         dma((NL,)), dma((NL,)), dma((NA,)), dma((CORES, NA)), dma((CORES, NA)), dma((CORES, NA)), dma((CORES, NA)), dma((NA,)),
         dma((NL, NT - 1)), dma((NL, NT)), dma((NL,)), dma((NL,)), dma((1,)), dma((8,)),
+        dma((NC,)), dma((NC,)), dma((NC * SUB,)), dma((NC * SUB,)), dma((3,)),
     ]
     return pl.pallas_call(
         functools.partial(body, dims),

time: 231 us -> 229 us (level)
    pallas_call x1, Pallas kernels: 224 us -> 222 us  [group_step(): pl.pallas_call(functools.partial(body, dims), out_shape=out_shape, in_spe...]
where the time goes in v11:
time: 229 us
  Pallas kernels  228 us (100%)
    pallas_call x1, Pallas kernels, group_step(): pl.pallas_call(functools.partial(body, dims), out_shape=out_shape, in_spe...  222 us
    pallas_call x1, Pallas kernels, finish_step(): pl.pallas_call(finish, out_shape=outs, in_specs=[hbm] * 6, out_specs=[hbm...  5.89 us

profile of v11, /device:TPU:0, one launch (start us, length us, event | category | flops | bytes accessed | tf_op | source)
XLA Modules:
  0.0 228.6 jit_solution(1337090376514304429)
XLA Ops:
  0.7 221.9 %neox_group.1 = (bf16[2,2,1024,512]{3,2,1,0:T(8,128)(2,1)}, f32[384,512]{1,0:T(8,128)}, f32[128,512]{1,0:T(8,128)}, f32[512,512]{1,0:T(8,128)}, f32[512,512]{1,0:T(8,128)}, /*index=5*/f32[8,512]{1,0:T(8,128)}) custom-call(bf16[2,2,1024,512]{3,2,1,0:T(8,128)(2,1)} %x.1, f32[2,2,1024,512]{3,2,1,0:T(8,128)} %g.1, bf16[384,512]{1,0:T(8,128)(2,1)} %bitcast.24, ...), custom_call_target="tpu_custom_call" | custom-call | tf_op jit(solution)/shard_map/neox_group/pallas_call | solution.py:1013
  222.6 5.9 %neox_out.1 = (bf16[2,2,1024,512]{3,2,1,0:T(8,128)(2,1)}, f32[384,512]{1,0:T(8,128)}, f32[128,512]{1,0:T(8,128)}, f32[512,512]{1,0:T(8,128)}, f32[512,512]{1,0:T...) custom-call(bf16[2,2,1024,512]{3,2,1,0:T(8,128)(2,1)} %get-tuple-ele, ...), custom_call_target="tpu_custom_call" | custom-call | tf_op jit(solution)/shard_map/neox_out/pallas_call | solution.py:966

commit v12 on v11

--- a/solution.py
+++ b/solution.py
@@ -43,6 +43,10 @@
     return lax.dot_general(a, b, (((0,), (0,)), ((), ())), preferred_element_type=F32)
 
 
+def loop(n, step, init, unroll=False):
+    return lax.fori_loop(0, n, step, init, unroll=unroll)
+
+
 def col_sum(v):
     return jnp.sum(v, axis=0, keepdims=True)
 
@@ -71,7 +75,7 @@
          WQ, WO, WU, WD, VEC, H, Q, K, V, KT, VT, CTX, P0, P1, P2, P3, HID, GP, RA, RB, PS, PF,
          GQ, GO, GU, GD, R2Q, R2O, R2U, R2D, DK, DV, TAB, GV, ZR, GZ, PR,
          AS, MS, PRE, DPB, DS, ST, N0, N1, N2, N3, N4, N5, N6, BQ, GX,
-         wl, ws, wy, wr, wf, w0s, w0r, xs, gs, sab, sc, ra_s, rb_s, rc_s, ys, yr, g1s, g1r, g2s, g2r, g3s, g3r, v1s, v1r, v2s, v2r, osem, ns, gxs, gxr, gs2, gs3, ygs):
+         wl, ws, wy, wr, wf, w0s, w0r, xs, gs, sab, sc, ra_s, rb_s, rc_s, ys, yr, g1s, g1r, g2s, g2r, g3s, g3r, v1s, v1r, v2s, v2r, osem, ns, gxs, gxr, gs2, gs3, ygs, ygr):
     S, D, E, C, F = dims
     E2 = 2 * E
     SR = C // SUB
@@ -306,6 +310,7 @@
                 back_copy(p, di, t).wait_recv()
 
     GP1 = NL % 3
+    HOME = NC // CORES
 
     def guest_copy(i):
         part = GX.at[i * C:(i + 1) * C]
@@ -364,11 +369,15 @@
                 guest_to_leaf(t).wait_recv()
 
     def guest_out(act):
-        for role, src in ((is_end, RB.at[GP1]), (inner, GX)):
+        low = slice(HOME * C, S)
+        for role, src in ((is_end, RB.at[GP1, low]), (inner, GX.at[low])):
             @pl.when(role)
             def _():
-                dst = y.at[1, c]
-                act(lcopy(src, dst, ygs.at[0]), rcopy(src, dst, ygs.at[1], yr.at[s + CORES], pp=sib), rcopy(src, dst, ygs.at[2], yr.at[s + CORES], pp=s + CORES))
+                dst = y.at[1, c, low]
+                act(lcopy(src, dst, ygs.at[0]), rcopy(src, dst, ygs.at[1], ygr.at[c], pp=sib), rcopy(src, dst, ygs.at[2], ygr.at[c], pp=s + CORES))
+
+    def guest_home(q):
+        return rcopy(y.at[1, q, HOME * C:S], y.at[1, q, HOME * C:S], ygs.at[0], ygr.at[q], pp=sib)
 
     def stats(hf):
         cen = hf - row_mean(hf)
@@ -387,7 +396,7 @@
             AS[rows(b * LB, LB), :] = (xhat * g1 + b1).astype(BF16)
             MS[rows(b * LB, LB), :] = (xhat * g2 + b2).astype(BF16)
             return carry
-        lax.fori_loop(0, C // LB, step, 0, unroll=True)
+        loop(C // LB, step, 0, unroll=True)
 
     def by_kind():
         return [(h * 3 + k) * E for k in range(3) for h in range(CORES)]
@@ -427,20 +436,20 @@
 
             def top(b, m):
                 return jnp.maximum(m, jnp.max(ST[rows(b * RBK, RBK), :].reshape(RBK // 8, 8, C), axis=0))
-            m = jnp.max(lax.fori_loop(0, r1 // RBK, top, jnp.full((8, C), -3e38, F32), unroll=True), axis=0, keepdims=True)
+            m = jnp.max(loop(r1 // RBK, top, jnp.full((8, C), -3e38, F32), unroll=True), axis=0, keepdims=True)
             mc = m * c1
 
             def expo(b, tot):
                 e = jnp.exp2(ST[rows(b * RBK, RBK), :] * c1 - mc)
                 ST[rows(b * RBK, RBK), :] = e
                 return tot + fold(e)
-            tot = col_sum(lax.fori_loop(0, r1 // RBK, expo, jnp.zeros((8, C), F32), unroll=True))
+            tot = col_sum(loop(r1 // RBK, expo, jnp.zeros((8, C), F32), unroll=True))
             inv = 1.0 / tot
 
             def put(b, carry):
                 PX[i][l, h, rows(b * RBK, RBK), :] = (ST[rows(b * RBK, RBK), :] * inv).astype(BF16)
                 return carry
-            lax.fori_loop(0, r1 // RBK, put, 0, unroll=True)
+            loop(r1 // RBK, put, 0, unroll=True)
             outs.append(nn(VT[:, :r1], PX[i][l, h]))
             if h == 0:
                 yield
@@ -467,7 +476,7 @@
             HID[l, rows(r0 + b * GB, GB), :] = (u * cdf).astype(BF16)
             GP[l, rows(r0 + b * GB, GB), :] = cdf + u * pdf
             return carry
-        lax.fori_loop(0, C // GB, act, 0, unroll=True)
+        loop(C // GB, act, 0, unroll=True)
         PF[r0:r1, :] += nn(HID[l, r0:r1, :], WD[l])
         yield
 
@@ -495,7 +504,7 @@
             d = PRE[rows(b * GB, GB), :] * GP[l, rows(r0 + b * GB, GB), :]
             DPB[rows(b * GB, GB), :] = d.astype(BF16)
             return tot + fold(d)
-        dbu = lax.fori_loop(0, C // GB, act, jnp.zeros((8, F), F32), unroll=True)
+        dbu = loop(C // GB, act, jnp.zeros((8, F), F32), unroll=True)
         acc_row(5, col_sum(dbu))
         acc(GD, tn(HID[l, r0:r1, :], dy))
         yield
@@ -523,7 +532,7 @@
                 pr = PX[i][l, h, rows(b * RBK, RBK), :].astype(F32)
                 DS[rows(b * RBK, RBK), :] = (pr * (ST[rows(b * RBK, RBK), :] - drow)).astype(BF16)
                 return carry
-            lax.fori_loop(0, r1 // RBK, sub, 0, unroll=True)
+            loop(r1 // RBK, sub, 0, unroll=True)
             dk = nn(DS[:r1, :], qm)
             dv = nn(PX[i][l, h], dcm)
             if first and h == 0:
@@ -564,7 +573,7 @@
                 PF[rows(f0 + b * LB, LB), :] = rstd * (dx - m1 - xhat * m2)
             terms = (da * xhat, da, dm * xhat, dm)
             return tuple(a + fold(v) for a, v in zip(tots, terms))
-        tots = lax.fori_loop(0, C // LB, lnb, tuple(jnp.zeros((8, D), F32) for _ in range(NA)), unroll=True)
+        tots = loop(C // LB, lnb, tuple(jnp.zeros((8, D), F32) for _ in range(NA)), unroll=True)
         for k in range(NA):
             acc_row(k, col_sum(tots[k]))
         yield
@@ -601,7 +610,7 @@
                 GP[l + 1, rr, :G_COLS[a]] = tot
                 HID[l, rr, :G_COLS[a]] = tot.astype(BF16)
                 return carry
-            lax.fori_loop(0, n // GR, add, 0)
+            loop(n // GR, add, 0)
 
             @pl.when(l // CORES != ys_)
             def _():
@@ -610,14 +619,14 @@
     def grads_last(l):
         @pl.when(l // CORES == ys_)
         def _():
-            for a in MLP + ATT:
+            for a in MLP[::-1] + ATT:
                 g2_copy(l, a).wait_recv()
 
                 def add(b, carry):
                     rr = rows(R1_OFF[a] + b * GR, GR)
                     GP[l + 1, rr, :G_COLS[a]] += R2[a][l % CORES, rows(b * GR, GR), :].astype(F32)
                     return carry
-                lax.fori_loop(0, G_HALF[a] // GR, add, 0)
+                loop(G_HALF[a] // GR, add, 0)
 
                 @pl.when(l == s)
                 def _():
@@ -688,23 +697,28 @@
                         ar_mid(p, j, u)
                     else:
                         ar_last(p, p, p + 1, j, u)
-                if m >= 0:
+                if m >= HOME:
                     @pl.when(l * ys_ < NL - 1)
                     def _():
                         go(l, m)
+                elif m >= 0:
+                    go(l, m)
                 else:
                     @pl.when(l > 0)
                     def _():
                         go(l - 1, m + NC)
             run(forward(l, i), FWD_AT, handle)
 
-            @pl.when(l * ys_ < NL - 1)
-            def _():
+            if i < HOME:
                 ar_send(l, i)
-
-            @pl.when(l * ys_ == NL - 1)
-            def _():
-                guest_send(i)
+            else:
+                @pl.when(l * ys_ < NL - 1)
+                def _():
+                    ar_send(l, i)
+
+                @pl.when(l * ys_ == NL - 1)
+                def _():
+                    guest_send(i)
             if i == 1:
                 @pl.when(l == 0)
                 def _():
@@ -727,22 +741,31 @@
                 def _():
                     settle(l + 1, FIRST, True)
         return carry
-    lax.fori_loop(0, NL, fwd_layer, 0)
-
-    y_local = lcopy(H.at[NL], y.at[ys_, c], ys.at[0])
-    y_sib = rcopy(H.at[NL], y.at[ys_, c], ys.at[1], yr.at[s], pp=sib)
-    y_far = rcopy(H.at[NL], y.at[ys_, c], ys.at[2], yr.at[s], pp=oy + c)
-    y_fwd = rcopy(y.at[1 - ys_, c], y.at[1 - ys_, c], ys.at[3], yr.at[oy + c], pp=sib)
-    y_own = rcopy(y.at[ys_, c], y.at[ys_, c], ys.at[2], yr.at[s], pp=sib)
-
-    def y_arrived(q):
-        rcopy(H.at[NL], y.at[q // CORES, q % CORES], ys.at[1], yr.at[q], pp=sib).wait_recv()
+    loop(NL, fwd_layer, 0)
+
+    def y_copies_of(q, n):
+        src, dst, got = H.at[NL, :n], y.at[q // CORES, c, :n], yr.at[q]
+        return lcopy(src, dst, ys.at[0]), rcopy(src, dst, ys.at[1], got, pp=sib), rcopy(src, dst, ys.at[2], got, pp=oy + c)
+
+    def y_pass(q, n):
+        part = y.at[q // CORES, c, :n]
+        return rcopy(part, part, ys.at[3], yr.at[q], pp=sib)
+
+    def y_arrived(q, n):
+        part = y.at[q // CORES, q % CORES, :n]
+        rcopy(part, part, ys.at[1], yr.at[q], pp=sib).wait_recv()
+
+    def each_row(do):
+        for row, n, other in ((0, S, HOME * C), (1, HOME * C, S)):
+            @pl.when(ys_ == row)
+            def _():
+                do(row, n, other)
 
     def ri(l):
         return jnp.where(l == NL - 1, NL + 1, l + 1)
 
     def pass_of(lb):
-        return NL - 1 + lb + (1 - ys_) * (1 + jnp.minimum(lb, 1))
+        return NL + lb + (1 - ys_) * jnp.minimum(lb, 1)
 
     def bwd_layer(lb, carry):
         l = NL - 1 - lb
@@ -783,11 +806,11 @@
                     what(j)
 
             def after(k):
-                if k == 0:
+                if k == 0 and i >= HOME:
                     guests(1, guest_in, i)
-                if k == 1:
-                    guests(1 if n else 2, guest_last, i + 1 if n else 0)
-                if k == NC:
+                if k == 1 and NC > i + 1 >= HOME:
+                    guests(1, guest_last, i + 1)
+                if k == NC and i >= HOME:
                     guests(1, guest_mid, i)
                 if k == 0 and n == 0:
                     @pl.when(lb > 0)
@@ -795,14 +818,18 @@
                         grads_mid(l + 1, ATT)
                         for a in ALL:
                             g1_copy(l + 1, a).wait_send()
-                if n == NC - 1 and k == 1:
-                    for a in MLP:
-                        g1_copy(l, a).start()
+                if n == NC - 1 and k < 2:
+                    g1_copy(l, MLP[1 - k]).start()
+                if n == NC - 1 and k in (3, 4):
+                    @pl.when(l == 0)
+                    def _():
+                        grads_mid(l, (MLP[4 - k],))
             run(backward(l, ri(l), i, False), BWD_AT, handle, after)
 
-            @pl.when(lb == 2 + NL * ys_)
-            def _():
-                guest_back(i)
+            if i >= HOME:
+                @pl.when(lb == 2 + NL * ys_)
+                def _():
+                    guest_back(i)
 
             @pl.when(l > 0)
             def _():
@@ -816,11 +843,13 @@
                 def _():
                     vec_mid(l + 1)
             if n == 2:
-                @pl.when(lb == NL * ys_)
-                def _():
-                    for j in range(NC):
-                        ar_wait(NL - 1, NL, j)
-                    start_all((y_local, y_sib, y_far))
+                @pl.when(lb == 0)
+                def _():
+                    def out(row, n, other):
+                        for j in range(n // C):
+                            ar_wait(NL - 1, NL, j)
+                        start_all(y_copies_of(CORES * row + c, n))
+                    each_row(out)
 
                 @pl.when(lb > 1)
                 def _():
@@ -829,18 +858,22 @@
         for a in ATT:
             g1_copy(l, a).start()
         start_all(v1_copies(l))
-        grads_mid(l, MLP)
+
+        @pl.when(l > 0)
+        def _():
+            grads_mid(l, MLP)
         return carry
-    lax.fori_loop(0, NL, bwd_layer, 0)
+    loop(NL, bwd_layer, 0)
 
     grads_mid(0, ATT)
 
-    @pl.when(ys_ == 1)
-    def _():
-        y_arrived(oy + c)
-        y_fwd.start()
-        y_arrived(s)
-        y_own.start()
+    def pass_on(row, n, other):
+        y_arrived(CORES * (1 - row) + c, other)
+        y_pass(CORES * (1 - row) + c, other).start()
+        if row:
+            guest_home(c).wait_recv()
+            guest_home(c).start()
+    each_row(pass_on)
     grads_last(1)
     vec_mid(0)
     grads_last(0)
@@ -866,29 +899,33 @@
         for cp in sent:
             cp.wait_send()
 
+    def all_out(row, n, other):
+        out_done(*y_copies_of(CORES * row + c, n))
+        y_pass(CORES * (1 - row) + c, other).wait_send()
+        y_arrived(CORES * row + 1 - c, n)
+        y_arrived(CORES * (1 - row) + 1 - c, other)
+        guest_home(1 - c).wait_recv()
+    each_row(all_out)
+
     @pl.when(ys_ == 0)
     def _():
-        out_done(y_local, y_sib, y_far)
         guest_out(out_done)
 
         @pl.when(is_end)
         def _():
-            for t in range(NC * SUB):
+            for t in range(HOME * SUB, NC * SUB):
                 guest_to_hub(t).wait_send()
 
         @pl.when(inner)
         def _():
-            for t in range(NC * SUB):
+            for t in range(HOME * SUB, NC * SUB):
                 guest_to_leaf(t).wait_send()
 
     @pl.when(ys_ == 1)
     def _():
-        y_fwd.wait_send()
-        y_own.wait_send()
-        for i in range(NC):
+        guest_home(c).wait_send()
+        for i in range(HOME, NC):
             guest_copy(i).wait_send()
-    y_arrived(sib)
-    y_arrived(oy + 1 - c)
     for a in range(NA):
         g1_copy(0, a).wait_send()
     for l in range(NL):
@@ -1008,7 +1045,7 @@
         dma((NC * SUB,)), dma((NC * SUB,)), dma((CORES, NC * SUB)), dma((CORES, NC * SUB)), dma((CORES, NC * SUB)),
         dma((NL,)), dma((NL,)), dma((NA,)), dma((CORES, NA)), dma((CORES, NA)), dma((CORES, NA)), dma((CORES, NA)), dma((NA,)),
         dma((NL, NT - 1)), dma((NL, NT)), dma((NL,)), dma((NL,)), dma((1,)), dma((8,)),
-        dma((NC,)), dma((NC,)), dma((NC * SUB,)), dma((NC * SUB,)), dma((3,)),
+        dma((NC,)), dma((NC,)), dma((NC * SUB,)), dma((NC * SUB,)), dma((3,)), dma((CORES,)),
     ]
     return pl.pallas_call(
         functools.partial(body, dims),

time: 229 us -> 228 us (level)
  no operation moved by 1% of the time
where the time goes in v12:
time: 228 us
  Pallas kernels  227 us (100%)
    pallas_call x1, Pallas kernels, group_step(): pl.pallas_call(functools.partial(body, dims), out_shape=out_shape, in_spe...  221 us
    pallas_call x1, Pallas kernels, finish_step(): pl.pallas_call(finish, out_shape=outs, in_specs=[hbm] * 6, out_specs=[hbm...  5.89 us

profile of v12, /device:TPU:0, one launch (start us, length us, event | category | flops | bytes accessed | tf_op | source)
XLA Modules:
  0.0 227.8 jit_solution(11506764968829147087)
XLA Ops:
  0.7 221.1 %neox_group.1 = (bf16[2,2,1024,512]{3,2,1,0:T(8,128)(2,1)}, f32[384,512]{1,0:T(8,128)}, f32[128,512]{1,0:T(8,128)}, f32[512,512]{1,0:T(8,128)}, f32[512,512]{1,0:T(8,128)}, /*index=5*/f32[8,512]{1,0:T(8,128)}) custom-call(bf16[2,2,1024,512]{3,2,1,0:T(8,128)(2,1)} %x.1, f32[2,2,1024,512]{3,2,1,0:T(8,128)} %g.1, bf16[384,512]{1,0:T(8,128)(2,1)} %bitcast.24, ...), custom_call_target="tpu_custom_call" | custom-call | tf_op jit(solution)/shard_map/neox_group/pallas_call | solution.py:1050
  221.7 5.9 %neox_out.1 = (bf16[2,2,1024,512]{3,2,1,0:T(8,128)(2,1)}, f32[384,512]{1,0:T(8,128)}, f32[128,512]{1,0:T(8,128)}, f32[512,512]{1,0:T(8,128)}, f32[512,512]{1,0:T...) custom-call(bf16[2,2,1024,512]{3,2,1,0:T(8,128)(2,1)} %get-tuple-ele, ...), custom_call_target="tpu_custom_call" | custom-call | tf_op jit(solution)/shard_map/neox_out/pallas_call | solution.py:1003

commit v13 on v12

--- a/solution.py
+++ b/solution.py
@@ -23,9 +23,9 @@
 NC = 4
 NA = 4
 CORES = 2
-SUB = 2
-FWD_AT = {0: (('mid', 1, 0), ('last', 2, 0)), 2: (('mid', 1, 1), ('last', 2, 1))}
-BWD_AT = {0: (('last', 2, 0),), 1: (('mid', 1, 0),), 3: (('last', 2, 1),), 4: (('mid', 1, 1),)}
+SUB = 4
+FWD_AT = {k: (('mid', 1, k), ('last', 2, k)) for k in range(SUB)}
+BWD_AT = {k: (('last', 2, k),) * (k < SUB) + (('mid', 1, k - 1),) * (k > 0) for k in range(SUB + 1)}
 LOG2E = 1.4426950408889634
 RSQRT2 = 0.7071067811865476
 INV_SQRT_2PI = 0.3989422804014327

time: 228 us -> 227 us (level)
  no operation moved by 1% of the time
where the time goes in v13:
time: 227 us
  Pallas kernels  226 us (100%)
    pallas_call x1, Pallas kernels, group_step(): pl.pallas_call(functools.partial(body, dims), out_shape=out_shape, in_spe...  221 us
    pallas_call x1, Pallas kernels, finish_step(): pl.pallas_call(finish, out_shape=outs, in_specs=[hbm] * 6, out_specs=[hbm...  5.89 us

profile of v13, /device:TPU:0, one launch (start us, length us, event | category | flops | bytes accessed | tf_op | source)
XLA Modules:
  0.0 227.3 jit_solution(2642541013395008810)
XLA Ops:
  0.7 220.5 %neox_group.1 = (bf16[2,2,1024,512]{3,2,1,0:T(8,128)(2,1)}, f32[384,512]{1,0:T(8,128)}, f32[128,512]{1,0:T(8,128)}, f32[512,512]{1,0:T(8,128)}, f32[512,512]{1,0:T(8,128)}, /*index=5*/f32[8,512]{1,0:T(8,128)}) custom-call(bf16[2,2,1024,512]{3,2,1,0:T(8,128)(2,1)} %x.1, f32[2,2,1024,512]{3,2,1,0:T(8,128)} %g.1, bf16[384,512]{1,0:T(8,128)(2,1)} %bitcast.24, ...), custom_call_target="tpu_custom_call" | custom-call | tf_op jit(solution)/shard_map/neox_group/pallas_call | solution.py:1050
  221.2 5.9 %neox_out.1 = (bf16[2,2,1024,512]{3,2,1,0:T(8,128)(2,1)}, f32[384,512]{1,0:T(8,128)}, f32[128,512]{1,0:T(8,128)}, f32[512,512]{1,0:T(8,128)}, f32[512,512]{1,0:T...) custom-call(bf16[2,2,1024,512]{3,2,1,0:T(8,128)(2,1)} %get-tuple-ele, ...), custom_call_target="tpu_custom_call" | custom-call | tf_op jit(solution)/shard_map/neox_out/pallas_call | solution.py:1003

commit v14 on v13

--- a/solution.py
+++ b/solution.py
@@ -821,7 +821,7 @@
                 if n == NC - 1 and k < 2:
                     g1_copy(l, MLP[1 - k]).start()
                 if n == NC - 1 and k in (3, 4):
-                    @pl.when(l == 0)
+                    @pl.when(l < 5 - k)
                     def _():
                         grads_mid(l, (MLP[4 - k],))
             run(backward(l, ri(l), i, False), BWD_AT, handle, after)
@@ -859,9 +859,13 @@
             g1_copy(l, a).start()
         start_all(v1_copies(l))
 
-        @pl.when(l > 0)
+        @pl.when(l > 1)
         def _():
             grads_mid(l, MLP)
+
+        @pl.when(l == 1)
+        def _():
+            grads_mid(l, MLP[:1])
         return carry
     loop(NL, bwd_layer, 0)
 

time: 227 us -> 227 us (level)
  no operation moved by 1% of the time
where the time goes in v14:
time: 227 us
  Pallas kernels  226 us (100%)
    pallas_call x1, Pallas kernels, group_step(): pl.pallas_call(functools.partial(body, dims), out_shape=out_shape, in_spe...  221 us
    pallas_call x1, Pallas kernels, finish_step(): pl.pallas_call(finish, out_shape=outs, in_specs=[hbm] * 6, out_specs=[hbm...  5.89 us

profile of v14, /device:TPU:0, one launch (start us, length us, event | category | flops | bytes accessed | tf_op | source)
XLA Modules:
  0.0 227.3 jit_solution(10767165225355076280)
XLA Ops:
  0.7 220.5 %neox_group.1 = (bf16[2,2,1024,512]{3,2,1,0:T(8,128)(2,1)}, f32[384,512]{1,0:T(8,128)}, f32[128,512]{1,0:T(8,128)}, f32[512,512]{1,0:T(8,128)}, f32[512,512]{1,0:T(8,128)}, /*index=5*/f32[8,512]{1,0:T(8,128)}) custom-call(bf16[2,2,1024,512]{3,2,1,0:T(8,128)(2,1)} %x.1, f32[2,2,1024,512]{3,2,1,0:T(8,128)} %g.1, bf16[384,512]{1,0:T(8,128)(2,1)} %bitcast.24, ...), custom_call_target="tpu_custom_call" | custom-call | tf_op jit(solution)/shard_map/neox_group/pallas_call | solution.py:1054
  221.2 5.9 %neox_out.1 = (bf16[2,2,1024,512]{3,2,1,0:T(8,128)(2,1)}, f32[384,512]{1,0:T(8,128)}, f32[128,512]{1,0:T(8,128)}, f32[512,512]{1,0:T(8,128)}, f32[512,512]{1,0:T...) custom-call(bf16[2,2,1024,512]{3,2,1,0:T(8,128)(2,1)} %get-tuple-ele, ...), custom_call_target="tpu_custom_call" | custom-call | tf_op jit(solution)/shard_map/neox_out/pallas_call | solution.py:1007

commit v15 on v13

--- a/solution.py
+++ b/solution.py
@@ -24,7 +24,7 @@
 NA = 4
 CORES = 2
 SUB = 4
-FWD_AT = {k: (('mid', 1, k), ('last', 2, k)) for k in range(SUB)}
+FWD_AT = {k: (('mid', 1, k // 2), ('last', 2, k // 2)) for k in (0, 2)}
 BWD_AT = {k: (('last', 2, k),) * (k < SUB) + (('mid', 1, k - 1),) * (k > 0) for k in range(SUB + 1)}
 LOG2E = 1.4426950408889634
 RSQRT2 = 0.7071067811865476
@@ -75,7 +75,7 @@
          WQ, WO, WU, WD, VEC, H, Q, K, V, KT, VT, CTX, P0, P1, P2, P3, HID, GP, RA, RB, PS, PF,
          GQ, GO, GU, GD, R2Q, R2O, R2U, R2D, DK, DV, TAB, GV, ZR, GZ, PR,
          AS, MS, PRE, DPB, DS, ST, N0, N1, N2, N3, N4, N5, N6, BQ, GX,
-         wl, ws, wy, wr, wf, w0s, w0r, xs, gs, sab, sc, ra_s, rb_s, rc_s, ys, yr, g1s, g1r, g2s, g2r, g3s, g3r, v1s, v1r, v2s, v2r, osem, ns, gxs, gxr, gs2, gs3, ygs, ygr):
+         fab, fc, fa_s, fb_s, fc_s, wl, ws, wy, wr, wf, w0s, w0r, xs, gs, sab, sc, ra_s, rb_s, rc_s, ys, yr, g1s, g1r, g2s, g2r, g3s, g3r, v1s, v1r, v2s, v2r, osem, ns, gxs, gxr, gs2, gs3, ygs, ygr):
     S, D, E, C, F = dims
     E2 = 2 * E
     SR = C // SUB
@@ -248,66 +248,85 @@
         cs, sa, sb = t
         return v * cs + pltpu.roll(v * sa, rot_half, 1) + pltpu.roll(v * sb, E2 - rot_half, 1)
 
-    def end_copy(p, t):
-        return rcopy(PS.at[t * SR:(t + 1) * SR], RA.at[p % CORES, t * SR:(t + 1) * SR], sab.at[t], ra_s.at[p % CORES, t], tp=hub)
-
-    def peer_copy(p, t):
-        return rcopy(PS.at[t * SR:(t + 1) * SR], RB.at[p % CORES, t * SR:(t + 1) * SR], sab.at[t], rb_s.at[p % CORES, t], tp=peer)
-
-    def back_copy(p, di, t):
-        return rcopy(H.at[di, t * SR:(t + 1) * SR], H.at[di, t * SR:(t + 1) * SR], sc.at[t], rc_s.at[p % CORES, t], tp=leaf)
+    WIDE = SUB // CORES
+    SEMS = {1: (sab, sc, ra_s, rb_s, rc_s), WIDE: (fab, fc, fa_s, fb_s, fc_s)}
+
+    def end_copy(p, t, w=1):
+        r = slice(t * SR, (t + w) * SR)
+        return rcopy(PS.at[r], RA.at[p % CORES, r], SEMS[w][0].at[t], SEMS[w][2].at[p % CORES, t], tp=hub)
+
+    def peer_copy(p, t, w=1):
+        r = slice(t * SR, (t + w) * SR)
+        return rcopy(PS.at[r], RB.at[p % CORES, r], SEMS[w][0].at[t], SEMS[w][3].at[p % CORES, t], tp=peer)
+
+    def back_copy(p, di, t, w=1):
+        r = slice(t * SR, (t + w) * SR)
+        return rcopy(H.at[di, r], H.at[di, r], SEMS[w][1].at[t], SEMS[w][4].at[p % CORES, t], tp=leaf)
+
+    def sent_before(copy, p, t, w):
+        if w > 1:
+            @pl.when(p > 0)
+            def _():
+                copy(p, t, w).wait_send()
+        else:
+            @pl.when(p > NL)
+            def _():
+                copy(p, t).wait_send()
+            if t % WIDE == 0:
+                @pl.when(p == NL)
+                def _():
+                    copy(p, t, WIDE).wait_send()
 
     def pf_row(i, back):
         return (NC if back and i == NC - 1 else i) * C
 
     def ar_send(p, i, back=False):
+        w = 1 if back else WIDE
+
         @pl.when(is_end)
         def _():
-            for t in range(i * SUB, (i + 1) * SUB):
-                @pl.when(p > 0)
-                def _():
-                    end_copy(p, t).wait_send()
+            for t in range(i * SUB, (i + 1) * SUB, w):
+                sent_before(end_copy, p, t, w)
                 f0 = pf_row(i, back) + (t - i * SUB) * SR
-                PS[t * SR:(t + 1) * SR, :] = PF[f0:f0 + SR, :].astype(BF16)
-                end_copy(p, t).start()
+                PS[t * SR:(t + w) * SR, :] = PF[f0:f0 + w * SR, :].astype(BF16)
+                end_copy(p, t, w).start()
 
     def out_bias(l):
         return VEC[l, 4:5, :] + VEC[l, 5:6, :]
 
     def ar_mid(p, i, u, back=False):
-        t = i * SUB + u
-        r = slice(t * SR, (t + 1) * SR)
-        f0 = pf_row(i, back) + u * SR
+        w = 1 if back else WIDE
+        t = i * SUB + u * w
+        r = slice(t * SR, (t + w) * SR)
+        f0 = pf_row(i, back) + u * w * SR
 
         @pl.when(inner)
         def _():
-            end_copy(p, t).wait_recv()
-            @pl.when(p > 0)
-            def _():
-                peer_copy(p, t).wait_send()
-            PS[r, :] = (PF[f0:f0 + SR, :] + RA[p % CORES, r, :].astype(F32)).astype(BF16)
-            peer_copy(p, t).start()
+            end_copy(p, t, w).wait_recv()
+            sent_before(peer_copy, p, t, w)
+            PS[r, :] = (PF[f0:f0 + w * SR, :] + RA[p % CORES, r, :].astype(F32)).astype(BF16)
+            peer_copy(p, t, w).start()
 
     def ar_last(p, ri, di, i, u, back=False):
-        t = i * SUB + u
-        r = slice(t * SR, (t + 1) * SR)
+        w = 1 if back else WIDE
+        t = i * SUB + u * w
+        r = slice(t * SR, (t + w) * SR)
 
         @pl.when(inner)
         def _():
-            peer_copy(p, t).wait_recv()
-            @pl.when(p > 0)
-            def _():
-                back_copy(p, di, t).wait_send()
+            peer_copy(p, t, w).wait_recv()
+
+            sent_before(lambda p, t, w=1: back_copy(p, di, t, w), p, t, w)
             both = PS[r, :].astype(F32) + RB[p % CORES, r, :].astype(F32)
             own = H[ri, r, :].astype(F32)
             H[di, r, :] = (own + both if back else own + both + out_bias(p)).astype(BF16)
-            back_copy(p, di, t).start()
-
-    def ar_wait(p, di, i, on=1):
+            back_copy(p, di, t, w).start()
+
+    def ar_wait(p, di, i, w, on=1):
         @pl.when(on * edge > 0)
         def _():
-            for t in range(i * SUB, (i + 1) * SUB):
-                back_copy(p, di, t).wait_recv()
+            for t in range(i * SUB, (i + 1) * SUB, w):
+                back_copy(p, di, t, w).wait_recv()
 
     GP1 = NL % 3
     HOME = NC // CORES
@@ -687,7 +706,7 @@
 
     def fwd_layer(l, carry):
         for i in range(NC):
-            ar_wait(l - 1, l, i, l)
+            ar_wait(l - 1, l, i, WIDE, l)
 
             def handle(op, lag, u):
                 m = i - lag
@@ -774,7 +793,7 @@
         for n in range(NC):
             i = NC - 1 - n
 
-            ar_wait(before, l + 1, i, lb)
+            ar_wait(before, l + 1, i, 1, lb)
 
             def handle(op, lag, u):
                 m = n - lag
@@ -793,12 +812,13 @@
                     def _():
                         go(before, l + 1, -1 - m)
 
-                    @pl.when(lb == NL * ys_)
-                    def _():
-                        if op == 'mid':
-                            ar_mid(NL - 1, m + NC, u)
-                        else:
-                            ar_last(NL - 1, NL - 1, NL, m + NC, u)
+                    if u % WIDE == 0:
+                        @pl.when(lb == NL * ys_)
+                        def _():
+                            if op == 'mid':
+                                ar_mid(NL - 1, m + NC, u // WIDE)
+                            else:
+                                ar_last(NL - 1, NL - 1, NL, m + NC, u // WIDE)
 
             def guests(layer, what, j):
                 @pl.when(lb == layer + NL * ys_)
@@ -847,7 +867,7 @@
                 def _():
                     def out(row, n, other):
                         for j in range(n // C):
-                            ar_wait(NL - 1, NL, j)
+                            ar_wait(NL - 1, NL, j, WIDE)
                         start_all(y_copies_of(CORES * row + c, n))
                     each_row(out)
 
@@ -1041,6 +1061,7 @@
         *[vm(*k, 8, D, dtype=F32) for k in ((NL,), (NL, NT), (NL,), (NL,))],
         vm(C, D), vm(C, D), vm(C, max(D, F), dtype=F32), vm(C, F), vm(S, C), vm(S, C, dtype=F32),
         *[vm(1, D, dtype=F32)] * 4, vm(1, D), vm(1, D), vm(1, F), vm(3, CORES, E), vm(S, D),
+        *[dma((NC * SUB,))] * 2, *[dma((CORES, NC * SUB))] * 3,
         dma((NA,)), dma((NA + 1,)), dma((CORES, NA + 1)), dma((NL, 2 * NA + 1)), dma((CORES, NA)), dma((3, NA)), dma((NA, 4)), dma((CORES,)), dma((1,)),
         dma((NC * SUB,)), dma((NC * SUB,)), dma((CORES, NC * SUB)), dma((CORES, NC * SUB)), dma((CORES, NC * SUB)),
         dma((NL,)), dma((NL,)), dma((NA,)), dma((CORES, NA)), dma((CORES, NA)), dma((CORES, NA)), dma((CORES, NA)), dma((NA,)),

time: 227 us -> 230 us (1.013)
  Pallas kernels: 226 us -> 229 us
where the time goes in v15:
time: 230 us; the launch traced here: 229 us
  Pallas kernels  229 us (100%)
    pallas_call x1, Pallas kernels, group_step(): pl.pallas_call(functools.partial(body, dims), out_shape=out_shape, in_spe...  223 us
    pallas_call x1, Pallas kernels, finish_step(): pl.pallas_call(finish, out_shape=outs, in_specs=[hbm] * 6, out_specs=[hbm...  5.89 us

profile of v15, /device:TPU:0, one launch (start us, length us, event | category | flops | bytes accessed | tf_op | source)
XLA Modules:
  0.0 229.4 jit_solution(16832163321998392350)
XLA Ops:
  0.7 222.6 %neox_group.1 = (bf16[2,2,1024,512]{3,2,1,0:T(8,128)(2,1)}, f32[384,512]{1,0:T(8,128)}, f32[128,512]{1,0:T(8,128)}, f32[512,512]{1,0:T(8,128)}, f32[512,512]{1,0:T(8,128)}, /*index=5*/f32[8,512]{1,0:T(8,128)}) custom-call(bf16[2,2,1024,512]{3,2,1,0:T(8,128)(2,1)} %x.1, f32[2,2,1024,512]{3,2,1,0:T(8,128)} %g.1, bf16[384,512]{1,0:T(8,128)(2,1)} %bitcast.24, ...), custom_call_target="tpu_custom_call" | custom-call | tf_op jit(solution)/shard_map/neox_group/pallas_call | solution.py:1071
  223.3 5.9 %neox_out.1 = (bf16[2,2,1024,512]{3,2,1,0:T(8,128)(2,1)}, f32[384,512]{1,0:T(8,128)}, f32[128,512]{1,0:T(8,128)}, f32[512,512]{1,0:T(8,128)}, f32[512,512]{1,0:T...) custom-call(bf16[2,2,1024,512]{3,2,1,0:T(8,128)(2,1)} %get-tuple-ele, ...), custom_call_target="tpu_custom_call" | custom-call | tf_op jit(solution)/shard_map/neox_out/pallas_call | solution.py:1023

commit v16 on v13

--- a/solution.py
+++ b/solution.py
@@ -24,7 +24,7 @@
 NA = 4
 CORES = 2
 SUB = 4
-FWD_AT = {k: (('mid', 1, k), ('last', 2, k)) for k in range(SUB)}
+FWD_AT = {0: (('mid', 1, 0), ('last', 2, 0), ('last', 2, 1)), 1: (('mid', 1, 1), ('last', 2, 2)), 2: (('mid', 1, 2),), 3: (('mid', 1, 3), ('last', 2, 3))}
 BWD_AT = {k: (('last', 2, k),) * (k < SUB) + (('mid', 1, k - 1),) * (k > 0) for k in range(SUB + 1)}
 LOG2E = 1.4426950408889634
 RSQRT2 = 0.7071067811865476

time: 227 us -> 227 us (level)
  no operation moved by 1% of the time
where the time goes in v16:
time: 227 us
  Pallas kernels  226 us (100%)
    pallas_call x1, Pallas kernels, group_step(): pl.pallas_call(functools.partial(body, dims), out_shape=out_shape, in_spe...  221 us
    pallas_call x1, Pallas kernels, finish_step(): pl.pallas_call(finish, out_shape=outs, in_specs=[hbm] * 6, out_specs=[hbm...  5.89 us

profile of v16, /device:TPU:0, one launch (start us, length us, event | category | flops | bytes accessed | tf_op | source)
XLA Modules:
  0.0 227.3 jit_solution(11947690253602483912)
XLA Ops:
  0.7 220.5 %neox_group.1 = (bf16[2,2,1024,512]{3,2,1,0:T(8,128)(2,1)}, f32[384,512]{1,0:T(8,128)}, f32[128,512]{1,0:T(8,128)}, f32[512,512]{1,0:T(8,128)}, f32[512,512]{1,0:T(8,128)}, /*index=5*/f32[8,512]{1,0:T(8,128)}) custom-call(bf16[2,2,1024,512]{3,2,1,0:T(8,128)(2,1)} %x.1, f32[2,2,1024,512]{3,2,1,0:T(8,128)} %g.1, bf16[384,512]{1,0:T(8,128)(2,1)} %bitcast.24, ...), custom_call_target="tpu_custom_call" | custom-call | tf_op jit(solution)/shard_map/neox_group/pallas_call | solution.py:1050
  221.2 5.9 %neox_out.1 = (bf16[2,2,1024,512]{3,2,1,0:T(8,128)(2,1)}, f32[384,512]{1,0:T(8,128)}, f32[128,512]{1,0:T(8,128)}, f32[512,512]{1,0:T(8,128)}, f32[512,512]{1,0:T...) custom-call(bf16[2,2,1024,512]{3,2,1,0:T(8,128)(2,1)} %get-tuple-ele, ...), custom_call_target="tpu_custom_call" | custom-call | tf_op jit(solution)/shard_map/neox_out/pallas_call | solution.py:1003
